TPU v7x, 512 devices: a 8x2x16 block of a 8x8x16 slice. The times are simulated.
512 devices in a mesh: groups: 2 (over y), ep: 32 (over z, core), tp: 8 (over x).
Axes of the slice: x: 8, y: 2, z: 16, core: 2. Of those that a mesh axis runs over, the one named last changes fastest.
The devices are a block of a 8x8x16 slice.
Arguments:
- context: bfloat16 [4096, 4096], P(('groups', 'ep'), 'tp'), parts along dimension 0, may hold values from -6 to 6
- stream: bfloat16 [4096, 4096], P(('groups', 'ep'), 'tp'), parts along dimension 0, may hold values from -14 to 14
- out_proj: bfloat16 [4096, 4096], P('tp', 'ep'), may hold values from -0.09375 to 0.09375
- norm_gain: bfloat16 [4096], P('tp'), may hold values from 0.099609375 to 1.8984375
- router: bfloat16 [4096, 4], P('tp'), may hold values from -0.0625 to 0.0625
- expert_ids: int32 [4096, 2], P(('groups', 'ep')), parts along dimension 0, may hold values from 0 to 3, all different within a row; in each aligned block of 64 rows (0 to 63, 64 to 127, ...) at most 36 rows name the same one
- w_gate: bfloat16 [4096, 28672], P('tp', 'ep'), may hold values from -0.09375 to 0.09375
- w_up: bfloat16 [4096, 28672], P('tp', 'ep'), may hold values from -0.09375 to 0.09375
- w_down: bfloat16 [28672, 4096], P('ep', 'tp'), may hold values from -0.125 to 0.125
Outputs:
- layer_out: bfloat16 [4096, 4096], P(('groups', 'ep'), 'tp'), parts along dimension 0
There are 2 independent parts, one for each index of `groups`. A program takes and returns all parts, laid end to end along the dimension named above; an argument that names none is the same for every part. Nothing has to cross between parts.
Inputs may be any that keep to these rules, and one draw needn't show every extreme that they name: `expert_ids`: each row names 2 different experts. In each aligned block of 64 rows (the rows of one index of ep) no expert is named by more than 36 rows, and in some blocks one expert is named by exactly 36 rows.
All inputs are finite; a program needn't handle non-finite values.
Results may differ from a plain program's by a relative error of at most 0.02.
Values may be sent and summed in bfloat16 or wider, within the bound.
No kernel may reach another device: no remote copies, remote signals or barrier semaphores. Data moves between devices by JAX's collectives and lax.ppermute only.
A program may use at most 64 MiB of HBM per device.

v0:
```python
import jax
import jax.numpy as jnp
from jax import lax
from jax.sharding import PartitionSpec as P

D = 4096
EXPERTS = 4
CAP = 36


def cut_along(x, dim, devices):
    before, after = (x.shape[:dim], x.shape[dim + 1 :])
    return jnp.moveaxis(x.reshape(*before, devices, -1, *after), dim, 0)


def sum_at_owner(x, axis, dim):
    devices = lax.axis_size(axis)
    parts = lax.all_to_all(cut_along(x, dim, devices), axis, 0, 0, tiled=True)
    return jnp.sum(parts.astype(jnp.float32), axis=0)


def per_device(context, stream, out_proj, norm_gain, router, expert_ids, w_gate, w_up, w_down):
    tok_rows = stream.shape[0]
    width_part = stream.shape[1]
    ep_count = lax.axis_size("ep")
    fanout = ep_count // EXPERTS
    head_part = jnp.dot(
        context,
        lax.all_gather(out_proj, "ep", axis=1, tiled=True),
        preferred_element_type=jnp.float32,
    )
    attention = sum_at_owner(head_part.astype(jnp.bfloat16), "tp", 1)
    hstate = (stream.astype(jnp.float32) + attention).astype(jnp.bfloat16)
    hfloat = hstate.astype(jnp.float32)
    gain_vec = norm_gain.astype(jnp.float32)
    router_wide = router.astype(jnp.float32)
    squares = jnp.sum(hfloat * hfloat, axis=1)
    unscaled = jnp.dot(hfloat * gain_vec[None, :], router_wide, precision=lax.Precision.HIGHEST)
    total_sq, raw_logits = lax.psum((squares, unscaled), "tp")
    inverse = lax.rsqrt(total_sq / D + 1e-05)[:, None]
    normed = hfloat * inverse * gain_vec[None, :]
    logits = raw_logits * inverse
    inputs = normed.astype(jnp.bfloat16)
    experts_range = jnp.arange(EXPERTS, dtype=jnp.int32)
    flat_ids = expert_ids.reshape(tok_rows * 2)
    onehot = (flat_ids[:, None] == experts_range[None, :]).astype(jnp.int32)
    before = jnp.cumsum(onehot, axis=0) - onehot
    slot_index = jnp.sum(before * onehot, axis=1)
    target = flat_ids * CAP + slot_index
    picked = onehot.reshape(tok_rows, 2, EXPERTS).astype(jnp.float32)
    chosen = jnp.sum(picked * logits[:, None, :], axis=2)
    leading = jax.nn.sigmoid(chosen[:, 0] - chosen[:, 1])
    weights = jnp.stack([leading, 1.0 - leading], axis=1)
    columns_all = jnp.arange(EXPERTS * CAP, dtype=jnp.int32)
    placement = (
        (target[:, None] == columns_all[None, :])
        .astype(jnp.float32)
        .reshape(tok_rows, 2, EXPERTS * CAP)
    )
    dispatch = jnp.sum(placement, axis=1)
    combine = jnp.sum(placement * weights[:, :, None], axis=1)
    sectioned = lax.dot_general(
        dispatch.astype(jnp.bfloat16),
        inputs,
        (((0,), (0,)), ((), ())),
        preferred_element_type=jnp.float32,
    ).astype(jnp.bfloat16)
    send_rows = jnp.broadcast_to(
        sectioned.reshape(EXPERTS, 1, CAP, width_part), (EXPERTS, fanout, CAP, width_part)
    ).reshape(ep_count, CAP, width_part)
    received = lax.all_to_all(send_rows, "ep", split_axis=0, concat_axis=0, tiled=True)
    slot_count = received.shape[1]
    flattened = received.reshape(ep_count * slot_count, width_part)
    gate_part = jnp.dot(flattened, w_gate, preferred_element_type=jnp.float32)
    up_part = jnp.dot(flattened, w_up, preferred_element_type=jnp.float32)
    gate_share = lax.psum_scatter(
        gate_part.astype(jnp.bfloat16), "tp", scatter_dimension=1, tiled=True
    ).astype(jnp.float32)
    up_share = lax.psum_scatter(
        up_part.astype(jnp.bfloat16), "tp", scatter_dimension=1, tiled=True
    ).astype(jnp.float32)
    hidden_share = (jax.nn.silu(gate_share) * up_share).astype(jnp.bfloat16)
    hidden = lax.all_gather(hidden_share, "tp", axis=1, tiled=True)
    partial_value = jnp.dot(hidden, w_down, preferred_element_type=jnp.float32).astype(jnp.bfloat16)
    returned_rows = lax.all_to_all(
        partial_value.reshape(ep_count, slot_count, width_part),
        "ep",
        split_axis=0,
        concat_axis=0,
        tiled=True,
    )
    summed = jnp.sum(
        returned_rows.astype(jnp.float32).reshape(EXPERTS, fanout, CAP, width_part), axis=1
    ).reshape(EXPERTS * CAP, width_part)
    expert_mix = jnp.dot(combine, summed, precision=lax.Precision.HIGHEST)
    return (hfloat + expert_mix).astype(jnp.bfloat16)


def solution(mesh):
    return jax.shard_map(
        per_device,
        mesh=mesh,
        in_specs=(
            P(("groups", "ep"), "tp"),
            P(("groups", "ep"), "tp"),
            P("tp", "ep"),
            P("tp"),
            P("tp", None),
            P(("groups", "ep"), None),
            P("tp", "ep"),
            P("tp", "ep"),
            P("ep", "tp"),
        ),
        out_specs=P(("groups", "ep"), "tp"),
        check_vma=False,
    )
```

profile of v0, /device:TPU:65, one launch (start us, length us, event | category | flops | bytes accessed | tf_op | source)
XLA Modules:
  0.0 476.4 jit_solution(887955439675530526)
XLA Ops:
  6.6 0.7 all-gather.3.cloned.1.call-update
  7.3 119.6 %all-gather.3.cloned.1.call-done = bf16[512,4096]{1,0:T(8,128)(2,1)} async-done(((bf16[512,128]{1,0:T(8,128)(2,1)}), bf16[512,4096]{1,0:T(8,128)(2,1)}) %all-gather.3.cloned.1.call-update) | async-done | bytes 4194320 | tf_op jit(solution)/shard_map/all_gather | solution.py:29
  127.0 3.1 convolution_convert_fusion
  130.1 0.8 copy.37
  130.9 6.4 %all-to-all-start = ((bf16[8,64,512]{2,1,0:T(8,128)(2,1)}), bf16[8,64,512]{2,1,0:T(8,128)(2,1)S(1)}, u32[]{:S(2)}, u32[]{:S(2)}) async-start(bf16[8,64,512]{2,1,0:T(8,128)(2,1)} %bitcast.22), calls=%async_computation | async-start | bytes 1048576 | tf_op jit(solution)/shard_map/all_to_all | solution.py:18
  137.8 0.2 reduce_window_sum.11
  137.9 0.2 select_reduce_fusion.1
  138.3 16.9 %all-to-all-done = bf16[8,64,512]{2,1,0:T(8,128)(2,1)S(1)} async-done(((bf16[8,64,512]{2,1,0:T(8,128)(2,1)}), bf16[8,64,512]{2,1,0:T(8,128)(2,1)S(1)}, u32[]{:S(2)}, u32[]{:S(2)}) %all-to-all-start) | async-done | bytes 524320 | tf_op jit(solution)/shard_map/all_to_all | solution.py:18
  155.6 11.0 %all-reduce = (f32[64,4]{0,1:T(4,128)S(1)}, f32[64]{0:T(128)S(1)}) all-reduce(f32[64,4]{0,1:T(4,128)S(1)} %fusion.6, f32[64]{0:T(128)S(1)} %get-tuple-element.11), channel_id=1, replica_groups=mesh['groups'=2,'ep'=32,'tp'=8] {'tp'}, use_global_device_ids=true, to_apply=%region_3.0 | all-reduce | flops 320 | bytes 2560 | tf_op jit(solution)/shard_map/psum | solution.py:39
  166.8 0.2 convolution_convert_fusion.4
  167.2 78.4 %all_to_all.15 = bf16[32,36,512]{2,1,0:T(8,128)(2,1)S(1)} all-to-all(bf16[32,36,512]{2,1,0:T(8,128)(2,1)S(1)} %bitcast.23), channel_id=1, replica_groups=mesh['groups'=2,'ep'=32,'tp'=8] {'ep'}, dimensions={0} | all-to-all | bytes 2359296 | tf_op jit(solution)/shard_map/all_to_all | solution.py:71
  245.6 0.2 reshape.57
  245.8 2.7 convolution_convert_fusion.1
  248.7 1.0 copy-done.5
  249.7 2.7 convolution_convert_fusion.2
  252.6 28.4 %reduce-scatter.5.cloned.1.call-done = bf16[1152,112]{0,1:T(8,128)(2,1)} async-done(((bf16[1152,896]{0,1:T(8,128)(2,1)}), bf16[1152,112]{0,1:T(8,128)(2,1)}) %reduce-scatter.5.cloned.1.call-update) | async-done | bytes 258064 | tf_op jit(solution)/shard_map/reduce_scatter | solution.py:79
  281.0 51.0 %reduce-scatter.3.cloned.1.call-done = bf16[1152,112]{0,1:T(8,128)(2,1)} async-done(((bf16[1152,896]{0,1:T(8,128)(2,1)}), bf16[1152,112]{0,1:T(8,128)(2,1)}) %reduce-scatter.3.cloned.1.call-update) | async-done | bytes 258064 | tf_op jit(solution)/shard_map/reduce_scatter | solution.py:76
  332.0 2.0 fusion.5
  334.0 46.3 %all-gather.5.cloned.1.call-done = bf16[1152,896]{0,1:T(8,128)(2,1)} async-done(((bf16[1152,112]{0,1:T(8,128)(2,1)}), bf16[1152,896]{0,1:T(8,128)(2,1)}) %all-gather.5.cloned.1.call-update) | async-done | bytes 2064400 | tf_op jit(solution)/shard_map/all_gather | solution.py:83
  380.3 3.0 convolution_convert_fusion.3
  383.3 0.3 reshape.58
  383.6 85.1 %all_to_all.16 = bf16[32,36,512]{2,1,0:T(8,128)(2,1)S(1)} all-to-all(bf16[32,36,512]{2,1,0:T(8,128)(2,1)S(1)} %reshape.58), channel_id=1, replica_groups=mesh['groups'=2,'ep'=32,'tp'=8] {'ep'}, dimensions={0} | all-to-all | bytes 2359296 | tf_op jit(solution)/shard_map/all_to_all | solution.py:85
  468.7 0.2 convert_reduce_fusion
  468.9 0.9 fusion
  (39 shorter events, 1.6 us)
Async XLA Ops:
  6.5 239.3 %copy-start = (bf16[512,896]{1,0:T(8,128)(2,1)S(1)}, bf16[512,896]{1,0:T(8,128)(2,1)}, u32[]{:S(2)}) copy-start(bf16[512,896]{1,0:T(8,128)(2,1)} %param.16) | copy-start | bytes 2752516
  6.6 120.4 %all-gather.3.cloned.1.call-start = ((), (), s32[]{:S(2)}) async-start(), calls=%async_computation.5 | async-start | bytes 4325376 | tf_op jit(solution)/shard_map/all_gather | solution.py:29
  130.0 7.4 %copy-start.4 = (bf16[512]{0:T(512)(128)(2,1)S(1)}, bf16[512]{0:T(512)(128)(2,1)}, u32[]{:S(2)}) copy-start(bf16[512]{0:T(512)(128)(2,1)} %param.12) | copy-start | bytes 3076
  130.0 7.4 %copy-start.2 = (s32[64,2]{0,1:T(2,128)S(1)}, s32[64,2]{0,1:T(2,128)}, u32[]{:S(2)}) copy-start(s32[64,2]{0,1:T(2,128)} %param.14) | copy-start | bytes 1540
  130.1 25.3 %copy-start.1 = (bf16[64,512]{1,0:T(8,128)(2,1)S(1)}, bf16[64,512]{1,0:T(8,128)(2,1)}, u32[]{:S(2)}) copy-start(bf16[64,512]{1,0:T(8,128)(2,1)} %param.10) | copy-start | bytes 196612
  130.1 25.4 %copy-start.3 = (bf16[512,4]{0,1:T(4,128)(2,1)S(1)}, bf16[512,4]{0,1:T(4,128)(2,1)}, u32[]{:S(2)}) copy-start(bf16[512,4]{0,1:T(4,128)(2,1)} %param.13) | copy-start | bytes 12292
  130.9 24.4 %all-to-all-start = ((bf16[8,64,512]{2,1,0:T(8,128)(2,1)}), bf16[8,64,512]{2,1,0:T(8,128)(2,1)S(1)}, u32[]{:S(2)}, u32[]{:S(2)}) async-start(bf16[8,64,512]{2,1,0:T(8,128)(2,1)} %bitcast.22), calls=%async_computation | async-start | bytes 1048576 | tf_op jit(solution)/shard_map/all_to_all | solution.py:18
  137.3 143.7 %reduce-scatter.5.cloned.1.call-start = ((), (), s32[]{:S(2)}) async-start(), calls=%async_computation.7 | async-start | bytes 2322432 | tf_op jit(solution)/shard_map/reduce_scatter | solution.py:79
  248.6 1.2 copy-start.5
  248.6 83.4 %reduce-scatter.3.cloned.1.call-start = ((), (), s32[]{:S(2)}) async-start(), calls=%async_computation.6 | async-start | bytes 2322432 | tf_op jit(solution)/shard_map/reduce_scatter | solution.py:76
  252.4 127.9 %copy-start.6 = (bf16[896,512]{1,0:T(8,128)(2,1)S(1)}, bf16[896,512]{1,0:T(8,128)(2,1)}, u32[]{:S(2)}) copy-start(bf16[896,512]{1,0:T(8,128)(2,1)} %param.17) | copy-start | bytes 2752516
  252.5 127.8 %all-gather.5.cloned.1.call-start = ((), (), s32[]{:S(2)}) async-start(), calls=%async_computation.8 | async-start | bytes 2322432 | tf_op jit(solution)/shard_map/all_gather | solution.py:83
Sparse Core Ops, SparseCore 0:
  9.4 117.4 all-gather.2
  248.8 32.2 reduce-scatter.4
  283.9 48.0 reduce-scatter.2
  334.1 46.1 all-gather.4
where the time goes:
time: 477 us; the launch traced here: 476 us
  waiting for transfers between devices  263 us (55%)
  blocking collectives  174 us (36%)
  between operations  13.3 us (3%)
  matrix products  12.8 us (3%)
  starting transfers between devices  6.61 us (1%)
    all_gather x1, waiting for transfers between devices, per_device(): lax.all_gather(out_proj, 'ep', axis=1, tiled=True)  120 us
    all_to_all x1, blocking collectives, per_device(): lax.all_to_all(partial_value.reshape(ep_count, slot_count, width_part), '...  85.1 us
    all_to_all x1, blocking collectives, per_device(): lax.all_to_all(send_rows, 'ep', split_axis=0, concat_axis=0, tiled=True)  78.4 us
    reduce_scatter x1, waiting for transfers between devices, per_device(): lax.psum_scatter(gate_part.astype(jnp.bfloat16), 'tp', scatter_dimension=...  51 us
    all_gather x1, waiting for transfers between devices, per_device(): hidden = lax.all_gather(hidden_share, 'tp', axis=1, tiled=True)  46.3 us
    reduce_scatter x1, waiting for transfers between devices, per_device(): lax.psum_scatter(up_part.astype(jnp.bfloat16), 'tp', scatter_dimension=1,...  28.4 us
    all_to_all x1, waiting for transfers between devices, sum_at_owner(): parts = lax.all_to_all(cut_along(x, dim, devices), axis, 0, 0, tiled=True)  16.9 us
    psum x1, blocking collectives, per_device(): total_sq, raw_logits = lax.psum((squares, unscaled), 'tp')  11 us
  transfers between devices with their start and end apart: 5, of which 5 were waited for; matrix products, arithmetic and copies ran while one was open for 1% of the time, Pallas kernels for 0%

commit v1 on v0

v1 whole, which is shorter than its diff:
```python
import jax
import jax.numpy as jnp
from jax import lax
from jax.sharding import Mesh, PartitionSpec as P

D = 4096
EXPERTS = 4
CAP = 36
CORES = 2
EP = ("a", "q", "core")


def per_device(context, stream, out_proj, norm_gain, router, expert_ids, w_gate, w_up, w_down):
    f32, bf16 = jnp.float32, jnp.bfloat16
    tok_rows, width = stream.shape
    tp = lax.axis_size("tp")
    quads = lax.axis_size("q")
    swap = [(0, 1), (1, 0)]

    w_both = lax.optimization_barrier(jnp.concatenate([w_gate, w_up], axis=1))

    head_part = jnp.dot(
        context, lax.all_gather(out_proj, EP, axis=1, tiled=True), preferred_element_type=f32
    ).astype(bf16)
    cut = jnp.moveaxis(head_part.reshape(tok_rows, tp, width), 1, 0)
    parts = lax.all_to_all(cut, "tp", 0, 0, tiled=True)
    hstate = (stream.astype(f32) + jnp.sum(parts.astype(f32), axis=0)).astype(bf16)
    hfloat = hstate.astype(f32)
    gain = norm_gain.astype(f32)

    experts_range = jnp.arange(EXPERTS, dtype=jnp.int32)
    flat_ids = expert_ids.reshape(tok_rows * 2)
    onehot = (flat_ids[:, None] == experts_range[None, :]).astype(jnp.int32)
    before = jnp.cumsum(onehot, axis=0) - onehot
    target = flat_ids * CAP + jnp.sum(before * onehot, axis=1)
    columns_all = jnp.arange(EXPERTS * CAP, dtype=jnp.int32)
    placement = (
        (target[:, None] == columns_all[None, :]).astype(f32).reshape(tok_rows, 2, EXPERTS * CAP)
    )
    dispatch = jnp.sum(placement, axis=1).astype(bf16)
    sectioned = lax.dot_general(
        dispatch, hstate, (((0,), (0,)), ((), ())), preferred_element_type=f32
    ).astype(bf16)

    mine = lax.all_to_all(sectioned.reshape(EXPERTS, CAP, width), "a", 0, 0, tiled=True)
    chunk = EXPERTS * CAP
    chip = lax.all_gather(mine.reshape(chunk, width), "q", axis=0, tiled=True)
    other = lax.ppermute(chip, "core", swap)
    rows = jnp.concatenate([chip, other], axis=0)

    rfloat = rows.astype(f32)
    scaled = (rfloat * gain[None, :]).astype(bf16)
    row_sq = jnp.sum(rfloat * rfloat, axis=1)
    both = jnp.dot(scaled, w_both, preferred_element_type=f32).astype(bf16)
    squares = jnp.sum(hfloat * hfloat, axis=1)
    unscaled = jnp.dot(
        hfloat * gain[None, :], router.astype(f32), precision=lax.Precision.HIGHEST
    )
    both, row_sq, squares, unscaled = lax.optimization_barrier((both, row_sq, squares, unscaled))
    share = lax.psum_scatter(both, "tp", scatter_dimension=0, tiled=True).astype(f32)
    row_total, total_sq, raw_logits = lax.psum((row_sq, squares, unscaled), "tp")
    my_total = lax.dynamic_slice_in_dim(row_total, lax.axis_index("tp") * chunk, chunk)
    row_inverse = lax.rsqrt(my_total / D + 1e-05)[:, None]
    ff = w_gate.shape[1]
    gate_share, up_share = share[:, :ff] * row_inverse, share[:, ff:] * row_inverse
    hidden_share = (jax.nn.silu(gate_share) * up_share).astype(bf16)
    hidden = lax.all_gather(hidden_share, "tp", axis=0, tiled=True)
    partial_value = jnp.dot(hidden, w_down, preferred_element_type=f32).astype(bf16)

    half = quads * chunk
    from_core = lax.ppermute(partial_value[half:], "core", swap)
    on_chip = (partial_value[:half].astype(f32) + from_core.astype(f32)).astype(bf16)
    from_chips = lax.all_to_all(on_chip.reshape(quads, chunk, width), "q", 0, 0, tiled=True)
    summed = jnp.sum(from_chips.astype(f32), axis=0).astype(bf16)
    back = lax.all_to_all(summed.reshape(EXPERTS, CAP, width), "a", 0, 0, tiled=True)

    inverse = lax.rsqrt(total_sq / D + 1e-05)[:, None]
    logits = raw_logits * inverse
    picked = onehot.reshape(tok_rows, 2, EXPERTS).astype(f32)
    chosen = jnp.sum(picked * logits[:, None, :], axis=2)
    leading = jax.nn.sigmoid(chosen[:, 0] - chosen[:, 1])
    weights = jnp.stack([leading, 1.0 - leading], axis=1)
    combine = jnp.sum(placement * weights[:, :, None], axis=1)
    expert_mix = jnp.dot(
        combine, back.reshape(chunk, width).astype(f32), precision=lax.Precision.HIGHEST
    )
    return (hfloat + expert_mix).astype(bf16)


def solution(mesh):
    groups, ep, tp = (mesh.shape[name] for name in ("groups", "ep", "tp"))
    fine = Mesh(
        mesh.devices.reshape(groups, EXPERTS, ep // (EXPERTS * CORES), CORES, tp),
        ("groups", *EP, "tp"),
    )
    rows = ("groups", *EP)
    return jax.shard_map(
        per_device,
        mesh=fine,
        in_specs=(
            P(rows, "tp"),
            P(rows, "tp"),
            P("tp", EP),
            P("tp"),
            P("tp", None),
            P(rows, None),
            P("tp", EP),
            P("tp", EP),
            P(EP, "tp"),
        ),
        out_specs=P(rows, "tp"),
        check_vma=False,
    )
```

time: 477 us -> 364 us (0.76)
  blocking collectives: 174 us -> 55.6 us
  starting transfers between devices: 6.61 us -> 38.9 us
  waiting for transfers between devices: 263 us -> 235 us
    all_to_all x2 -> x1, blocking collectives: 163 us -> 19 us  [per_device(): lax.all_to_all(sectioned.reshape(EXPERTS, CAP, width), 'a', 0, 0, tiled=T...]
    reduce_scatter x2 -> x1, waiting for transfers between devices: 79.4 us -> 25.6 us  [per_device(): lax.psum_scatter(both, 'tp', scatter_dimension=0, tiled=True).astype(f32)]
    all_to_all x1 -> x3, waiting for transfers between devices: 16.9 us -> 44.5 us  [the longest x1 16.9 us: per_device(): parts = lax.all_to_all(cut, 'tp', 0, 0, tiled=True)]
    all_to_all x1 -> x3, starting transfers between devices: 6.42 us -> 22.7 us  [the longest x1 11.4 us: per_device(): lax.all_to_all(summed.reshape(EXPERTS, CAP, width), 'a', 0, 0, tiled=True)]
    ppermute x0 -> x2, starting transfers between devices: none -> 16.2 us  [the longest x1 9.33 us: per_device(): other = lax.ppermute(chip, 'core', swap)]
    all_gather x0 -> x1, blocking collectives: none -> 13.8 us  [per_device(): chip = lax.all_gather(mine.reshape(chunk, width), 'q', axis=0, tiled=True)]
    psum x1, blocking collectives: 11 us -> 22.9 us  [per_device(): lax.psum((row_sq, squares, unscaled), 'tp')]
    dot_general x7 -> x6, matrix products: 12.8 us -> 11.5 us  [the longest x1 4.26 us: per_device(): both = jnp.dot(scaled, w_both, preferred_element_type=f32).astype(bf16)]
  transfers between devices with their start and end apart: 5 -> 8, of which waited for: 5 -> 8; matrix products, arithmetic and copies ran while one was open for 1% -> 0% of each run, Pallas kernels for 0% -> 0%
where the time goes in v1:
time: 364 us; the launch traced here: 362 us
  waiting for transfers between devices  235 us (65%)
  blocking collectives  55.6 us (15%)
  starting transfers between devices  38.9 us (11%)
  between operations  13.3 us (4%)
  matrix products  11.5 us (3%)
  other arithmetic  4.52 us (1%)
    all_gather x1, waiting for transfers between devices, per_device(): lax.all_gather(out_proj, EP, axis=1, tiled=True)  120 us
    all_gather x1, waiting for transfers between devices, per_device(): hidden = lax.all_gather(hidden_share, 'tp', axis=0, tiled=True)  42 us
    reduce_scatter x1, waiting for transfers between devices, per_device(): lax.psum_scatter(both, 'tp', scatter_dimension=0, tiled=True).astype(f32)  25.6 us
    psum x1, blocking collectives, per_device(): lax.psum((row_sq, squares, unscaled), 'tp')  22.9 us
    all_to_all x1, blocking collectives, per_device(): lax.all_to_all(sectioned.reshape(EXPERTS, CAP, width), 'a', 0, 0, tiled=T...  19 us
    all_to_all x1, waiting for transfers between devices, per_device(): parts = lax.all_to_all(cut, 'tp', 0, 0, tiled=True)  16.9 us
    all_to_all x1, waiting for transfers between devices, per_device(): lax.all_to_all(on_chip.reshape(quads, chunk, width), 'q', 0, 0, tiled=True)  15.4 us
    all_gather x1, blocking collectives, per_device(): chip = lax.all_gather(mine.reshape(chunk, width), 'q', axis=0, tiled=True)  13.8 us
  transfers between devices with their start and end apart: 8, of which 8 were waited for; matrix products, arithmetic and copies ran while one was open for 0% of the time, Pallas kernels for 0%

profile of v1, /device:TPU:65, one launch (start us, length us, event | category | flops | bytes accessed | tf_op | source)
XLA Modules:
  0.0 361.5 jit_solution(5461499767241366825)
XLA Ops:
  7.3 119.6 %all-gather.3.cloned.1.call-done = bf16[512,4096]{1,0:T(8,128)(2,1)} async-done(((bf16[512,128]{1,0:T(8,128)(2,1)}), bf16[512,4096]{1,0:T(8,128)(2,1)}) %all-gather.3.cloned.1.call-update) | async-done | bytes 4194320 | tf_op jit(solution)/shard_map/all_gather | solution.py:23
  127.0 3.1 convolution_convert_fusion.1
  130.1 0.8 copy.37
  130.9 6.6 %all-to-all-start = ((bf16[8,64,512]{2,1,0:T(8,128)(2,1)}), bf16[8,64,512]{2,1,0:T(8,128)(2,1)S(1)}, u32[]{:S(2)}, u32[]{:S(2)}) async-start(bf16[8,64,512]{2,1,0:T(8,128)(2,1)} %bitcast.17), calls=%async_computation | async-start | bytes 1048576 | tf_op jit(solution)/shard_map/all_to_all | solution.py:26
  138.5 16.9 %all-to-all-done = bf16[8,64,512]{2,1,0:T(8,128)(2,1)S(1)} async-done(((bf16[8,64,512]{2,1,0:T(8,128)(2,1)}), bf16[8,64,512]{2,1,0:T(8,128)(2,1)S(1)}, u32[]{:S(2)}, u32[]{:S(2)}) %all-to-all-start) | async-done | bytes 524320 | tf_op jit(solution)/shard_map/all_to_all | solution.py:26
  155.9 19.0 %all_to_all.20 = bf16[4,36,512]{2,1,0:T(8,128)(2,1)S(1)} all-to-all(bf16[4,36,512]{2,1,0:T(8,128)(2,1)S(1)} %reshape.52), channel_id=1, replica_groups=mesh['groups'=2,'a'=4,'q'=4,'core'=2,'tp'=8] {'a'}, dimensions={0} | all-to-all | bytes 294912 | tf_op jit(solution)/shard_map/all_to_all | solution.py:45
  174.9 13.8 %all_gather.10 = bf16[576,512]{1,0:T(8,128)(2,1)S(1)} all-gather(bf16[144,512]{1,0:T(8,128)(2,1)S(1)} %reshape.53), channel_id=1, replica_groups=mesh['groups'=2,'a'=4,'q'=4,'core'=2,'tp'=8] {'q'}, dimensions={0}, use_global_device_ids=true | all-gather | bytes 737280 | tf_op jit(solution)/shard_map/all_gather | solution.py:47
  188.6 9.3 %collective-permute-start = (bf16[576,512]{1,0:T(8,128)(2,1)S(1)}, bf16[576,512]{1,0:T(8,128)(2,1)S(1)}, u32[]{:S(2)}, u32[]{:S(2)}) collective-permute-start(bf16[576,512]{1,0:T(8,128)(2,1)S(1)} %all_gather.10), channel_id=1, source_target_pairs={{0,8},{8,0},{1,9},{9,1},{2,10},{10,2},{3,11},{11,3},{4,12},{12,4},... | collective-permute-start | bytes 1769480 | tf_op jit(solution)/shard_map/ppermute | solution.py:48
  198.3 1.3 collective-permute-done
  199.9 4.3 %convolution_convert_fusion = bf16[1152,1792]{1,0:T(8,128)(2,1)} fusion(bf16[512,1792]{1,0:T(8,128)(2,1)S(1)} %pad_maximum_fusion, f32[512]{0:T(512)S(1)} %convert_element_type.83, bf16[576,512]{1,0:T(8,128)(2,1)S(1)} %collective-permute-done, bf16[576,512]{1,0:T(8,128)(2,1)S(1)} %all_gather.10), kind=kOutput, calls=%fused_computation | convolution fusion | flops 2119532544 | bytes 7145472 | tf_op jit(solution)/shard_map/dot_general | solution.py:54
  204.3 22.9 %all-reduce = (f32[64,4]{0,1:T(4,128)S(1)}, f32[64]{0:T(128)S(1)}, f32[1152]{0:T(1024)S(1)}) all-reduce(f32[64,4]{0,1:T(4,128)S(1)} %fusion.8, f32[64]{0:T(128)S(1)} %get-tuple-element.10, f32[1152]{0:T(1024)S(1)} %fusion.1), channel_id=1, replica_groups=mesh['groups'=2,'a'=4,'q'=4,'core'=2,'tp'=8] {'tp'}, use_global_device_ids=true, to_apply=%region_6.7 | all-reduce | flops 1472 | bytes 11776 | tf_op jit(solution)/shard_map/psum | solution.py:61
  227.3 25.6 %reduce-scatter.2.cloned.1.call-done = bf16[144,1792]{1,0:T(8,128)(2,1)} async-done(((bf16[1152,1792]{1,0:T(8,128)(2,1)}), bf16[144,1792]{1,0:T(8,128)(2,1)}) %reduce-scatter.2.cloned.1.call-update) | async-done | bytes 516112 | tf_op jit(solution)/shard_map/reduce_scatter | solution.py:60
  252.9 1.1 convert_element_type.86
  254.0 0.9 fusion.6
  255.0 42.0 %all-gather.5.cloned.1.call-done = bf16[1152,896]{1,0:T(8,128)(2,1)} async-done(((bf16[144,896]{1,0:T(8,128)(2,1)}), bf16[1152,896]{1,0:T(8,128)(2,1)}) %all-gather.5.cloned.1.call-update) | async-done | bytes 2064400 | tf_op jit(solution)/shard_map/all_gather | solution.py:67
  297.0 3.0 convolution_convert_fusion.2
  300.0 6.8 %collective-permute-start.1 = (bf16[576,512]{1,0:T(8,128)(2,1)S(1)}, bf16[576,512]{1,0:T(8,128)(2,1)S(1)}, u32[]{:S(2)}, u32[]{:S(2)}) collective-permute-start(bf16[576,512]{1,0:T(8,128)(2,1)S(1)} %slice.27), channel_id=1, source_target_pairs={{0,8},{8,0},{1,9},{9,1},{2,10},{10,2},{3,11},{11,3},{4,12},{12,4},... | collective-permute-start | bytes 1769480 | tf_op jit(solution)/shard_map/ppermute | solution.py:71
  306.8 1.6 collective-permute-done.1
  308.4 1.0 add_convert_fusion
  309.4 4.7 %all-to-all-start.2 = ((bf16[4,144,512]{2,1,0:T(8,128)(2,1)}), bf16[4,144,512]{2,1,0:T(8,128)(2,1)S(1)}, u32[]{:S(2)}, u32[]{:S(2)}) async-start(bf16[4,144,512]{2,1,0:T(8,128)(2,1)} %bitcast.1), calls=%async_computation.3 | async-start | bytes 1179648 | tf_op jit(solution)/shard_map/all_to_all | solution.py:73
  314.2 15.4 %all-to-all-done.2 = bf16[4,144,512]{2,1,0:T(8,128)(2,1)S(1)} async-done(((bf16[4,144,512]{2,1,0:T(8,128)(2,1)}), bf16[4,144,512]{2,1,0:T(8,128)(2,1)S(1)}, u32[]{:S(2)}, u32[]{:S(2)}) %all-to-all-start.2) | async-done | bytes 589856 | tf_op jit(solution)/shard_map/all_to_all | solution.py:73
  330.4 11.4 %all-to-all-start.3 = ((bf16[4,36,512]{2,1,0:T(8,128)(2,1)}), bf16[4,36,512]{2,1,0:T(8,128)(2,1)S(1)}, u32[]{:S(2)}, u32[]{:S(2)}) async-start(bf16[4,36,512]{2,1,0:T(8,128)(2,1)} %reshape.55), calls=%async_computation.4 | async-start | bytes 327680 | tf_op jit(solution)/shard_map/all_to_all | solution.py:75
  341.9 12.2 %all-to-all-done.3 = bf16[4,36,512]{2,1,0:T(8,128)(2,1)S(1)} async-done(((bf16[4,36,512]{2,1,0:T(8,128)(2,1)}), bf16[4,36,512]{2,1,0:T(8,128)(2,1)S(1)}, u32[]{:S(2)}, u32[]{:S(2)}) %all-to-all-start.3) | async-done | bytes 147488 | tf_op jit(solution)/shard_map/all_to_all | solution.py:75
  354.1 0.8 fusion.4
  (49 shorter events, 4.1 us)
Async XLA Ops:
  6.5 290.4 %copy-start = (bf16[896,512]{1,0:T(8,128)(2,1)S(1)}, bf16[896,512]{1,0:T(8,128)(2,1)}, u32[]{:S(2)}) copy-start(bf16[896,512]{1,0:T(8,128)(2,1)} %param.17) | copy-start | bytes 2752516
  6.6 120.4 %all-gather.3.cloned.1.call-start = ((), (), s32[]{:S(2)}) async-start(), calls=%async_computation.5 | async-start | bytes 4325376 | tf_op jit(solution)/shard_map/all_gather | solution.py:23
  130.0 7.5 %copy-start.4 = (s32[64,2]{0,1:T(2,128)S(1)}, s32[64,2]{0,1:T(2,128)}, u32[]{:S(2)}) copy-start(s32[64,2]{0,1:T(2,128)} %param.14) | copy-start | bytes 1540
  130.0 25.4 %copy-start.3 = (bf16[64,512]{1,0:T(8,128)(2,1)S(1)}, bf16[64,512]{1,0:T(8,128)(2,1)}, u32[]{:S(2)}) copy-start(bf16[64,512]{1,0:T(8,128)(2,1)} %param.10) | copy-start | bytes 196612
  130.9 67.1 %copy-start.6 = (bf16[512]{0:T(512)(128)(2,1)S(1)}, bf16[512]{0:T(512)(128)(2,1)}, u32[]{:S(2)}) copy-start(bf16[512]{0:T(512)(128)(2,1)} %param.12) | copy-start | bytes 3076
  130.9 67.1 %copy-start.1 = (bf16[512,896]{1,0:T(8,128)(2,1)S(1)}, bf16[512,896]{1,0:T(8,128)(2,1)}, u32[]{:S(2)}) copy-start(bf16[512,896]{1,0:T(8,128)(2,1)} %param.16) | copy-start | bytes 2752516
  130.9 67.1 %copy-start.2 = (bf16[512,896]{1,0:T(8,128)(2,1)S(1)}, bf16[512,896]{1,0:T(8,128)(2,1)}, u32[]{:S(2)}) copy-start(bf16[512,896]{1,0:T(8,128)(2,1)} %param.15) | copy-start | bytes 2752516
  130.9 24.5 %all-to-all-start = ((bf16[8,64,512]{2,1,0:T(8,128)(2,1)}), bf16[8,64,512]{2,1,0:T(8,128)(2,1)S(1)}, u32[]{:S(2)}, u32[]{:S(2)}) async-start(bf16[8,64,512]{2,1,0:T(8,128)(2,1)} %bitcast.17), calls=%async_computation | async-start | bytes 1048576 | tf_op jit(solution)/shard_map/all_to_all | solution.py:26
  137.4 115.4 %reduce-scatter.2.cloned.1.call-start = ((), (), s32[]{:S(2)}) async-start(), calls=%async_computation.6 | async-start | bytes 4644864 | tf_op jit(solution)/shard_map/reduce_scatter | solution.py:60
  174.9 23.3 %copy-start.5 = (bf16[512,4]{0,1:T(4,128)(2,1)S(1)}, bf16[512,4]{0,1:T(4,128)(2,1)}, u32[]{:S(2)}) copy-start(bf16[512,4]{0,1:T(4,128)(2,1)} %param.13) | copy-start | bytes 12292
  188.6 10.9 %collective-permute-start = (bf16[576,512]{1,0:T(8,128)(2,1)S(1)}, bf16[576,512]{1,0:T(8,128)(2,1)S(1)}, u32[]{:S(2)}, u32[]{:S(2)}) collective-permute-start(bf16[576,512]{1,0:T(8,128)(2,1)S(1)} %all_gather.10), channel_id=1, source_target_pairs={{0,8},{8,0},{1,9},{9,1},{2,10},{10,2},{3,11},{11,3},{4,12},{12,4},... | collective-permute-start | bytes 1769480 | tf_op jit(solution)/shard_map/ppermute | solution.py:48
  204.2 92.8 %all-gather.5.cloned.1.call-start = ((), (), s32[]{:S(2)}) async-start(), calls=%async_computation.7 | async-start | bytes 2322432 | tf_op jit(solution)/shard_map/all_gather | solution.py:67
  300.0 8.4 %collective-permute-start.1 = (bf16[576,512]{1,0:T(8,128)(2,1)S(1)}, bf16[576,512]{1,0:T(8,128)(2,1)S(1)}, u32[]{:S(2)}, u32[]{:S(2)}) collective-permute-start(bf16[576,512]{1,0:T(8,128)(2,1)S(1)} %slice.27), channel_id=1, source_target_pairs={{0,8},{8,0},{1,9},{9,1},{2,10},{10,2},{3,11},{11,3},{4,12},{12,4},... | collective-permute-start | bytes 1769480 | tf_op jit(solution)/shard_map/ppermute | solution.py:71
  309.4 20.2 %all-to-all-start.2 = ((bf16[4,144,512]{2,1,0:T(8,128)(2,1)}), bf16[4,144,512]{2,1,0:T(8,128)(2,1)S(1)}, u32[]{:S(2)}, u32[]{:S(2)}) async-start(bf16[4,144,512]{2,1,0:T(8,128)(2,1)} %bitcast.1), calls=%async_computation.3 | async-start | bytes 1179648 | tf_op jit(solution)/shard_map/all_to_all | solution.py:73
  330.4 23.7 %all-to-all-start.3 = ((bf16[4,36,512]{2,1,0:T(8,128)(2,1)}), bf16[4,36,512]{2,1,0:T(8,128)(2,1)S(1)}, u32[]{:S(2)}, u32[]{:S(2)}) async-start(bf16[4,36,512]{2,1,0:T(8,128)(2,1)} %reshape.55), calls=%async_computation.4 | async-start | bytes 327680 | tf_op jit(solution)/shard_map/all_to_all | solution.py:75
Sparse Core Ops, SparseCore 0:
  9.4 117.4 all-gather.2
  204.3 48.4 reduce-scatter.1
  255.1 41.8 all-gather.4

commit v2 on v1

v2 whole, which is shorter than its diff:
```python
import jax
import jax.numpy as jnp
from jax import lax
from jax.sharding import Mesh, PartitionSpec as P

D = 4096
EXPERTS = 4
CAP = 36
CORES = 2
EP = ("a", "q", "core")


def per_device(context, stream, out_proj, norm_gain, router, expert_ids, w_gate, w_up, w_down):
    f32, bf16 = jnp.float32, jnp.bfloat16
    tok_rows, width = stream.shape
    tp = lax.axis_size("tp")
    quads = lax.axis_size("q")
    swap = [(0, 1), (1, 0)]

    w_both = lax.optimization_barrier(jnp.concatenate([w_gate, w_up], axis=1))

    experts_range = jnp.arange(EXPERTS, dtype=jnp.int32)
    flat_ids = expert_ids.reshape(tok_rows * 2)
    onehot = (flat_ids[:, None] == experts_range[None, :]).astype(jnp.int32)
    before = jnp.cumsum(onehot, axis=0) - onehot
    target = flat_ids * CAP + jnp.sum(before * onehot, axis=1)
    columns_all = jnp.arange(EXPERTS * CAP, dtype=jnp.int32)
    placement = (
        (target[:, None] == columns_all[None, :]).astype(f32).reshape(tok_rows, 2, EXPERTS * CAP)
    )
    dispatch = jnp.sum(placement, axis=1).astype(bf16)
    proj_all = lax.all_gather(out_proj, EP, axis=1, tiled=True)
    proj_all, w_down, dispatch, placement, onehot = lax.optimization_barrier(
        (proj_all, w_down, dispatch, placement, onehot)
    )
    down_all = lax.all_gather(w_down, "tp", axis=0)
    head_part = jnp.dot(context, proj_all, preferred_element_type=f32).astype(bf16)
    cut = jnp.moveaxis(head_part.reshape(tok_rows, tp, width), 1, 0)
    parts = lax.all_to_all(cut, "tp", 0, 0, tiled=True)
    hstate = (stream.astype(f32) + jnp.sum(parts.astype(f32), axis=0)).astype(bf16)
    hfloat = hstate.astype(f32)
    gain = norm_gain.astype(f32)

    sectioned = lax.dot_general(
        dispatch, hstate, (((0,), (0,)), ((), ())), preferred_element_type=f32
    ).astype(bf16)

    mine = lax.all_to_all(sectioned.reshape(EXPERTS, CAP, width), "a", 0, 0, tiled=True)
    chunk = EXPERTS * CAP
    chip = lax.all_gather(mine.reshape(chunk, width), "q", axis=0, tiled=True)
    other = lax.ppermute(chip, "core", swap)
    first = lax.axis_index("core") == 0
    rows = jnp.concatenate([jnp.where(first, chip, other), jnp.where(first, other, chip)], axis=0)

    rfloat = rows.astype(f32)
    scaled = (rfloat * gain[None, :]).astype(bf16)
    row_sq = jnp.sum(rfloat * rfloat, axis=1)
    both = jnp.dot(scaled, w_both, preferred_element_type=f32).astype(bf16)
    squares = jnp.sum(hfloat * hfloat, axis=1)
    unscaled = jnp.dot(
        hfloat * gain[None, :], router.astype(f32), precision=lax.Precision.HIGHEST
    )
    both, down_all, row_sq, squares, unscaled = lax.optimization_barrier(
        (both, down_all, row_sq, squares, unscaled)
    )
    share = lax.psum_scatter(both, "tp", scatter_dimension=0, tiled=True)
    row_total, total_sq, raw_logits = lax.psum((row_sq, squares, unscaled), "tp")
    my_total = lax.dynamic_slice_in_dim(row_total, lax.axis_index("tp") * chunk, chunk)
    row_inverse = lax.rsqrt(my_total / D + 1e-05)[:, None]
    inverse = lax.rsqrt(total_sq / D + 1e-05)[:, None]
    logits = raw_logits * inverse
    picked = onehot.reshape(tok_rows, 2, EXPERTS).astype(f32)
    chosen = jnp.sum(picked * logits[:, None, :], axis=2)
    leading = jax.nn.sigmoid(chosen[:, 0] - chosen[:, 1])
    weights = jnp.stack([leading, 1.0 - leading], axis=1)
    combine = jnp.sum(placement * weights[:, :, None], axis=1)
    where = lax.axis_index("a")
    picks = [(where + step) % EXPERTS for step in range(EXPERTS)]
    mixed = combine.reshape(tok_rows, EXPERTS, CAP)
    by_step = [
        lax.dynamic_index_in_dim(mixed, (where - step) % EXPERTS, 1, keepdims=False)
        for step in range(EXPERTS)
    ]
    share, row_inverse, picks, by_step = lax.optimization_barrier(
        (share, row_inverse, picks, by_step)
    )
    ff = w_gate.shape[1]
    wide = share.astype(f32)
    gate_share, up_share = wide[:, :ff] * row_inverse, wide[:, ff:] * row_inverse
    hidden = (jax.nn.silu(gate_share) * up_share).astype(bf16)
    partial_value = jnp.stack(
        [
            jnp.dot(hidden, down_all[f], preferred_element_type=f32).astype(bf16)
            for f in range(tp)
        ]
    )

    halves = partial_value.reshape(CORES, quads, chunk, width)
    from_core = lax.all_to_all(halves, "core", 0, 0, tiled=True)
    on_chip = jnp.sum(from_core.astype(f32), axis=0).astype(bf16)
    from_chips = lax.all_to_all(on_chip, "q", 0, 0, tiled=True)
    summed = jnp.sum(from_chips.astype(f32), axis=0).astype(bf16).reshape(EXPERTS, CAP, width)

    sends = []
    for step in range(EXPERTS):
        pairs = []
        for e in range(EXPERTS):
            for q in range(quads):
                for c in range(CORES):
                    for t in range(tp):
                        dest = ((e + step) % EXPERTS, t % quads, t // quads, c * quads + q)
                        pairs.append((flat(quads, tp, e, q, c, t), flat(quads, tp, *dest)))
        piece = lax.dynamic_index_in_dim(summed, picks[step], 0, keepdims=False)
        sends.append(lax.ppermute(piece, (*EP, "tp"), pairs))
    expert_mix = sum(
        jnp.dot(weight, piece.astype(f32), precision=lax.Precision.HIGHEST)
        for weight, piece in zip(by_step, sends, strict=True)
    )
    return (hfloat + expert_mix).astype(bf16)


def flat(quads, tp, a, q, core, t):
    return ((a * quads + q) * CORES + core) * tp + t


def solution(mesh):
    groups, ep, tp = (mesh.shape[name] for name in ("groups", "ep", "tp"))
    fine = Mesh(
        mesh.devices.reshape(groups, EXPERTS, ep // (EXPERTS * CORES), CORES, tp),
        ("groups", *EP, "tp"),
    )
    rows = ("groups", *EP)
    return jax.shard_map(
        per_device,
        mesh=fine,
        in_specs=(
            P(rows, "tp"),
            P(rows, "tp"),
            P("tp", EP),
            P("tp"),
            P("tp", None),
            P(rows, None),
            P("tp", EP),
            P("tp", EP),
            P(EP, "tp"),
        ),
        out_specs=P(rows, "tp"),
        check_vma=False,
    )
```

time: 364 us -> 360 us (0.989)
  waiting for transfers between devices: 235 us -> 191 us
  blocking collectives: 55.6 us -> 84.4 us
  starting transfers between devices: 38.9 us -> 47.2 us
  matrix products: 11.5 us -> 16 us
    all_to_all x0 -> x2, blocking collectives: none -> 31.5 us  [the longest x1 26.5 us: per_device(): parts = lax.all_to_all(cut, 'tp', 0, 0, tiled=True)]
    all_to_all x3 -> x1, waiting for transfers between devices: 44.5 us -> 15.5 us  [per_device(): from_chips = lax.all_to_all(on_chip, 'q', 0, 0, tiled=True)]
    ppermute x1 -> x4, starting transfers between devices: 6.83 us -> 33.6 us  [per_device(): sends.append(lax.ppermute(piece, (*EP, 'tp'), pairs))]
    all_gather x2, waiting for transfers between devices: 162 us -> 136 us  [the longest x1 117 us: per_device(): proj_all = lax.all_gather(out_proj, EP, axis=1, tiled=True)]
    all_to_all x3 -> x1, starting transfers between devices: 22.7 us -> 4.66 us  [per_device(): from_chips = lax.all_to_all(on_chip, 'q', 0, 0, tiled=True)]
    reduce_scatter x1, waiting for transfers between devices: 25.6 us -> 33.3 us  [per_device(): share = lax.psum_scatter(both, 'tp', scatter_dimension=0, tiled=True)]
    dot_general x3 -> x13, matrix products: 6.87 us -> 11.2 us  [the longest x8 6.5 us: per_device(): jnp.dot(hidden, down_all[f], preferred_element_type=f32).astype(bf16)]
  transfers between devices with their start and end apart: 8 -> 9, of which waited for: 8 -> 7; matrix products, arithmetic and copies ran while one was open for 0% -> 4% of each run, Pallas kernels for 0% -> 0%
where the time goes in v2:
time: 360 us
  waiting for transfers between devices  191 us (53%)
  blocking collectives  84.4 us (23%)
  starting transfers between devices  47.2 us (13%)
  matrix products  16 us (4%)
  between operations  13.7 us (4%)
  other arithmetic  5.07 us (1%)
    all_gather x1, waiting for transfers between devices, per_device(): proj_all = lax.all_gather(out_proj, EP, axis=1, tiled=True)  117 us
    ppermute x4, starting transfers between devices, per_device(): sends.append(lax.ppermute(piece, (*EP, 'tp'), pairs))  33.6 us
    reduce_scatter x1, waiting for transfers between devices, per_device(): share = lax.psum_scatter(both, 'tp', scatter_dimension=0, tiled=True)  33.3 us
    all_to_all x1, blocking collectives, per_device(): parts = lax.all_to_all(cut, 'tp', 0, 0, tiled=True)  26.5 us
    psum x1, blocking collectives, per_device(): lax.psum((row_sq, squares, unscaled), 'tp')  22.5 us
    all_gather x1, waiting for transfers between devices, per_device(): down_all = lax.all_gather(w_down, 'tp', axis=0)  18.5 us
    all_to_all x1, blocking collectives, per_device(): lax.all_to_all(sectioned.reshape(EXPERTS, CAP, width), 'a', 0, 0, tiled=T...  17.2 us
    all_to_all x1, waiting for transfers between devices, per_device(): from_chips = lax.all_to_all(on_chip, 'q', 0, 0, tiled=True)  15.5 us
  transfers between devices with their start and end apart: 9, of which 7 were waited for; matrix products, arithmetic and copies ran while one was open for 4% of the time, Pallas kernels for 0%

profile of v2, /device:TPU:65, one launch (start us, length us, event | category | flops | bytes accessed | tf_op | source)
XLA Modules:
  0.0 359.6 jit_solution(8203502157461635499)
XLA Ops:
  9.8 117.1 %all-gather.4.cloned.1.call-done = bf16[512,4096]{1,0:T(8,128)(2,1)} async-done(((bf16[512,128]{1,0:T(8,128)(2,1)}), bf16[512,4096]{1,0:T(8,128)(2,1)}) %all-gather.4.cloned.1.call-update) | async-done | bytes 4194320 | tf_op jit(solution)/shard_map/all_gather | solution.py:32
  127.1 3.0 convolution_convert_fusion.1
  130.2 26.5 %all_to_all.20 = bf16[8,64,512]{2,1,0:T(8,128)(2,1)S(1)} all-to-all(bf16[8,64,512]{2,1,0:T(8,128)(2,1)S(1)} %bitcast.110), channel_id=1, replica_groups=mesh['groups'=2,'a'=4,'q'=4,'core'=2,'tp'=8] {'tp'}, dimensions={0} | all-to-all | bytes 1048576 | tf_op jit(solution)/shard_map/all_to_all | solution.py:39
  157.2 17.2 %all_to_all.21 = bf16[4,36,512]{2,1,0:T(8,128)(2,1)S(1)} all-to-all(bf16[4,36,512]{2,1,0:T(8,128)(2,1)S(1)} %reshape.45), channel_id=1, replica_groups=mesh['groups'=2,'a'=4,'q'=4,'core'=2,'tp'=8] {'a'}, dimensions={0} | all-to-all | bytes 294912 | tf_op jit(solution)/shard_map/all_to_all | solution.py:48
  174.4 13.2 %all_gather.13 = bf16[576,512]{1,0:T(8,128)(2,1)S(1)} all-gather(bf16[144,512]{1,0:T(8,128)(2,1)S(1)} %reshape.46), channel_id=1, replica_groups=mesh['groups'=2,'a'=4,'q'=4,'core'=2,'tp'=8] {'q'}, dimensions={0}, use_global_device_ids=true | all-gather | bytes 737280 | tf_op jit(solution)/shard_map/all_gather | solution.py:50
  187.6 8.8 %collective-permute-start = (bf16[576,512]{1,0:T(8,128)(2,1)S(1)}, bf16[576,512]{1,0:T(8,128)(2,1)S(1)}, u32[]{:S(2)}, u32[]{:S(2)}) collective-permute-start(bf16[576,512]{1,0:T(8,128)(2,1)S(1)} %all_gather.13), channel_id=1, source_target_pairs={{0,8},{8,0},{1,9},{9,1},{2,10},{10,2},{3,11},{11,3},{4,12},{12,4},... | collective-permute-start | bytes 1769480 | tf_op jit(solution)/shard_map/ppermute | solution.py:51
  196.7 1.3 collective-permute-done
  198.4 4.4 %convolution_convert_fusion = bf16[1152,1792]{1,0:T(8,128)(2,1)} fusion(bf16[512,1792]{1,0:T(8,128)(2,1)S(1)} %pad_maximum_fusion, f32[512]{0:T(512)S(1)} %convert_element_type.100, bf16[576,512]{1,0:T(8,128)(2,1)S(1)} %get-tuple-element.53, bf16[576,512]{1,0:T(8,128)(2,1)S(1)} %get-tuple-element.52), kind=kOutput, calls=%fused_computation | convolution fusion | flops 2119532544 | bytes 7145472 | tf_op jit(solution)/shard_map/dot_general | solution.py:58
  202.8 18.5 %all-gather.6.cloned.1.call-done = bf16[7168,512]{1,0:T(8,128)(2,1)} async-done(((bf16[896,512]{1,0:T(8,128)(2,1)}), bf16[7168,512]{1,0:T(8,128)(2,1)}) %all-gather.6.cloned.1.call-update) | async-done | bytes 7340048 | tf_op jit(solution)/shard_map/all_gather | solution.py:36
  221.4 22.5 %all-reduce = (f32[1152]{0:T(1024)S(1)}, f32[64,4]{0,1:T(4,128)S(1)}, f32[64]{0:T(128)S(1)}) all-reduce(f32[1152]{0:T(1024)S(1)} %fusion.1, f32[64,4]{0,1:T(4,128)S(1)} %fusion.43, f32[64]{0:T(128)S(1)} %get-tuple-element.33), channel_id=1, replica_groups=mesh['groups'=2,'a'=4,'q'=4,'core'=2,'tp'=8] {'tp'}, use_global_device_ids=true, to_apply=%region_7.8 | all-reduce | flops 1472 | bytes 11776 | tf_op jit(solution)/shard_map/psum | solution.py:67
  244.9 33.3 %reduce-scatter.2.cloned.1.call-done = bf16[144,1792]{1,0:T(8,128)(2,1)} async-done(((bf16[1152,1792]{1,0:T(8,128)(2,1)}), bf16[144,1792]{1,0:T(8,128)(2,1)}) %reduce-scatter.2.cloned.1.call-update) | async-done | bytes 516112 | tf_op jit(solution)/shard_map/reduce_scatter | solution.py:66
  278.2 1.3 convert_element_type.104
  279.6 1.8 fusion.5
  281.5 1.5 fusion.7
  283.0 1.5 fusion.9
  286.2 5.1 %all_to_all.22 = bf16[2,4,144,512]{3,2,1,0:T(8,128)(2,1)S(1)} all-to-all(bf16[2,4,144,512]{3,2,1,0:T(8,128)(2,1)S(1)} %bitcast.111), channel_id=1, replica_groups=mesh['groups'=2,'a'=4,'q'=4,'core'=2,'tp'=8] {'core'}, dimensions={0} | all-to-all | bytes 2359296 | tf_op jit(solution)/shard_map/all_to_all | solution.py:99
  291.3 1.2 reduce_sum.100
  292.4 4.7 %all-to-all-start.3 = ((bf16[4,144,512]{2,1,0:T(8,128)(2,1)}), bf16[4,144,512]{2,1,0:T(8,128)(2,1)S(1)}, u32[]{:S(2)}, u32[]{:S(2)}) async-start(bf16[4,144,512]{2,1,0:T(8,128)(2,1)} %reduce_sum.100), calls=%async_computation.4 | async-start | bytes 1179648 | tf_op jit(solution)/shard_map/all_to_all | solution.py:101
  297.1 15.5 %all-to-all-done.3 = bf16[4,144,512]{2,1,0:T(8,128)(2,1)S(1)} async-done(((bf16[4,144,512]{2,1,0:T(8,128)(2,1)}), bf16[4,144,512]{2,1,0:T(8,128)(2,1)S(1)}, u32[]{:S(2)}, u32[]{:S(2)}) %all-to-all-start.3) | async-done | bytes 589856 | tf_op jit(solution)/shard_map/all_to_all | solution.py:101
  312.7 11.6 %collective-permute-start.2 = (bf16[36,512]{1,0:T(8,128)(2,1)S(1)}, bf16[36,512]{1,0:T(8,128)(2,1)S(1)}, u32[]{:S(2)}, u32[]{:S(2)}) collective-permute-start(bf16[36,512]{1,0:T(8,128)(2,1)S(1)} %get-tuple-element.57), channel_id=1, source_target_pairs={{0,64},{1,80},{2,96},{3,112},{4,72},{5,88},{6,104},{7,120},{8,68},... | collective-permute-start | bytes 110600 | tf_op jit(solution)/shard_map/ppermute | solution.py:114
  324.3 8.4 %collective-permute-start.3 = (bf16[36,512]{1,0:T(8,128)(2,1)S(1)}, bf16[36,512]{1,0:T(8,128)(2,1)S(1)}, u32[]{:S(2)}, u32[]{:S(2)}) collective-permute-start(bf16[36,512]{1,0:T(8,128)(2,1)S(1)} %get-tuple-element.56), channel_id=1, source_target_pairs={{0,128},{1,144},{2,160},{3,176},{4,136},{5,152},{6,168},{7,184},{8... | collective-permute-start | bytes 110600 | tf_op jit(solution)/shard_map/ppermute | solution.py:114
  332.7 10.2 %collective-permute-start.4 = (bf16[36,512]{1,0:T(8,128)(2,1)S(1)}, bf16[36,512]{1,0:T(8,128)(2,1)S(1)}, u32[]{:S(2)}, u32[]{:S(2)}) collective-permute-start(bf16[36,512]{1,0:T(8,128)(2,1)S(1)} %get-tuple-element.55), channel_id=1, source_target_pairs={{0,192},{1,208},{2,224},{3,240},{4,200},{5,216},{6,232},{7,248},{8... | collective-permute-start | bytes 110600 | tf_op jit(solution)/shard_map/ppermute | solution.py:114
  342.9 3.5 collective-permute-start.1
  347.4 4.7 %collective-permute-done.1 = bf16[36,512]{1,0:T(8,128)(2,1)S(1)} collective-permute-done((bf16[36,512]{1,0:T(8,128)(2,1)S(1)}, bf16[36,512]{1,0:T(8,128)(2,1)S(1)}, u32[]{:S(2)}, u32[]{:S(2)}) %collective-permute-start.1) | collective-permute-done | bytes 36896 | tf_op jit(solution)/shard_map/ppermute | solution.py:114
  (73 shorter events, 9.5 us)
Async XLA Ops:
  6.5 120.5 %copy-start = (bf16[64,512]{1,0:T(8,128)(2,1)S(1)}, bf16[64,512]{1,0:T(8,128)(2,1)}, u32[]{:S(2)}) copy-start(bf16[64,512]{1,0:T(8,128)(2,1)} %param.9) | copy-start | bytes 196612
  6.6 120.4 %all-gather.4.cloned.1.call-start = ((), (), s32[]{:S(2)}) async-start(), calls=%async_computation.5 | async-start | bytes 4325376 | tf_op jit(solution)/shard_map/all_gather | solution.py:32
  7.3 213.9 %all-gather.6.cloned.1.call-start = ((), (), s32[]{:S(2)}) async-start(), calls=%async_computation.7 | async-start | bytes 8257536 | tf_op jit(solution)/shard_map/all_gather | solution.py:36
  127.0 151.1 %reduce-scatter.2.cloned.1.call-start = ((), (), s32[]{:S(2)}) async-start(), calls=%async_computation.6 | async-start | bytes 4644864 | tf_op jit(solution)/shard_map/reduce_scatter | solution.py:66
  130.1 26.6 %copy-start.3 = (bf16[64,512]{1,0:T(8,128)(2,1)S(1)}, bf16[64,512]{1,0:T(8,128)(2,1)}, u32[]{:S(2)}) copy-start(bf16[64,512]{1,0:T(8,128)(2,1)} %param.10) | copy-start | bytes 196612
  130.1 66.3 %copy-start.5 = (bf16[512]{0:T(512)(128)(2,1)S(1)}, bf16[512]{0:T(512)(128)(2,1)}, u32[]{:S(2)}) copy-start(bf16[512]{0:T(512)(128)(2,1)} %param.12) | copy-start | bytes 3076
  130.2 66.3 %copy-start.1 = (bf16[512,896]{1,0:T(8,128)(2,1)S(1)}, bf16[512,896]{1,0:T(8,128)(2,1)}, u32[]{:S(2)}) copy-start(bf16[512,896]{1,0:T(8,128)(2,1)} %param.16) | copy-start | bytes 2752516
  130.2 66.3 %copy-start.2 = (bf16[512,896]{1,0:T(8,128)(2,1)S(1)}, bf16[512,896]{1,0:T(8,128)(2,1)}, u32[]{:S(2)}) copy-start(bf16[512,896]{1,0:T(8,128)(2,1)} %param.15) | copy-start | bytes 2752516
  174.3 22.2 %copy-start.4 = (bf16[512,4]{0,1:T(4,128)(2,1)S(1)}, bf16[512,4]{0,1:T(4,128)(2,1)}, u32[]{:S(2)}) copy-start(bf16[512,4]{0,1:T(4,128)(2,1)} %param.13) | copy-start | bytes 12292
  187.6 10.4 %collective-permute-start = (bf16[576,512]{1,0:T(8,128)(2,1)S(1)}, bf16[576,512]{1,0:T(8,128)(2,1)S(1)}, u32[]{:S(2)}, u32[]{:S(2)}) collective-permute-start(bf16[576,512]{1,0:T(8,128)(2,1)S(1)} %all_gather.13), channel_id=1, source_target_pairs={{0,8},{8,0},{1,9},{9,1},{2,10},{10,2},{3,11},{11,3},{4,12},{12,4},... | collective-permute-start | bytes 1769480 | tf_op jit(solution)/shard_map/ppermute | solution.py:51
  278.1 6.4 %copy-start.6 = (bf16[7168,512]{1,0:T(8,128)(2,1)S(1)}, bf16[7168,512]{1,0:T(8,128)(2,1)}, u32[]{:S(2)}) copy-start(bf16[7168,512]{1,0:T(8,128)(2,1)} %all-gather.6.cloned.1.call-done) | copy-start | bytes 22020100
  292.4 20.1 %all-to-all-start.3 = ((bf16[4,144,512]{2,1,0:T(8,128)(2,1)}), bf16[4,144,512]{2,1,0:T(8,128)(2,1)S(1)}, u32[]{:S(2)}, u32[]{:S(2)}) async-start(bf16[4,144,512]{2,1,0:T(8,128)(2,1)} %reduce_sum.100), calls=%async_computation.4 | async-start | bytes 1179648 | tf_op jit(solution)/shard_map/all_to_all | solution.py:101
  312.7 33.6 %collective-permute-start.2 = (bf16[36,512]{1,0:T(8,128)(2,1)S(1)}, bf16[36,512]{1,0:T(8,128)(2,1)S(1)}, u32[]{:S(2)}, u32[]{:S(2)}) collective-permute-start(bf16[36,512]{1,0:T(8,128)(2,1)S(1)} %get-tuple-element.57), channel_id=1, source_target_pairs={{0,64},{1,80},{2,96},{3,112},{4,72},{5,88},{6,104},{7,120},{8,68},... | collective-permute-start | bytes 110600 | tf_op jit(solution)/shard_map/ppermute | solution.py:114
  324.3 22.3 %collective-permute-start.3 = (bf16[36,512]{1,0:T(8,128)(2,1)S(1)}, bf16[36,512]{1,0:T(8,128)(2,1)S(1)}, u32[]{:S(2)}, u32[]{:S(2)}) collective-permute-start(bf16[36,512]{1,0:T(8,128)(2,1)S(1)} %get-tuple-element.56), channel_id=1, source_target_pairs={{0,128},{1,144},{2,160},{3,176},{4,136},{5,152},{6,168},{7,184},{8... | collective-permute-start | bytes 110600 | tf_op jit(solution)/shard_map/ppermute | solution.py:114
  332.7 14.5 %collective-permute-start.4 = (bf16[36,512]{1,0:T(8,128)(2,1)S(1)}, bf16[36,512]{1,0:T(8,128)(2,1)S(1)}, u32[]{:S(2)}, u32[]{:S(2)}) collective-permute-start(bf16[36,512]{1,0:T(8,128)(2,1)S(1)} %get-tuple-element.55), channel_id=1, source_target_pairs={{0,192},{1,208},{2,224},{3,240},{4,200},{5,216},{6,232},{7,248},{8... | collective-permute-start | bytes 110600 | tf_op jit(solution)/shard_map/ppermute | solution.py:114
  342.9 9.3 %collective-permute-start.1 = (bf16[36,512]{1,0:T(8,128)(2,1)S(1)}, bf16[36,512]{1,0:T(8,128)(2,1)S(1)}, u32[]{:S(2)}, u32[]{:S(2)}) collective-permute-start(bf16[36,512]{1,0:T(8,128)(2,1)S(1)} %get-tuple-element.54), channel_id=1, source_target_pairs={{0,0},{1,16},{2,32},{3,48},{4,8},{5,24},{6,40},{7,56},{8,4},{9,20}... | collective-permute-start | bytes 110600 | tf_op jit(solution)/shard_map/ppermute | solution.py:114
Sparse Core Ops, SparseCore 0:
  9.4 117.4 all-gather.3
  129.0 92.1 all-gather.5
  224.1 53.9 reduce-scatter.1

commit v3 on v2

--- a/solution.py
+++ b/solution.py
@@ -8,6 +8,7 @@
 CAP = 36
 CORES = 2
 EP = ("a", "q", "core")
+GROUP = ("q", "core")
 
 
 def per_device(context, stream, out_proj, norm_gain, router, expert_ids, w_gate, w_up, w_down):
@@ -29,13 +30,21 @@
         (target[:, None] == columns_all[None, :]).astype(f32).reshape(tok_rows, 2, EXPERTS * CAP)
     )
     dispatch = jnp.sum(placement, axis=1).astype(bf16)
-    proj_all = lax.all_gather(out_proj, EP, axis=1, tiled=True)
-    proj_all, w_down, dispatch, placement, onehot = lax.optimization_barrier(
-        (proj_all, w_down, dispatch, placement, onehot)
+    down_all = lax.all_gather(w_down, "tp", axis=0)
+    context_all = lax.all_gather(context, GROUP, axis=0, tiled=True)
+    proj_some = lax.all_gather(out_proj, "a", axis=1, tiled=True)
+    proj_some, dispatch, placement, onehot = lax.optimization_barrier(
+        (proj_some, dispatch, placement, onehot)
     )
-    down_all = lax.all_gather(w_down, "tp", axis=0)
-    head_part = jnp.dot(context, proj_all, preferred_element_type=f32).astype(bf16)
-    cut = jnp.moveaxis(head_part.reshape(tok_rows, tp, width), 1, 0)
+    members = quads * CORES
+    head_part = jnp.dot(context_all, proj_some, preferred_element_type=f32).astype(bf16)
+    head_part = lax.all_to_all(
+        head_part.reshape(members, tok_rows, -1), GROUP, 0, 0, tiled=True
+    )
+    cols = out_proj.shape[1]
+    per = width // cols
+    cut = head_part.reshape(members // per, per, tok_rows, EXPERTS, cols)
+    cut = jnp.transpose(cut, (3, 0, 2, 1, 4)).reshape(tp, tok_rows, width)
     parts = lax.all_to_all(cut, "tp", 0, 0, tiled=True)
     hstate = (stream.astype(f32) + jnp.sum(parts.astype(f32), axis=0)).astype(bf16)
     hfloat = hstate.astype(f32)
@@ -74,16 +83,7 @@
     leading = jax.nn.sigmoid(chosen[:, 0] - chosen[:, 1])
     weights = jnp.stack([leading, 1.0 - leading], axis=1)
     combine = jnp.sum(placement * weights[:, :, None], axis=1)
-    where = lax.axis_index("a")
-    picks = [(where + step) % EXPERTS for step in range(EXPERTS)]
-    mixed = combine.reshape(tok_rows, EXPERTS, CAP)
-    by_step = [
-        lax.dynamic_index_in_dim(mixed, (where - step) % EXPERTS, 1, keepdims=False)
-        for step in range(EXPERTS)
-    ]
-    share, row_inverse, picks, by_step = lax.optimization_barrier(
-        (share, row_inverse, picks, by_step)
-    )
+    share, row_inverse, combine = lax.optimization_barrier((share, row_inverse, combine))
     ff = w_gate.shape[1]
     wide = share.astype(f32)
     gate_share, up_share = wide[:, :ff] * row_inverse, wide[:, ff:] * row_inverse
@@ -101,26 +101,22 @@
     from_chips = lax.all_to_all(on_chip, "q", 0, 0, tiled=True)
     summed = jnp.sum(from_chips.astype(f32), axis=0).astype(bf16).reshape(EXPERTS, CAP, width)
 
-    sends = []
-    for step in range(EXPERTS):
-        pairs = []
-        for e in range(EXPERTS):
-            for q in range(quads):
-                for c in range(CORES):
-                    for t in range(tp):
-                        dest = ((e + step) % EXPERTS, t % quads, t // quads, c * quads + q)
-                        pairs.append((flat(quads, tp, e, q, c, t), flat(quads, tp, *dest)))
-        piece = lax.dynamic_index_in_dim(summed, picks[step], 0, keepdims=False)
-        sends.append(lax.ppermute(piece, (*EP, "tp"), pairs))
-    expert_mix = sum(
-        jnp.dot(weight, piece.astype(f32), precision=lax.Precision.HIGHEST)
-        for weight, piece in zip(by_step, sends, strict=True)
+    pairs = []
+    for q in range(quads):
+        for c in range(CORES):
+            for t in range(tp):
+                dest = flat(tp, t % quads, t // quads, c * quads + q)
+                pairs.append((flat(tp, q, c, t), dest))
+    turned = lax.ppermute(summed, (*GROUP, "tp"), pairs)
+    back = lax.all_to_all(turned, "a", 0, 0, tiled=True)
+    expert_mix = jnp.dot(
+        combine, back.reshape(chunk, width).astype(f32), precision=lax.Precision.HIGHEST
     )
     return (hfloat + expert_mix).astype(bf16)
 
 
-def flat(quads, tp, a, q, core, t):
-    return ((a * quads + q) * CORES + core) * tp + t
+def flat(tp, q, core, t):
+    return (q * CORES + core) * tp + t
 
 
 def solution(mesh):

time: 360 us -> 333 us (0.925)
  blocking collectives: 84.4 us -> 247 us
  waiting for transfers between devices: 191 us -> 35.6 us
  starting transfers between devices: 47.2 us -> 14.7 us
    all_gather x1 -> x0, waiting for transfers between devices: 117 us -> none  [per_device(): proj_all = lax.all_gather(out_proj, EP, axis=1, tiled=True)]
    all_gather x0 -> x2, blocking collectives: none -> 97.5 us  [the longest x1 64 us: per_device(): proj_some = lax.all_gather(out_proj, 'a', axis=1, tiled=True)]
    all_to_all x0 -> x3, blocking collectives: none -> 63.6 us  [the longest x1 24.2 us: per_device(): back = lax.all_to_all(turned, 'a', 0, 0, tiled=True)]
    ppermute x4 -> x1, starting transfers between devices: 33.6 us -> 6.21 us  [per_device(): turned = lax.ppermute(summed, (*GROUP, 'tp'), pairs)]
    all_gather x1, waiting for transfers between devices: 18.5 us -> 0.01 us  [per_device(): down_all = lax.all_gather(w_down, 'tp', axis=0)]
    all_to_all x1 -> x0, waiting for transfers between devices: 15.5 us -> none  [per_device(): from_chips = lax.all_to_all(on_chip, 'q', 0, 0, tiled=True)]
    reduce_scatter x1, waiting for transfers between devices: 33.3 us -> 26.7 us  [per_device(): share = lax.psum_scatter(both, 'tp', scatter_dimension=0, tiled=True)]
    all_to_all x1 -> x0, starting transfers between devices: 4.66 us -> none  [per_device(): from_chips = lax.all_to_all(on_chip, 'q', 0, 0, tiled=True)]
  transfers between devices with their start and end apart: 9 -> 4, of which waited for: 7 -> 3; matrix products, arithmetic and copies ran while one was open for 4% -> 3% of each run, Pallas kernels for 0% -> 0%
where the time goes in v3:
time: 333 us; the launch traced here: 330 us
  blocking collectives  247 us (74%)
  waiting for transfers between devices  35.6 us (11%)
  starting transfers between devices  14.7 us (4%)
  between operations  13.8 us (4%)
  matrix products  12.5 us (4%)
  other arithmetic  4.46 us (1%)
    all_gather x1, blocking collectives, per_device(): proj_some = lax.all_gather(out_proj, 'a', axis=1, tiled=True)  64 us
    all_gather x1, blocking collectives, per_device(): context_all = lax.all_gather(context, GROUP, axis=0, tiled=True)  33.5 us
    reduce_scatter x1, waiting for transfers between devices, per_device(): share = lax.psum_scatter(both, 'tp', scatter_dimension=0, tiled=True)  26.7 us
    all_to_all x1, blocking collectives, per_device(): parts = lax.all_to_all(cut, 'tp', 0, 0, tiled=True)  24.3 us
    all_to_all x1, blocking collectives, per_device(): back = lax.all_to_all(turned, 'a', 0, 0, tiled=True)  24.2 us
    psum x1, blocking collectives, per_device(): lax.psum((row_sq, squares, unscaled), 'tp')  22.8 us
    all_to_all x1, blocking collectives, per_device(): lax.all_to_all(sectioned.reshape(EXPERTS, CAP, width), 'a', 0, 0, tiled=T...  20.5 us
    all_to_all x1, blocking collectives, per_device(): from_chips = lax.all_to_all(on_chip, 'q', 0, 0, tiled=True)  19.9 us
  transfers between devices with their start and end apart: 4, of which 3 were waited for; matrix products, arithmetic and copies ran while one was open for 3% of the time, Pallas kernels for 0%

profile of v3, /device:TPU:65, one launch (start us, length us, event | category | flops | bytes accessed | tf_op | source)
XLA Modules:
  0.0 330.2 jit_solution(4296510884938671475)
XLA Ops:
  6.6 0.7 all-gather.3.cloned.1.call-update
  7.4 0.8 copy.38
  9.0 0.7 multiply_add_fusion
  9.7 64.0 %all_gather.15 = bf16[512,512]{1,0:T(8,128)(2,1)S(1)} all-gather(bf16[512,128]{1,0:T(8,128)(2,1)} %param.11), channel_id=1, replica_groups=mesh['groups'=2,'a'=4,'q'=4,'core'=2,'tp'=8] {'a'}, dimensions={1}, use_global_device_ids=true | all-gather | bytes 655360 | tf_op jit(solution)/shard_map/all_gather | solution.py:35
  73.9 33.5 %all_gather.16 = bf16[512,512]{1,0:T(8,128)(2,1)S(1)} all-gather(bf16[64,512]{1,0:T(8,128)(2,1)S(1)} %copy-done.3), channel_id=1, replica_groups=mesh['groups'=2,'a'=4,'q'=4,'core'=2,'tp'=8] {'q','core'}, dimensions={0}, use_global_device_ids=true | all-gather | bytes 589824 | tf_op jit(solution)/shard_map/all_gather | solution.py:34
  107.8 19.5 %all_to_all.30 = bf16[8,64,512]{2,1,0:T(8,128)(2,1)S(1)} all-to-all(bf16[8,64,512]{2,1,0:T(8,128)(2,1)S(1)} %bitcast.81), channel_id=1, replica_groups=mesh['groups'=2,'a'=4,'q'=4,'core'=2,'tp'=8] {'q','core'}, dimensions={0} | all-to-all | bytes 1048576 | tf_op jit(solution)/shard_map/all_to_all | solution.py:41
  128.0 24.3 %all_to_all.31 = bf16[8,64,512]{2,1,0:T(8,128)(2,1)S(1)} all-to-all(bf16[8,64,512]{2,1,0:T(8,128)(2,1)S(1)} %reshape.52), channel_id=1, replica_groups=mesh['groups'=2,'a'=4,'q'=4,'core'=2,'tp'=8] {'tp'}, dimensions={0} | all-to-all | bytes 1048576 | tf_op jit(solution)/shard_map/all_to_all | solution.py:48
  152.8 20.5 %all_to_all.32 = bf16[4,36,512]{2,1,0:T(8,128)(2,1)S(1)} all-to-all(bf16[4,36,512]{2,1,0:T(8,128)(2,1)S(1)} %reshape.53), channel_id=1, replica_groups=mesh['groups'=2,'a'=4,'q'=4,'core'=2,'tp'=8] {'a'}, dimensions={0} | all-to-all | bytes 294912 | tf_op jit(solution)/shard_map/all_to_all | solution.py:57
  173.4 12.9 %all_gather.17 = bf16[576,512]{1,0:T(8,128)(2,1)S(1)} all-gather(bf16[144,512]{1,0:T(8,128)(2,1)S(1)} %reshape.54), channel_id=1, replica_groups=mesh['groups'=2,'a'=4,'q'=4,'core'=2,'tp'=8] {'q'}, dimensions={0}, use_global_device_ids=true | all-gather | bytes 737280 | tf_op jit(solution)/shard_map/all_gather | solution.py:59
  186.3 8.4 %collective-permute-start = (bf16[576,512]{1,0:T(8,128)(2,1)S(1)}, bf16[576,512]{1,0:T(8,128)(2,1)S(1)}, u32[]{:S(2)}, u32[]{:S(2)}) collective-permute-start(bf16[576,512]{1,0:T(8,128)(2,1)S(1)} %all_gather.17), channel_id=1, source_target_pairs={{0,8},{8,0},{1,9},{9,1},{2,10},{10,2},{3,11},{11,3},{4,12},{12,4},... | collective-permute-start | bytes 1769480 | tf_op jit(solution)/shard_map/ppermute | solution.py:60
  195.0 1.3 collective-permute-done
  196.7 4.4 %convolution_convert_fusion = bf16[1152,1792]{1,0:T(8,128)(2,1)} fusion(bf16[512,1792]{1,0:T(8,128)(2,1)S(1)} %pad_maximum_fusion, f32[512]{0:T(512)S(1)} %convert_element_type.97, bf16[576,512]{1,0:T(8,128)(2,1)S(1)} %get-tuple-element.37, bf16[576,512]{1,0:T(8,128)(2,1)S(1)} %get-tuple-element.36), kind=kOutput, calls=%fused_computation | convolution fusion | flops 2119532544 | bytes 7145472 | tf_op jit(solution)/shard_map/dot_general | solution.py:67
  201.2 22.8 %all-reduce = (f32[1152]{0:T(1024)S(1)}, f32[64,4]{0,1:T(4,128)S(1)}, f32[64]{0:T(128)S(1)}) all-reduce(f32[1152]{0:T(1024)S(1)} %fusion.1, f32[64,4]{0,1:T(4,128)S(1)} %fusion.40, f32[64]{0:T(128)S(1)} %get-tuple-element.24), channel_id=1, replica_groups=mesh['groups'=2,'a'=4,'q'=4,'core'=2,'tp'=8] {'tp'}, use_global_device_ids=true, to_apply=%region_7.8 | all-reduce | flops 1472 | bytes 11776 | tf_op jit(solution)/shard_map/psum | solution.py:76
  224.8 26.7 %reduce-scatter.2.cloned.1.call-done = bf16[144,1792]{1,0:T(8,128)(2,1)} async-done(((bf16[1152,1792]{1,0:T(8,128)(2,1)}), bf16[144,1792]{1,0:T(8,128)(2,1)}) %reduce-scatter.2.cloned.1.call-update) | async-done | bytes 516112 | tf_op jit(solution)/shard_map/reduce_scatter | solution.py:75
  251.5 1.3 convert_element_type.101
  253.0 1.8 fusion.5
  254.8 1.5 fusion.7
  256.3 1.5 fusion.9
  259.5 5.1 %all_to_all.33 = bf16[2,4,144,512]{3,2,1,0:T(8,128)(2,1)S(1)} all-to-all(bf16[2,4,144,512]{3,2,1,0:T(8,128)(2,1)S(1)} %bitcast.83), channel_id=1, replica_groups=mesh['groups'=2,'a'=4,'q'=4,'core'=2,'tp'=8] {'core'}, dimensions={0} | all-to-all | bytes 2359296 | tf_op jit(solution)/shard_map/all_to_all | solution.py:99
  265.2 19.9 %all_to_all.34 = bf16[4,144,512]{2,1,0:T(8,128)(2,1)S(1)} all-to-all(bf16[4,144,512]{2,1,0:T(8,128)(2,1)S(1)} %reduce_sum.100), channel_id=1, replica_groups=mesh['groups'=2,'a'=4,'q'=4,'core'=2,'tp'=8] {'q'}, dimensions={0} | all-to-all | bytes 1179648 | tf_op jit(solution)/shard_map/all_to_all | solution.py:101
  285.2 6.2 %collective-permute-start.1 = (bf16[4,36,512]{2,1,0:T(8,128)(2,1)S(1)}, bf16[4,36,512]{2,1,0:T(8,128)(2,1)S(1)}, u32[]{:S(2)}, u32[]{:S(2)}) collective-permute-start(bf16[4,36,512]{2,1,0:T(8,128)(2,1)S(1)} %reshape.56), channel_id=1, source_target_pairs={{0,0},{1,16},{2,32},{3,48},{4,8},{5,24},{6,40},{7,56},{8,4},{9,20}... | collective-permute-start | bytes 442376 | tf_op jit(solution)/shard_map/ppermute | solution.py:110
  291.4 6.8 %collective-permute-done.1 = bf16[4,36,512]{2,1,0:T(8,128)(2,1)S(1)} collective-permute-done((bf16[4,36,512]{2,1,0:T(8,128)(2,1)S(1)}, bf16[4,36,512]{2,1,0:T(8,128)(2,1)S(1)}, u32[]{:S(2)}, u32[]{:S(2)}) %collective-permute-start.1) | collective-permute-done | bytes 147488 | tf_op jit(solution)/shard_map/ppermute | solution.py:110
  298.2 24.2 %all_to_all.35 = bf16[4,36,512]{2,1,0:T(8,128)(2,1)S(1)} all-to-all(bf16[4,36,512]{2,1,0:T(8,128)(2,1)S(1)} %collective-permute-done.1), channel_id=1, replica_groups=mesh['groups'=2,'a'=4,'q'=4,'core'=2,'tp'=8] {'a'}, dimensions={0} | all-to-all | bytes 294912 | tf_op jit(solution)/shard_map/all_to_all | solution.py:111
  322.5 0.8 fusion.20
  (63 shorter events, 6.8 us)
Async XLA Ops:
  6.5 188.4 %copy-start = (bf16[512,4]{0,1:T(4,128)(2,1)S(1)}, bf16[512,4]{0,1:T(4,128)(2,1)}, u32[]{:S(2)}) copy-start(bf16[512,4]{0,1:T(4,128)(2,1)} %param.13) | copy-start | bytes 12292
  6.6 67.3 %copy-start.3 = (bf16[64,512]{1,0:T(8,128)(2,1)S(1)}, bf16[64,512]{1,0:T(8,128)(2,1)}, u32[]{:S(2)}) copy-start(bf16[64,512]{1,0:T(8,128)(2,1)} %param.9) | copy-start | bytes 196612
  6.6 194.6 %all-gather.3.cloned.1.call-start = ((), (), s32[]{:S(2)}) async-start(), calls=%async_computation.8 | async-start | bytes 8257536 | tf_op jit(solution)/shard_map/all_gather | solution.py:33
  7.3 244.2 %reduce-scatter.2.cloned.1.call-start = ((), (), s32[]{:S(2)}) async-start(), calls=%async_computation.7 | async-start | bytes 4644864 | tf_op jit(solution)/shard_map/reduce_scatter | solution.py:75
  127.4 25.0 %copy-start.4 = (bf16[64,512]{1,0:T(8,128)(2,1)S(1)}, bf16[64,512]{1,0:T(8,128)(2,1)}, u32[]{:S(2)}) copy-start(bf16[64,512]{1,0:T(8,128)(2,1)} %param.10) | copy-start | bytes 196612
  128.0 66.7 %copy-start.5 = (bf16[512]{0:T(512)(128)(2,1)S(1)}, bf16[512]{0:T(512)(128)(2,1)}, u32[]{:S(2)}) copy-start(bf16[512]{0:T(512)(128)(2,1)} %param.12) | copy-start | bytes 3076
  128.0 66.7 %copy-start.1 = (bf16[512,896]{1,0:T(8,128)(2,1)S(1)}, bf16[512,896]{1,0:T(8,128)(2,1)}, u32[]{:S(2)}) copy-start(bf16[512,896]{1,0:T(8,128)(2,1)} %param.16) | copy-start | bytes 2752516
  152.3 42.4 %copy-start.2 = (bf16[512,896]{1,0:T(8,128)(2,1)S(1)}, bf16[512,896]{1,0:T(8,128)(2,1)}, u32[]{:S(2)}) copy-start(bf16[512,896]{1,0:T(8,128)(2,1)} %param.15) | copy-start | bytes 2752516
  186.3 10.0 %collective-permute-start = (bf16[576,512]{1,0:T(8,128)(2,1)S(1)}, bf16[576,512]{1,0:T(8,128)(2,1)S(1)}, u32[]{:S(2)}, u32[]{:S(2)}) collective-permute-start(bf16[576,512]{1,0:T(8,128)(2,1)S(1)} %all_gather.17), channel_id=1, source_target_pairs={{0,8},{8,0},{1,9},{9,1},{2,10},{10,2},{3,11},{11,3},{4,12},{12,4},... | collective-permute-start | bytes 1769480 | tf_op jit(solution)/shard_map/ppermute | solution.py:60
  251.5 6.3 %copy-start.6 = (bf16[7168,512]{1,0:T(8,128)(2,1)S(1)}, bf16[7168,512]{1,0:T(8,128)(2,1)}, u32[]{:S(2)}) copy-start(bf16[7168,512]{1,0:T(8,128)(2,1)} %all-gather.3.cloned.1.call-done) | copy-start | bytes 22020100
  285.2 13.1 %collective-permute-start.1 = (bf16[4,36,512]{2,1,0:T(8,128)(2,1)S(1)}, bf16[4,36,512]{2,1,0:T(8,128)(2,1)S(1)}, u32[]{:S(2)}, u32[]{:S(2)}) collective-permute-start(bf16[4,36,512]{2,1,0:T(8,128)(2,1)S(1)} %reshape.56), channel_id=1, source_target_pairs={{0,0},{1,16},{2,32},{3,48},{4,8},{5,24},{6,40},{7,56},{8,4},{9,20}... | collective-permute-start | bytes 442376 | tf_op jit(solution)/shard_map/ppermute | solution.py:110
Sparse Core Ops, SparseCore 0:
  9.4 124.7 all-gather.2
  201.3 50.1 reduce-scatter.1

commit v4 on v3

--- a/solution.py
+++ b/solution.py
@@ -1,6 +1,8 @@
 import jax
 import jax.numpy as jnp
 from jax import lax
+from jax.experimental import pallas as pl
+from jax.experimental.pallas import tpu as pltpu
 from jax.sharding import Mesh, PartitionSpec as P
 
 D = 4096
@@ -8,7 +10,6 @@
 CAP = 36
 CORES = 2
 EP = ("a", "q", "core")
-GROUP = ("q", "core")
 
 
 def per_device(context, stream, out_proj, norm_gain, router, expert_ids, w_gate, w_up, w_down):
@@ -30,20 +31,17 @@
         (target[:, None] == columns_all[None, :]).astype(f32).reshape(tok_rows, 2, EXPERTS * CAP)
     )
     dispatch = jnp.sum(placement, axis=1).astype(bf16)
+    context_all = lax.all_gather(context, "q", axis=0, tiled=True)
+    proj_some = lax.all_gather(out_proj, ("a", "core"), axis=1, tiled=True)
+    context_all, proj_some, w_down, dispatch, placement, onehot = lax.optimization_barrier(
+        (context_all, proj_some, w_down, dispatch, placement, onehot)
+    )
     down_all = lax.all_gather(w_down, "tp", axis=0)
-    context_all = lax.all_gather(context, GROUP, axis=0, tiled=True)
-    proj_some = lax.all_gather(out_proj, "a", axis=1, tiled=True)
-    proj_some, dispatch, placement, onehot = lax.optimization_barrier(
-        (proj_some, dispatch, placement, onehot)
-    )
-    members = quads * CORES
     head_part = jnp.dot(context_all, proj_some, preferred_element_type=f32).astype(bf16)
-    head_part = lax.all_to_all(
-        head_part.reshape(members, tok_rows, -1), GROUP, 0, 0, tiled=True
-    )
-    cols = out_proj.shape[1]
+    head_part = lax.all_to_all(head_part.reshape(quads, tok_rows, -1), "q", 0, 0, tiled=True)
+    cols = CORES * out_proj.shape[1]
     per = width // cols
-    cut = head_part.reshape(members // per, per, tok_rows, EXPERTS, cols)
+    cut = head_part.reshape(quads // per, per, tok_rows, EXPERTS, cols)
     cut = jnp.transpose(cut, (3, 0, 2, 1, 4)).reshape(tp, tok_rows, width)
     parts = lax.all_to_all(cut, "tp", 0, 0, tiled=True)
     hstate = (stream.astype(f32) + jnp.sum(parts.astype(f32), axis=0)).astype(bf16)
@@ -84,16 +82,7 @@
     weights = jnp.stack([leading, 1.0 - leading], axis=1)
     combine = jnp.sum(placement * weights[:, :, None], axis=1)
     share, row_inverse, combine = lax.optimization_barrier((share, row_inverse, combine))
-    ff = w_gate.shape[1]
-    wide = share.astype(f32)
-    gate_share, up_share = wide[:, :ff] * row_inverse, wide[:, ff:] * row_inverse
-    hidden = (jax.nn.silu(gate_share) * up_share).astype(bf16)
-    partial_value = jnp.stack(
-        [
-            jnp.dot(hidden, down_all[f], preferred_element_type=f32).astype(bf16)
-            for f in range(tp)
-        ]
-    )
+    partial_value = down_product(share, row_inverse, down_all)
 
     halves = partial_value.reshape(CORES, quads, chunk, width)
     from_core = lax.all_to_all(halves, "core", 0, 0, tiled=True)
@@ -107,12 +96,50 @@
             for t in range(tp):
                 dest = flat(tp, t % quads, t // quads, c * quads + q)
                 pairs.append((flat(tp, q, c, t), dest))
-    turned = lax.ppermute(summed, (*GROUP, "tp"), pairs)
+    turned = lax.ppermute(summed, ("q", "core", "tp"), pairs)
     back = lax.all_to_all(turned, "a", 0, 0, tiled=True)
     expert_mix = jnp.dot(
         combine, back.reshape(chunk, width).astype(f32), precision=lax.Precision.HIGHEST
     )
     return (hfloat + expert_mix).astype(bf16)
+
+
+def down_body(share_ref, inverse_ref, down_ref, out_ref, hidden_ref):
+    ff = hidden_ref.shape[1]
+
+    @pl.when(pl.program_id(0) == 0)
+    def _():
+        wide = share_ref[...].astype(jnp.float32) * inverse_ref[...]
+        gate, up = wide[:, :ff], wide[:, ff:]
+        hidden_ref[...] = (jax.nn.silu(gate) * up).astype(jnp.bfloat16)
+
+    out_ref[0] = jnp.dot(
+        hidden_ref[...], down_ref[0], preferred_element_type=jnp.float32
+    ).astype(jnp.bfloat16)
+
+
+def down_product(share, inverse, down_all):
+    blocks, ff, width = down_all.shape
+    rows = share.shape[0]
+    return pl.pallas_call(
+        down_body,
+        grid=(blocks,),
+        in_specs=[
+            pl.BlockSpec((rows, 2 * ff), lambda i: (0, 0)),
+            pl.BlockSpec((rows, 1), lambda i: (0, 0)),
+            pl.BlockSpec((1, ff, width), lambda i: (i, 0, 0)),
+        ],
+        out_specs=pl.BlockSpec((1, rows, width), lambda i: (i, 0, 0)),
+        out_shape=jax.ShapeDtypeStruct((blocks, rows, width), jnp.bfloat16),
+        scratch_shapes=[pltpu.VMEM((rows, ff), jnp.bfloat16)],
+        cost_estimate=pl.CostEstimate(
+            flops=2 * blocks * rows * ff * width,
+            bytes_accessed=2 * blocks * (ff + rows) * width,
+            transcendentals=rows * ff,
+        ),
+        compiler_params=pltpu.CompilerParams(vmem_limit_bytes=57 * 1024 * 1024),
+        name="down",
+    )(share, inverse, down_all)
 
 
 def flat(tp, q, core, t):

time: 333 us -> 343 us (1.030)
  waiting for transfers between devices: 35.6 us -> 117 us
  blocking collectives: 247 us -> 174 us
  Pallas kernels: 0 us -> 8.06 us
  matrix products: 12.5 us -> 7.27 us
    all_gather x2 -> x1, blocking collectives: 97.5 us -> 19.7 us  [per_device(): context_all = lax.all_gather(context, 'q', axis=0, tiled=True)]
    all_gather x0 -> x1, waiting for transfers between devices: none -> 67.2 us  [per_device(): proj_some = lax.all_gather(out_proj, ('a', 'core'), axis=1, tiled=True)]
    reduce_scatter x1, waiting for transfers between devices: 26.7 us -> 40.6 us  [per_device(): share = lax.psum_scatter(both, 'tp', scatter_dimension=0, tiled=True)]
    pallas_call x0 -> x1, Pallas kernels: none -> 8.06 us  [down_product(): pl.pallas_call(down_body, grid=(blocks,), in_specs=[pl.BlockSpec((rows, 2...]
    all_to_all x1, blocking collectives: 24.3 us -> 32.3 us  [per_device(): parts = lax.all_to_all(cut, 'tp', 0, 0, tiled=True)]
    dot_general x8 -> x0, matrix products: 6.48 us -> none  [per_device(): jnp.dot(hidden, down_all[f], preferred_element_type=f32).astype(bf16)]
  transfers between devices with their start and end apart: 4 -> 5, of which waited for: 3 -> 5; matrix products, arithmetic and copies ran while one was open for 3% -> 4% of each run, Pallas kernels for 0% -> 0%
where the time goes in v4:
time: 343 us; the launch traced here: 340 us
  blocking collectives  174 us (51%)
  waiting for transfers between devices  117 us (34%)
  between operations  13.4 us (4%)
  starting transfers between devices  13.3 us (4%)
  Pallas kernels  8.06 us (2%)
  matrix products  7.27 us (2%)
  local copies, waits for them, and re-layouts  3.75 us (1%)
  other arithmetic  3.61 us (1%)
    all_gather x1, waiting for transfers between devices, per_device(): proj_some = lax.all_gather(out_proj, ('a', 'core'), axis=1, tiled=True)  67.2 us
    reduce_scatter x1, waiting for transfers between devices, per_device(): share = lax.psum_scatter(both, 'tp', scatter_dimension=0, tiled=True)  40.6 us
    all_to_all x1, blocking collectives, per_device(): parts = lax.all_to_all(cut, 'tp', 0, 0, tiled=True)  32.3 us
    all_to_all x1, blocking collectives, per_device(): back = lax.all_to_all(turned, 'a', 0, 0, tiled=True)  24.5 us
    psum x1, blocking collectives, per_device(): lax.psum((row_sq, squares, unscaled), 'tp')  21.6 us
    all_to_all x1, blocking collectives, per_device(): from_chips = lax.all_to_all(on_chip, 'q', 0, 0, tiled=True)  19.9 us
    all_gather x1, blocking collectives, per_device(): context_all = lax.all_gather(context, 'q', axis=0, tiled=True)  19.7 us
    all_to_all x1, blocking collectives, per_device(): lax.all_to_all(sectioned.reshape(EXPERTS, CAP, width), 'a', 0, 0, tiled=T...  18.8 us
  transfers between devices with their start and end apart: 5, of which 5 were waited for; matrix products, arithmetic and copies ran while one was open for 4% of the time, Pallas kernels for 0%

profile of v4, /device:TPU:65, one launch (start us, length us, event | category | flops | bytes accessed | tf_op | source)
XLA Modules:
  0.0 340.3 jit_solution(645577320484878972)
XLA Ops:
  6.6 0.7 all-gather.4.cloned.1.call-update
  7.4 0.8 copy.42
  9.0 19.7 %all_gather.15 = bf16[256,512]{1,0:T(8,128)(2,1)S(1)} all-gather(bf16[64,512]{1,0:T(8,128)(2,1)} %param.9), channel_id=1, replica_groups=mesh['groups'=2,'a'=4,'q'=4,'core'=2,'tp'=8] {'q'}, dimensions={0}, use_global_device_ids=true | all-gather | bytes 327680 | tf_op jit(solution)/shard_map/all_gather | solution.py:34
  28.6 0.7 multiply_add_fusion
  29.4 0.7 fusion.7
  30.1 67.2 %all-gather.4.cloned.1.call-done = bf16[512,1024]{1,0:T(8,128)(2,1)} async-done(((bf16[512,128]{1,0:T(8,128)(2,1)}), bf16[512,1024]{1,0:T(8,128)(2,1)}) %all-gather.4.cloned.1.call-update) | async-done | bytes 1048592 | tf_op jit(solution)/shard_map/all_gather | solution.py:35
  97.4 1.7 convolution_convert_fusion.1
  99.1 16.9 %all_to_all.30 = bf16[4,64,1024]{2,1,0:T(8,128)(2,1)S(1)} all-to-all(bf16[4,64,1024]{2,1,0:T(8,128)(2,1)S(1)} %bitcast.16), channel_id=1, replica_groups=mesh['groups'=2,'a'=4,'q'=4,'core'=2,'tp'=8] {'q'}, dimensions={0} | all-to-all | bytes 1048576 | tf_op jit(solution)/shard_map/all_to_all | solution.py:41
  117.4 32.3 %all_to_all.31 = bf16[8,64,512]{2,1,0:T(8,128)(2,1)S(1)} all-to-all(bf16[8,64,512]{2,1,0:T(8,128)(2,1)S(1)} %reshape.52), channel_id=1, replica_groups=mesh['groups'=2,'a'=4,'q'=4,'core'=2,'tp'=8] {'tp'}, dimensions={0} | all-to-all | bytes 1048576 | tf_op jit(solution)/shard_map/all_to_all | solution.py:46
  150.2 18.8 %all_to_all.32 = bf16[4,36,512]{2,1,0:T(8,128)(2,1)S(1)} all-to-all(bf16[4,36,512]{2,1,0:T(8,128)(2,1)S(1)} %reshape.53), channel_id=1, replica_groups=mesh['groups'=2,'a'=4,'q'=4,'core'=2,'tp'=8] {'a'}, dimensions={0} | all-to-all | bytes 294912 | tf_op jit(solution)/shard_map/all_to_all | solution.py:55
  169.0 13.6 %all_gather.17 = bf16[576,512]{1,0:T(8,128)(2,1)S(1)} all-gather(bf16[144,512]{1,0:T(8,128)(2,1)S(1)} %reshape.54), channel_id=1, replica_groups=mesh['groups'=2,'a'=4,'q'=4,'core'=2,'tp'=8] {'q'}, dimensions={0}, use_global_device_ids=true | all-gather | bytes 737280 | tf_op jit(solution)/shard_map/all_gather | solution.py:57
  182.7 6.9 %collective-permute-start = (bf16[576,512]{1,0:T(8,128)(2,1)S(1)}, bf16[576,512]{1,0:T(8,128)(2,1)S(1)}, u32[]{:S(2)}, u32[]{:S(2)}) collective-permute-start(bf16[576,512]{1,0:T(8,128)(2,1)S(1)} %all_gather.17), channel_id=1, source_target_pairs={{0,8},{8,0},{1,9},{9,1},{2,10},{10,2},{3,11},{11,3},{4,12},{12,4},... | collective-permute-start | bytes 1769480 | tf_op jit(solution)/shard_map/ppermute | solution.py:58
  189.9 1.3 collective-permute-done
  191.5 4.4 %convolution_convert_fusion = bf16[1152,1792]{1,0:T(8,128)(2,1)} fusion(bf16[512,1792]{1,0:T(8,128)(2,1)S(1)} %pad_maximum_fusion, f32[512]{0:T(512)S(1)} %convert_element_type.63, bf16[576,512]{1,0:T(8,128)(2,1)S(1)} %get-tuple-element.41, bf16[576,512]{1,0:T(8,128)(2,1)S(1)} %get-tuple-element.40), kind=kOutput, calls=%fused_computation | convolution fusion | flops 2119532544 | bytes 7145472 | tf_op jit(solution)/shard_map/dot_general | solution.py:65
  196.6 21.6 %all-reduce = (f32[1152]{0:T(1024)S(1)}, f32[64,4]{0,1:T(4,128)S(1)}, f32[64]{0:T(128)S(1)}) all-reduce(f32[1152]{0:T(1024)S(1)} %fusion.1, f32[64,4]{0,1:T(4,128)S(1)} %fusion.6, f32[64]{0:T(128)S(1)} %get-tuple-element.28), channel_id=1, replica_groups=mesh['groups'=2,'a'=4,'q'=4,'core'=2,'tp'=8] {'tp'}, use_global_device_ids=true, to_apply=%region_7.8 | all-reduce | flops 1472 | bytes 11776 | tf_op jit(solution)/shard_map/psum | solution.py:74
  219.0 40.6 %reduce-scatter.2.cloned.1.call-done.share_ref = bf16[144,1792]{1,0:T(8,128)(2,1)} async-done(((bf16[1152,1792]{1,0:T(8,128)(2,1)}), bf16[144,1792]{1,0:T(8,128)(2,1)}) %reduce-scatter.2.cloned.1.call-update) | async-done | bytes 516112 | tf_op jit(solution)/shard_map/reduce_scatter | solution.py:73
  259.6 0.7 copy.48.inverse_ref
  260.4 8.1 %down.1 = bf16[8,144,512]{2,1,0:T(8,128)(2,1)} custom-call(bf16[144,1792]{1,0:T(8,128)(2,1)} %reduce-scatter.2.cloned.1.call-done.share_ref, f32[144,1]{1,0:T(8,128)} %copy.48.inverse_ref, bf16[8,896,512]{2,1,0:T(8,128)(2,1)} %bitcast.14), custom_call_target="tpu_custom_call" | custom-call | flops 1056964608 | bytes 8519680 | tf_op jit(solution)/shard_map/down/pallas_call | solution.py:124
  268.4 6.2 %all_to_all.33 = bf16[2,4,144,512]{3,2,1,0:T(8,128)(2,1)S(1)} all-to-all(bf16[2,4,144,512]{3,2,1,0:T(8,128)(2,1)} %bitcast.15), channel_id=1, replica_groups=mesh['groups'=2,'a'=4,'q'=4,'core'=2,'tp'=8] {'core'}, dimensions={0} | all-to-all | bytes 2359296 | tf_op jit(solution)/shard_map/all_to_all | solution.py:88
  275.2 19.9 %all_to_all.34 = bf16[4,144,512]{2,1,0:T(8,128)(2,1)S(1)} all-to-all(bf16[4,144,512]{2,1,0:T(8,128)(2,1)S(1)} %reduce_sum.100), channel_id=1, replica_groups=mesh['groups'=2,'a'=4,'q'=4,'core'=2,'tp'=8] {'q'}, dimensions={0} | all-to-all | bytes 1179648 | tf_op jit(solution)/shard_map/all_to_all | solution.py:90
  295.2 6.4 %collective-permute-start.1 = (bf16[4,36,512]{2,1,0:T(8,128)(2,1)S(1)}, bf16[4,36,512]{2,1,0:T(8,128)(2,1)S(1)}, u32[]{:S(2)}, u32[]{:S(2)}) collective-permute-start(bf16[4,36,512]{2,1,0:T(8,128)(2,1)S(1)} %reshape.56), channel_id=1, source_target_pairs={{0,0},{1,16},{2,32},{3,48},{4,8},{5,24},{6,40},{7,56},{8,4},{9,20}... | collective-permute-start | bytes 442376 | tf_op jit(solution)/shard_map/ppermute | solution.py:99
  301.6 6.8 %collective-permute-done.1 = bf16[4,36,512]{2,1,0:T(8,128)(2,1)S(1)} collective-permute-done((bf16[4,36,512]{2,1,0:T(8,128)(2,1)S(1)}, bf16[4,36,512]{2,1,0:T(8,128)(2,1)S(1)}, u32[]{:S(2)}, u32[]{:S(2)}) %collective-permute-start.1) | collective-permute-done | bytes 147488 | tf_op jit(solution)/shard_map/ppermute | solution.py:99
  308.4 24.5 %all_to_all.35 = bf16[4,36,512]{2,1,0:T(8,128)(2,1)S(1)} all-to-all(bf16[4,36,512]{2,1,0:T(8,128)(2,1)S(1)} %collective-permute-done.1), channel_id=1, replica_groups=mesh['groups'=2,'a'=4,'q'=4,'core'=2,'tp'=8] {'a'}, dimensions={0} | all-to-all | bytes 294912 | tf_op jit(solution)/shard_map/all_to_all | solution.py:100
  332.9 0.8 fusion.4
  (59 shorter events, 5.7 us)
Async XLA Ops:
  6.5 183.2 %copy-start = (bf16[512,4]{0,1:T(4,128)(2,1)S(1)}, bf16[512,4]{0,1:T(4,128)(2,1)}, u32[]{:S(2)}) copy-start(bf16[512,4]{0,1:T(4,128)(2,1)} %param.13) | copy-start | bytes 12292
  6.6 90.8 %all-gather.4.cloned.1.call-start = ((), (), s32[]{:S(2)}) async-start(), calls=%async_computation.7 | async-start | bytes 1179648 | tf_op jit(solution)/shard_map/all_gather | solution.py:35
  7.3 189.2 %all-gather.6.cloned.1.call-start = ((), (), s32[]{:S(2)}) async-start(), calls=%async_computation.9 | async-start | bytes 8257536 | tf_op jit(solution)/shard_map/all_gather | solution.py:39
  8.4 108.0 %copy-start.3 = (s32[128,4]{1,0:T(8,128)}, s32[128,4]{1,0:T(8,128)S(1)}, u32[]{:S(2)}) copy-start(s32[128,4]{1,0:T(8,128)S(1)} %fusion.9) | copy-start | bytes 6148
  97.4 162.3 %reduce-scatter.2.cloned.1.call-start = ((), (), s32[]{:S(2)}) async-start(), calls=%async_computation.8 | async-start | bytes 4644864 | tf_op jit(solution)/shard_map/reduce_scatter | solution.py:73
  116.0 33.7 %copy-start.6 = (bf16[64,512]{1,0:T(8,128)(2,1)S(1)}, bf16[64,512]{1,0:T(8,128)(2,1)}, u32[]{:S(2)}) copy-start(bf16[64,512]{1,0:T(8,128)(2,1)} %param.10) | copy-start | bytes 196612
  117.0 72.6 %copy-start.7 = (bf16[512]{0:T(512)(128)(2,1)S(1)}, bf16[512]{0:T(512)(128)(2,1)}, u32[]{:S(2)}) copy-start(bf16[512]{0:T(512)(128)(2,1)} %param.12) | copy-start | bytes 3076
  117.0 72.6 %copy-start.1 = (bf16[512,896]{1,0:T(8,128)(2,1)S(1)}, bf16[512,896]{1,0:T(8,128)(2,1)}, u32[]{:S(2)}) copy-start(bf16[512,896]{1,0:T(8,128)(2,1)} %param.16) | copy-start | bytes 2752516
  117.0 72.6 %copy-start.2 = (bf16[512,896]{1,0:T(8,128)(2,1)S(1)}, bf16[512,896]{1,0:T(8,128)(2,1)}, u32[]{:S(2)}) copy-start(bf16[512,896]{1,0:T(8,128)(2,1)} %param.15) | copy-start | bytes 2752516
  182.7 8.5 %collective-permute-start = (bf16[576,512]{1,0:T(8,128)(2,1)S(1)}, bf16[576,512]{1,0:T(8,128)(2,1)S(1)}, u32[]{:S(2)}, u32[]{:S(2)}) collective-permute-start(bf16[576,512]{1,0:T(8,128)(2,1)S(1)} %all_gather.17), channel_id=1, source_target_pairs={{0,8},{8,0},{1,9},{9,1},{2,10},{10,2},{3,11},{11,3},{4,12},{12,4},... | collective-permute-start | bytes 1769480 | tf_op jit(solution)/shard_map/ppermute | solution.py:58
  195.9 22.4 %copy-start.4 = (s32[128,4]{1,0:T(8,128)S(1)}, s32[128,4]{1,0:T(8,128)}, u32[]{:S(2)}) copy-start(s32[128,4]{1,0:T(8,128)} %copy-done.3) | copy-start | bytes 6148
  195.9 23.0 %copy-start.5 = (f32[64,2,144]{2,0,1:T(8,128)S(1)}, f32[64,2,144]{2,0,1:T(8,128)}, u32[]{:S(2)}) copy-start(f32[64,2,144]{2,0,1:T(8,128)} %fusion.7) | copy-start | bytes 221188
  295.2 13.2 %collective-permute-start.1 = (bf16[4,36,512]{2,1,0:T(8,128)(2,1)S(1)}, bf16[4,36,512]{2,1,0:T(8,128)(2,1)S(1)}, u32[]{:S(2)}, u32[]{:S(2)}) collective-permute-start(bf16[4,36,512]{2,1,0:T(8,128)(2,1)S(1)} %reshape.56), channel_id=1, source_target_pairs={{0,0},{1,16},{2,32},{3,48},{4,8},{5,24},{6,40},{7,56},{8,4},{9,20}... | collective-permute-start | bytes 442376 | tf_op jit(solution)/shard_map/ppermute | solution.py:99
Sparse Core Ops, SparseCore 0:
  9.5 87.7 all-gather.3
  99.4 97.1 all-gather.5
  199.4 60.1 reduce-scatter.1

commit v5 on v3

--- a/solution.py
+++ b/solution.py
@@ -8,7 +8,6 @@
 CAP = 36
 CORES = 2
 EP = ("a", "q", "core")
-GROUP = ("q", "core")
 
 
 def per_device(context, stream, out_proj, norm_gain, router, expert_ids, w_gate, w_up, w_down):
@@ -31,22 +30,29 @@
     )
     dispatch = jnp.sum(placement, axis=1).astype(bf16)
     down_all = lax.all_gather(w_down, "tp", axis=0)
-    context_all = lax.all_gather(context, GROUP, axis=0, tiled=True)
-    proj_some = lax.all_gather(out_proj, "a", axis=1, tiled=True)
-    proj_some, dispatch, placement, onehot = lax.optimization_barrier(
-        (proj_some, dispatch, placement, onehot)
+    proj_own = lax.all_gather(out_proj, "a", axis=1, tiled=True)
+    context, proj_own, dispatch, placement, onehot = lax.optimization_barrier(
+        (context, proj_own, dispatch, placement, onehot)
     )
-    members = quads * CORES
-    head_part = jnp.dot(context_all, proj_some, preferred_element_type=f32).astype(bf16)
-    head_part = lax.all_to_all(
-        head_part.reshape(members, tok_rows, -1), GROUP, 0, 0, tiled=True
+    proj_other = lax.ppermute(proj_own, "core", swap)
+    context_all = lax.all_gather(context, "q", axis=0, tiled=True)
+    context_all, proj_other = lax.optimization_barrier((context_all, proj_other))
+    first = lax.axis_index("core") == 0
+    own, other = (
+        jnp.dot(context_all, part, preferred_element_type=f32).astype(bf16)
+        for part in (proj_own, proj_other)
     )
+    head_part = jnp.concatenate(
+        [jnp.where(first, own, other), jnp.where(first, other, own)], axis=1
+    )
+    head_part = lax.all_to_all(head_part.reshape(quads, tok_rows, -1), "q", 0, 0, tiled=True)
     cols = out_proj.shape[1]
-    per = width // cols
-    cut = head_part.reshape(members // per, per, tok_rows, EXPERTS, cols)
-    cut = jnp.transpose(cut, (3, 0, 2, 1, 4)).reshape(tp, tok_rows, width)
+    per = width // (CORES * cols)
+    cut = head_part.reshape(quads // per, per, tok_rows, CORES, EXPERTS, cols)
+    cut = jnp.transpose(cut, (4, 0, 2, 1, 3, 5)).reshape(tp, tok_rows, width)
     parts = lax.all_to_all(cut, "tp", 0, 0, tiled=True)
-    hstate = (stream.astype(f32) + jnp.sum(parts.astype(f32), axis=0)).astype(bf16)
+    attention = jnp.sum(parts.astype(f32), axis=0)
+    hstate = (stream.astype(f32) + attention).astype(bf16)
     hfloat = hstate.astype(f32)
     gain = norm_gain.astype(f32)
 
@@ -58,7 +64,6 @@
     chunk = EXPERTS * CAP
     chip = lax.all_gather(mine.reshape(chunk, width), "q", axis=0, tiled=True)
     other = lax.ppermute(chip, "core", swap)
-    first = lax.axis_index("core") == 0
     rows = jnp.concatenate([jnp.where(first, chip, other), jnp.where(first, other, chip)], axis=0)
 
     rfloat = rows.astype(f32)
@@ -107,7 +112,7 @@
             for t in range(tp):
                 dest = flat(tp, t % quads, t // quads, c * quads + q)
                 pairs.append((flat(tp, q, c, t), dest))
-    turned = lax.ppermute(summed, (*GROUP, "tp"), pairs)
+    turned = lax.ppermute(summed, ("q", "core", "tp"), pairs)
     back = lax.all_to_all(turned, "a", 0, 0, tiled=True)
     expert_mix = jnp.dot(
         combine, back.reshape(chunk, width).astype(f32), precision=lax.Precision.HIGHEST

time: 333 us -> 332 us (level)
  blocking collectives: 247 us -> 233 us
  starting transfers between devices: 14.7 us -> 28.1 us
    all_gather x2, blocking collectives: 97.5 us -> 82.9 us  [the longest x1 64 us: per_device(): proj_own = lax.all_gather(out_proj, 'a', axis=1, tiled=True)]
    ppermute x1 -> x2, starting transfers between devices: 6.21 us -> 20.3 us  [the longest x1 14.1 us: per_device(): proj_other = lax.ppermute(proj_own, 'core', swap)]
    all_to_all x1, blocking collectives: 20.5 us -> 24.1 us  [per_device(): lax.all_to_all(sectioned.reshape(EXPERTS, CAP, width), 'a', 0, 0, tiled=T...]
    ppermute x1 -> x2, waiting for transfers between devices: 6.85 us -> 6.88 us  [the longest x1 6.88 us: per_device(): turned = lax.ppermute(summed, ('q', 'core', 'tp'), pairs)]
  transfers between devices with their start and end apart: 4 -> 5, of which waited for: 3 -> 3; matrix products, arithmetic and copies ran while one was open for 3% -> 3% of each run, Pallas kernels for 0% -> 0%
where the time goes in v5:
time: 332 us; the launch traced here: 329 us
  blocking collectives  233 us (70%)
  waiting for transfers between devices  34.5 us (10%)
  starting transfers between devices  28.1 us (8%)
  between operations  13.8 us (4%)
  matrix products  12.7 us (4%)
  other arithmetic  4.52 us (1%)
    all_gather x1, blocking collectives, per_device(): proj_own = lax.all_gather(out_proj, 'a', axis=1, tiled=True)  64 us
    reduce_scatter x1, waiting for transfers between devices, per_device(): share = lax.psum_scatter(both, 'tp', scatter_dimension=0, tiled=True)  25.6 us
    all_to_all x1, blocking collectives, per_device(): back = lax.all_to_all(turned, 'a', 0, 0, tiled=True)  24.2 us
    psum x1, blocking collectives, per_device(): lax.psum((row_sq, squares, unscaled), 'tp')  24.1 us
    all_to_all x1, blocking collectives, per_device(): lax.all_to_all(sectioned.reshape(EXPERTS, CAP, width), 'a', 0, 0, tiled=T...  24.1 us
    all_to_all x1, blocking collectives, per_device(): parts = lax.all_to_all(cut, 'tp', 0, 0, tiled=True)  22.6 us
    all_to_all x1, blocking collectives, per_device(): from_chips = lax.all_to_all(on_chip, 'q', 0, 0, tiled=True)  19.9 us
    all_gather x1, blocking collectives, per_device(): context_all = lax.all_gather(context, 'q', axis=0, tiled=True)  18.8 us
  transfers between devices with their start and end apart: 5, of which 3 were waited for; matrix products, arithmetic and copies ran while one was open for 3% of the time, Pallas kernels for 0%

profile of v5, /device:TPU:65, one launch (start us, length us, event | category | flops | bytes accessed | tf_op | source)
XLA Modules:
  0.0 329.1 jit_solution(10622154643786828563)
XLA Ops:
  6.6 0.7 all-gather.3.cloned.1.call-update
  7.4 0.8 copy.38
  9.7 64.0 %all_gather.15 = bf16[512,512]{1,0:T(8,128)(2,1)S(1)} all-gather(bf16[512,128]{1,0:T(8,128)(2,1)} %param.11), channel_id=1, replica_groups=mesh['groups'=2,'a'=4,'q'=4,'core'=2,'tp'=8] {'a'}, dimensions={1}, use_global_device_ids=true | all-gather | bytes 655360 | tf_op jit(solution)/shard_map/all_gather | solution.py:33
  73.9 14.1 %collective-permute-start = (bf16[512,512]{1,0:T(8,128)(2,1)S(1)}, bf16[512,512]{1,0:T(8,128)(2,1)S(1)}, u32[]{:S(2)}, u32[]{:S(2)}) collective-permute-start(bf16[512,512]{1,0:T(8,128)(2,1)S(1)} %all_gather.15), channel_id=1, source_target_pairs={{0,8},{8,0},{1,9},{9,1},{2,10},{10,2},{3,11},{11,3},{4,12},{12,4},... | collective-permute-start | bytes 1572872 | tf_op jit(solution)/shard_map/ppermute | solution.py:37
  88.0 18.8 %all_gather.16 = bf16[256,512]{1,0:T(8,128)(2,1)S(1)} all-gather(bf16[64,512]{1,0:T(8,128)(2,1)S(1)} %copy-done.3), channel_id=1, replica_groups=mesh['groups'=2,'a'=4,'q'=4,'core'=2,'tp'=8] {'q'}, dimensions={0}, use_global_device_ids=true | all-gather | bytes 327680 | tf_op jit(solution)/shard_map/all_gather | solution.py:38
  107.5 17.3 %all_to_all.30 = bf16[4,64,1024]{2,1,0:T(8,128)(2,1)S(1)} all-to-all(bf16[4,64,1024]{2,1,0:T(8,128)(2,1)S(1)} %bitcast.81), channel_id=1, replica_groups=mesh['groups'=2,'a'=4,'q'=4,'core'=2,'tp'=8] {'q'}, dimensions={0} | all-to-all | bytes 1048576 | tf_op jit(solution)/shard_map/all_to_all | solution.py:48
  125.9 22.6 %all_to_all.31 = bf16[8,64,512]{2,1,0:T(8,128)(2,1)S(1)} all-to-all(bf16[8,64,512]{2,1,0:T(8,128)(2,1)S(1)} %reshape.52), channel_id=1, replica_groups=mesh['groups'=2,'a'=4,'q'=4,'core'=2,'tp'=8] {'tp'}, dimensions={0} | all-to-all | bytes 1048576 | tf_op jit(solution)/shard_map/all_to_all | solution.py:53
  149.0 24.1 %all_to_all.32 = bf16[4,36,512]{2,1,0:T(8,128)(2,1)S(1)} all-to-all(bf16[4,36,512]{2,1,0:T(8,128)(2,1)S(1)} %reshape.53), channel_id=1, replica_groups=mesh['groups'=2,'a'=4,'q'=4,'core'=2,'tp'=8] {'a'}, dimensions={0} | all-to-all | bytes 294912 | tf_op jit(solution)/shard_map/all_to_all | solution.py:63
  173.1 12.6 %all_gather.17 = bf16[576,512]{1,0:T(8,128)(2,1)S(1)} all-gather(bf16[144,512]{1,0:T(8,128)(2,1)S(1)} %reshape.54), channel_id=1, replica_groups=mesh['groups'=2,'a'=4,'q'=4,'core'=2,'tp'=8] {'q'}, dimensions={0}, use_global_device_ids=true | all-gather | bytes 737280 | tf_op jit(solution)/shard_map/all_gather | solution.py:65
  185.6 7.7 %collective-permute-start.1 = (bf16[576,512]{1,0:T(8,128)(2,1)S(1)}, bf16[576,512]{1,0:T(8,128)(2,1)S(1)}, u32[]{:S(2)}, u32[]{:S(2)}) collective-permute-start(bf16[576,512]{1,0:T(8,128)(2,1)S(1)} %all_gather.17), channel_id=1, source_target_pairs={{0,8},{8,0},{1,9},{9,1},{2,10},{10,2},{3,11},{11,3},{4,12},{12,4},... | collective-permute-start | bytes 1769480 | tf_op jit(solution)/shard_map/ppermute | solution.py:66
  193.7 1.3 collective-permute-done.1
  195.4 4.4 %convolution_convert_fusion = bf16[1152,1792]{1,0:T(8,128)(2,1)} fusion(bf16[512,1792]{1,0:T(8,128)(2,1)S(1)} %pad_maximum_fusion, f32[512]{0:T(512)S(1)} %convert_element_type.97, bf16[576,512]{1,0:T(8,128)(2,1)S(1)} %get-tuple-element.43, bf16[576,512]{1,0:T(8,128)(2,1)S(1)} %get-tuple-element.42), kind=kOutput, calls=%fused_computation | convolution fusion | flops 2119532544 | bytes 7145472 | tf_op jit(solution)/shard_map/dot_general | solution.py:72
  199.8 24.1 %all-reduce = (f32[1152]{0:T(1024)S(1)}, f32[64,4]{0,1:T(4,128)S(1)}, f32[64]{0:T(128)S(1)}) all-reduce(f32[1152]{0:T(1024)S(1)} %fusion.1, f32[64,4]{0,1:T(4,128)S(1)} %fusion.40, f32[64]{0:T(128)S(1)} %get-tuple-element.30), channel_id=1, replica_groups=mesh['groups'=2,'a'=4,'q'=4,'core'=2,'tp'=8] {'tp'}, use_global_device_ids=true, to_apply=%region_7.8 | all-reduce | flops 1472 | bytes 11776 | tf_op jit(solution)/shard_map/psum | solution.py:81
  224.8 25.6 %reduce-scatter.2.cloned.1.call-done = bf16[144,1792]{1,0:T(8,128)(2,1)} async-done(((bf16[1152,1792]{1,0:T(8,128)(2,1)}), bf16[144,1792]{1,0:T(8,128)(2,1)}) %reduce-scatter.2.cloned.1.call-update) | async-done | bytes 516112 | tf_op jit(solution)/shard_map/reduce_scatter | solution.py:80
  250.4 1.3 convert_element_type.101
  251.8 1.8 fusion.5
  253.7 1.5 fusion.7
  255.2 1.5 fusion.9
  258.4 5.1 %all_to_all.33 = bf16[2,4,144,512]{3,2,1,0:T(8,128)(2,1)S(1)} all-to-all(bf16[2,4,144,512]{3,2,1,0:T(8,128)(2,1)S(1)} %bitcast.83), channel_id=1, replica_groups=mesh['groups'=2,'a'=4,'q'=4,'core'=2,'tp'=8] {'core'}, dimensions={0} | all-to-all | bytes 2359296 | tf_op jit(solution)/shard_map/all_to_all | solution.py:104
  264.0 19.9 %all_to_all.34 = bf16[4,144,512]{2,1,0:T(8,128)(2,1)S(1)} all-to-all(bf16[4,144,512]{2,1,0:T(8,128)(2,1)S(1)} %reduce_sum.100), channel_id=1, replica_groups=mesh['groups'=2,'a'=4,'q'=4,'core'=2,'tp'=8] {'q'}, dimensions={0} | all-to-all | bytes 1179648 | tf_op jit(solution)/shard_map/all_to_all | solution.py:106
  284.1 6.2 %collective-permute-start.2 = (bf16[4,36,512]{2,1,0:T(8,128)(2,1)S(1)}, bf16[4,36,512]{2,1,0:T(8,128)(2,1)S(1)}, u32[]{:S(2)}, u32[]{:S(2)}) collective-permute-start(bf16[4,36,512]{2,1,0:T(8,128)(2,1)S(1)} %reshape.56), channel_id=1, source_target_pairs={{0,0},{1,16},{2,32},{3,48},{4,8},{5,24},{6,40},{7,56},{8,4},{9,20}... | collective-permute-start | bytes 442376 | tf_op jit(solution)/shard_map/ppermute | solution.py:115
  290.3 6.9 %collective-permute-done.2 = bf16[4,36,512]{2,1,0:T(8,128)(2,1)S(1)} collective-permute-done((bf16[4,36,512]{2,1,0:T(8,128)(2,1)S(1)}, bf16[4,36,512]{2,1,0:T(8,128)(2,1)S(1)}, u32[]{:S(2)}, u32[]{:S(2)}) %collective-permute-start.2) | collective-permute-done | bytes 147488 | tf_op jit(solution)/shard_map/ppermute | solution.py:115
  297.1 24.2 %all_to_all.35 = bf16[4,36,512]{2,1,0:T(8,128)(2,1)S(1)} all-to-all(bf16[4,36,512]{2,1,0:T(8,128)(2,1)S(1)} %collective-permute-done.2), channel_id=1, replica_groups=mesh['groups'=2,'a'=4,'q'=4,'core'=2,'tp'=8] {'a'}, dimensions={0} | all-to-all | bytes 294912 | tf_op jit(solution)/shard_map/all_to_all | solution.py:116
  321.4 0.8 fusion.20
  (67 shorter events, 7.9 us)
Async XLA Ops:
  6.5 187.0 %copy-start = (bf16[512,4]{0,1:T(4,128)(2,1)S(1)}, bf16[512,4]{0,1:T(4,128)(2,1)}, u32[]{:S(2)}) copy-start(bf16[512,4]{0,1:T(4,128)(2,1)} %param.13) | copy-start | bytes 12292
  6.6 81.4 %copy-start.3 = (bf16[64,512]{1,0:T(8,128)(2,1)S(1)}, bf16[64,512]{1,0:T(8,128)(2,1)}, u32[]{:S(2)}) copy-start(bf16[64,512]{1,0:T(8,128)(2,1)} %param.9) | copy-start | bytes 196612
  6.6 193.2 %all-gather.3.cloned.1.call-start = ((), (), s32[]{:S(2)}) async-start(), calls=%async_computation.8 | async-start | bytes 8257536 | tf_op jit(solution)/shard_map/all_gather | solution.py:32
  7.3 243.0 %reduce-scatter.2.cloned.1.call-start = ((), (), s32[]{:S(2)}) async-start(), calls=%async_computation.7 | async-start | bytes 4644864 | tf_op jit(solution)/shard_map/reduce_scatter | solution.py:80
  73.9 33.0 %collective-permute-start = (bf16[512,512]{1,0:T(8,128)(2,1)S(1)}, bf16[512,512]{1,0:T(8,128)(2,1)S(1)}, u32[]{:S(2)}, u32[]{:S(2)}) collective-permute-start(bf16[512,512]{1,0:T(8,128)(2,1)S(1)} %all_gather.15), channel_id=1, source_target_pairs={{0,8},{8,0},{1,9},{9,1},{2,10},{10,2},{3,11},{11,3},{4,12},{12,4},... | collective-permute-start | bytes 1572872 | tf_op jit(solution)/shard_map/ppermute | solution.py:37
  125.2 23.4 %copy-start.4 = (bf16[64,512]{1,0:T(8,128)(2,1)S(1)}, bf16[64,512]{1,0:T(8,128)(2,1)}, u32[]{:S(2)}) copy-start(bf16[64,512]{1,0:T(8,128)(2,1)} %param.10) | copy-start | bytes 196612
  125.9 67.5 %copy-start.5 = (bf16[512]{0:T(512)(128)(2,1)S(1)}, bf16[512]{0:T(512)(128)(2,1)}, u32[]{:S(2)}) copy-start(bf16[512]{0:T(512)(128)(2,1)} %param.12) | copy-start | bytes 3076
  125.9 67.5 %copy-start.1 = (bf16[512,896]{1,0:T(8,128)(2,1)S(1)}, bf16[512,896]{1,0:T(8,128)(2,1)}, u32[]{:S(2)}) copy-start(bf16[512,896]{1,0:T(8,128)(2,1)} %param.16) | copy-start | bytes 2752516
  148.5 44.9 %copy-start.2 = (bf16[512,896]{1,0:T(8,128)(2,1)S(1)}, bf16[512,896]{1,0:T(8,128)(2,1)}, u32[]{:S(2)}) copy-start(bf16[512,896]{1,0:T(8,128)(2,1)} %param.15) | copy-start | bytes 2752516
  185.6 9.3 %collective-permute-start.1 = (bf16[576,512]{1,0:T(8,128)(2,1)S(1)}, bf16[576,512]{1,0:T(8,128)(2,1)S(1)}, u32[]{:S(2)}, u32[]{:S(2)}) collective-permute-start(bf16[576,512]{1,0:T(8,128)(2,1)S(1)} %all_gather.17), channel_id=1, source_target_pairs={{0,8},{8,0},{1,9},{9,1},{2,10},{10,2},{3,11},{11,3},{4,12},{12,4},... | collective-permute-start | bytes 1769480 | tf_op jit(solution)/shard_map/ppermute | solution.py:66
  250.4 6.3 %copy-start.6 = (bf16[7168,512]{1,0:T(8,128)(2,1)S(1)}, bf16[7168,512]{1,0:T(8,128)(2,1)}, u32[]{:S(2)}) copy-start(bf16[7168,512]{1,0:T(8,128)(2,1)} %all-gather.3.cloned.1.call-done) | copy-start | bytes 22020100
  284.1 13.1 %collective-permute-start.2 = (bf16[4,36,512]{2,1,0:T(8,128)(2,1)S(1)}, bf16[4,36,512]{2,1,0:T(8,128)(2,1)S(1)}, u32[]{:S(2)}, u32[]{:S(2)}) collective-permute-start(bf16[4,36,512]{2,1,0:T(8,128)(2,1)S(1)} %reshape.56), channel_id=1, source_target_pairs={{0,0},{1,16},{2,32},{3,48},{4,8},{5,24},{6,40},{7,56},{8,4},{9,20}... | collective-permute-start | bytes 442376 | tf_op jit(solution)/shard_map/ppermute | solution.py:115
Sparse Core Ops, SparseCore 0:
  9.4 124.7 all-gather.2
  200.0 50.3 reduce-scatter.1

commit v6 on v5

--- a/solution.py
+++ b/solution.py
@@ -1,6 +1,8 @@
 import jax
 import jax.numpy as jnp
 from jax import lax
+from jax.experimental import pallas as pl
+from jax.experimental.pallas import tpu as pltpu
 from jax.sharding import Mesh, PartitionSpec as P
 
 D = 4096
@@ -31,11 +33,13 @@
     dispatch = jnp.sum(placement, axis=1).astype(bf16)
     down_all = lax.all_gather(w_down, "tp", axis=0)
     proj_own = lax.all_gather(out_proj, "a", axis=1, tiled=True)
-    context, proj_own, dispatch, placement, onehot = lax.optimization_barrier(
-        (context, proj_own, dispatch, placement, onehot)
+    proj_own, dispatch, placement, onehot = lax.optimization_barrier(
+        (proj_own, dispatch, placement, onehot)
     )
     proj_other = lax.ppermute(proj_own, "core", swap)
-    context_all = lax.all_gather(context, "q", axis=0, tiled=True)
+    context_all = lax.all_to_all(
+        jnp.broadcast_to(context, (quads, *context.shape)), "q", 0, 0, tiled=True
+    ).reshape(quads * tok_rows, -1)
     context_all, proj_other = lax.optimization_barrier((context_all, proj_other))
     first = lax.axis_index("core") == 0
     own, other = (
@@ -89,16 +93,7 @@
     weights = jnp.stack([leading, 1.0 - leading], axis=1)
     combine = jnp.sum(placement * weights[:, :, None], axis=1)
     share, row_inverse, combine = lax.optimization_barrier((share, row_inverse, combine))
-    ff = w_gate.shape[1]
-    wide = share.astype(f32)
-    gate_share, up_share = wide[:, :ff] * row_inverse, wide[:, ff:] * row_inverse
-    hidden = (jax.nn.silu(gate_share) * up_share).astype(bf16)
-    partial_value = jnp.stack(
-        [
-            jnp.dot(hidden, down_all[f], preferred_element_type=f32).astype(bf16)
-            for f in range(tp)
-        ]
-    )
+    partial_value = down_product(share, row_inverse, down_all)
 
     halves = partial_value.reshape(CORES, quads, chunk, width)
     from_core = lax.all_to_all(halves, "core", 0, 0, tiled=True)
@@ -118,6 +113,45 @@
         combine, back.reshape(chunk, width).astype(f32), precision=lax.Precision.HIGHEST
     )
     return (hfloat + expert_mix).astype(bf16)
+
+
+def down_body(share_ref, inverse_ref, down_ref, out_ref, near_ref, sems):
+    blocks, ff, _ = near_ref.shape
+    copies = [
+        pltpu.make_async_copy(down_ref.at[f], near_ref.at[f], sems.at[f]) for f in range(blocks)
+    ]
+    for copy in copies:
+        copy.start()
+    wide = share_ref[...].astype(jnp.float32) * inverse_ref[...]
+    hidden = (jax.nn.silu(wide[:, :ff]) * wide[:, ff:]).astype(jnp.bfloat16)
+    for f in range(blocks):
+        copies[f].wait()
+        out_ref[f] = jnp.dot(
+            hidden, near_ref[f], preferred_element_type=jnp.float32
+        ).astype(jnp.bfloat16)
+
+
+def down_product(share, inverse, down_all):
+    blocks, ff, width = down_all.shape
+    rows = share.shape[0]
+    near = pl.BlockSpec(memory_space=pltpu.VMEM)
+    return pl.pallas_call(
+        down_body,
+        in_specs=[near, near, pl.BlockSpec(memory_space=pltpu.HBM)],
+        out_specs=near,
+        out_shape=jax.ShapeDtypeStruct((blocks, rows, width), jnp.bfloat16),
+        scratch_shapes=[
+            pltpu.VMEM(down_all.shape, jnp.bfloat16),
+            pltpu.SemaphoreType.DMA((blocks,)),
+        ],
+        compiler_params=pltpu.CompilerParams(vmem_limit_bytes=54 * 1024 * 1024),
+        cost_estimate=pl.CostEstimate(
+            flops=2 * blocks * rows * ff * width,
+            bytes_accessed=2 * blocks * (ff + rows) * width,
+            transcendentals=rows * ff,
+        ),
+        name="down",
+    )(share, inverse, down_all)
 
 
 def flat(tp, q, core, t):

time: 332 us -> 329 us (level)
  blocking collectives: 233 us -> 224 us
  matrix products: 12.7 us -> 6.19 us
  Pallas kernels: 0 us -> 5.95 us
  waiting for transfers between devices: 34.5 us -> 38.6 us
    all_gather x1 -> x0, blocking collectives: 18.8 us -> none  [per_device(): context_all = lax.all_gather(context, 'q', axis=0, tiled=True)]
    all_to_all x1, blocking collectives: 17.3 us -> 34.7 us  [per_device(): lax.all_to_all(head_part.reshape(quads, tok_rows, -1), 'q', 0, 0, tiled=T...]
    all_to_all x0 -> x1, starting transfers between devices: none -> 13 us  [per_device(): lax.all_to_all(jnp.broadcast_to(context, (quads, *context.shape)), 'q', 0...]
    ppermute x1, starting transfers between devices: 14.1 us -> 5.01 us  [per_device(): proj_other = lax.ppermute(proj_own, 'core', swap)]
    all_gather x1, blocking collectives: 64 us -> 55.5 us  [per_device(): proj_own = lax.all_gather(out_proj, 'a', axis=1, tiled=True)]
    dot_general x8 -> x0, matrix products: 6.48 us -> none  [per_device(): jnp.dot(hidden, down_all[f], preferred_element_type=f32).astype(bf16)]
    pallas_call x0 -> x1, Pallas kernels: none -> 5.95 us  [down_product(): pl.pallas_call(down_body, in_specs=[near, near, pl.BlockSpec(memory_space...]
  transfers between devices with their start and end apart: 5 -> 6, of which waited for: 3 -> 4; matrix products, arithmetic and copies ran while one was open for 3% -> 3% of each run, Pallas kernels for 0% -> 0%
where the time goes in v6:
time: 329 us; the launch traced here: 327 us
  blocking collectives  224 us (68%)
  waiting for transfers between devices  38.6 us (12%)
  starting transfers between devices  31.2 us (9%)
  between operations  13.7 us (4%)
  matrix products  6.19 us (2%)
  Pallas kernels  5.95 us (2%)
  local copies, waits for them, and re-layouts  5.02 us (2%)
    all_gather x1, blocking collectives, per_device(): proj_own = lax.all_gather(out_proj, 'a', axis=1, tiled=True)  55.5 us
    all_to_all x1, blocking collectives, per_device(): lax.all_to_all(head_part.reshape(quads, tok_rows, -1), 'q', 0, 0, tiled=T...  34.7 us
    reduce_scatter x1, waiting for transfers between devices, per_device(): share = lax.psum_scatter(both, 'tp', scatter_dimension=0, tiled=True)  28.1 us
    all_to_all x1, blocking collectives, per_device(): parts = lax.all_to_all(cut, 'tp', 0, 0, tiled=True)  24.5 us
    all_to_all x1, blocking collectives, per_device(): back = lax.all_to_all(turned, 'a', 0, 0, tiled=True)  24.2 us
    all_to_all x1, blocking collectives, per_device(): lax.all_to_all(sectioned.reshape(EXPERTS, CAP, width), 'a', 0, 0, tiled=T...  22.5 us
    psum x1, blocking collectives, per_device(): lax.psum((row_sq, squares, unscaled), 'tp')  22.3 us
    all_to_all x1, blocking collectives, per_device(): from_chips = lax.all_to_all(on_chip, 'q', 0, 0, tiled=True)  19.9 us
  transfers between devices with their start and end apart: 6, of which 4 were waited for; matrix products, arithmetic and copies ran while one was open for 3% of the time, Pallas kernels for 0%

profile of v6, /device:TPU:65, one launch (start us, length us, event | category | flops | bytes accessed | tf_op | source)
XLA Modules:
  0.0 326.6 jit_solution(3176634990639509626)
XLA Ops:
  6.6 0.7 all-gather.3.cloned.1.call-update
  7.3 1.6 broadcast_in_dim.4
  8.9 13.0 %all-to-all-start = ((bf16[4,64,512]{2,1,0:T(8,128)(2,1)}), bf16[4,64,512]{2,1,0:T(8,128)(2,1)S(1)}, u32[]{:S(2)}, u32[]{:S(2)}) async-start(bf16[4,64,512]{2,1,0:T(8,128)(2,1)} %broadcast_in_dim.4), calls=%async_computation | async-start | bytes 524288 | tf_op jit(solution)/shard_map/all_to_all | solution.py:40
  21.8 0.8 copy.42
  23.4 55.5 %all_gather.12 = bf16[512,512]{1,0:T(8,128)(2,1)S(1)} all-gather(bf16[512,128]{1,0:T(8,128)(2,1)} %param.11), channel_id=1, replica_groups=mesh['groups'=2,'a'=4,'q'=4,'core'=2,'tp'=8] {'a'}, dimensions={1}, use_global_device_ids=true | all-gather | bytes 655360 | tf_op jit(solution)/shard_map/all_gather | solution.py:35
  79.1 5.0 %collective-permute-start = (bf16[512,512]{1,0:T(8,128)(2,1)S(1)}, bf16[512,512]{1,0:T(8,128)(2,1)S(1)}, u32[]{:S(2)}, u32[]{:S(2)}) collective-permute-start(bf16[512,512]{1,0:T(8,128)(2,1)S(1)} %all_gather.12), channel_id=1, source_target_pairs={{0,8},{8,0},{1,9},{9,1},{2,10},{10,2},{3,11},{11,3},{4,12},{12,4},... | collective-permute-start | bytes 1572872 | tf_op jit(solution)/shard_map/ppermute | solution.py:39
  84.1 1.5 collective-permute-done
  86.3 34.7 %all_to_all.35 = bf16[4,64,1024]{2,1,0:T(8,128)(2,1)S(1)} all-to-all(bf16[4,64,1024]{2,1,0:T(8,128)(2,1)S(1)} %bitcast.21), channel_id=1, replica_groups=mesh['groups'=2,'a'=4,'q'=4,'core'=2,'tp'=8] {'q'}, dimensions={0} | all-to-all | bytes 1048576 | tf_op jit(solution)/shard_map/all_to_all | solution.py:52
  122.1 24.5 %all_to_all.36 = bf16[8,64,512]{2,1,0:T(8,128)(2,1)S(1)} all-to-all(bf16[8,64,512]{2,1,0:T(8,128)(2,1)S(1)} %reshape.56), channel_id=1, replica_groups=mesh['groups'=2,'a'=4,'q'=4,'core'=2,'tp'=8] {'tp'}, dimensions={0} | all-to-all | bytes 1048576 | tf_op jit(solution)/shard_map/all_to_all | solution.py:57
  147.0 22.5 %all_to_all.37 = bf16[4,36,512]{2,1,0:T(8,128)(2,1)S(1)} all-to-all(bf16[4,36,512]{2,1,0:T(8,128)(2,1)S(1)} %reshape.57), channel_id=1, replica_groups=mesh['groups'=2,'a'=4,'q'=4,'core'=2,'tp'=8] {'a'}, dimensions={0} | all-to-all | bytes 294912 | tf_op jit(solution)/shard_map/all_to_all | solution.py:67
  169.5 13.9 %all_gather.13 = bf16[576,512]{1,0:T(8,128)(2,1)S(1)} all-gather(bf16[144,512]{1,0:T(8,128)(2,1)S(1)} %reshape.58), channel_id=1, replica_groups=mesh['groups'=2,'a'=4,'q'=4,'core'=2,'tp'=8] {'q'}, dimensions={0}, use_global_device_ids=true | all-gather | bytes 737280 | tf_op jit(solution)/shard_map/all_gather | solution.py:69
  183.4 7.0 %collective-permute-start.1 = (bf16[576,512]{1,0:T(8,128)(2,1)S(1)}, bf16[576,512]{1,0:T(8,128)(2,1)S(1)}, u32[]{:S(2)}, u32[]{:S(2)}) collective-permute-start(bf16[576,512]{1,0:T(8,128)(2,1)S(1)} %all_gather.13), channel_id=1, source_target_pairs={{0,8},{8,0},{1,9},{9,1},{2,10},{10,2},{3,11},{11,3},{4,12},{12,4},... | collective-permute-start | bytes 1769480 | tf_op jit(solution)/shard_map/ppermute | solution.py:70
  190.7 1.3 collective-permute-done.1
  192.4 4.4 %convolution_convert_fusion = bf16[1152,1792]{1,0:T(8,128)(2,1)} fusion(bf16[512,1792]{1,0:T(8,128)(2,1)S(1)} %pad_maximum_fusion, f32[512]{0:T(512)S(1)} %convert_element_type.67, bf16[576,512]{1,0:T(8,128)(2,1)S(1)} %get-tuple-element.41, bf16[576,512]{1,0:T(8,128)(2,1)S(1)} %get-tuple-element.40), kind=kOutput, calls=%fused_computation | convolution fusion | flops 2119532544 | bytes 7145472 | tf_op jit(solution)/shard_map/dot_general | solution.py:76
  196.8 22.3 %all-reduce = (f32[1152]{0:T(1024)S(1)}, f32[64,4]{0,1:T(4,128)S(1)}, f32[64]{0:T(128)S(1)}) all-reduce(f32[1152]{0:T(1024)S(1)} %fusion.1, f32[64,4]{0,1:T(4,128)S(1)} %fusion.6, f32[64]{0:T(128)S(1)} %get-tuple-element.28), channel_id=1, replica_groups=mesh['groups'=2,'a'=4,'q'=4,'core'=2,'tp'=8] {'tp'}, use_global_device_ids=true, to_apply=%region_7.8 | all-reduce | flops 1472 | bytes 11776 | tf_op jit(solution)/shard_map/psum | solution.py:85
  220.0 28.1 %reduce-scatter.2.cloned.1.call-done.share_ref = bf16[144,1792]{1,0:T(8,128)(2,1)} async-done(((bf16[1152,1792]{1,0:T(8,128)(2,1)}), bf16[144,1792]{1,0:T(8,128)(2,1)}) %reduce-scatter.2.cloned.1.call-update) | async-done | bytes 516112 | tf_op jit(solution)/shard_map/reduce_scatter | solution.py:84
  248.1 0.7 copy.48.inverse_ref
  248.9 6.0 %down.1 = bf16[8,144,512]{2,1,0:T(8,128)(2,1)} custom-call(bf16[144,1792]{1,0:T(8,128)(2,1)} %reduce-scatter.2.cloned.1.call-done.share_ref, f32[144,1]{1,0:T(8,128)} %copy.48.inverse_ref, bf16[8,896,512]{2,1,0:T(8,128)(2,1)} %bitcast.17), custom_call_target="tpu_custom_call" | custom-call | flops 1056964608 | bytes 8519680 | tf_op jit(solution)/shard_map/down/pallas_call | solution.py:138
  254.8 6.2 %all_to_all.38 = bf16[2,4,144,512]{3,2,1,0:T(8,128)(2,1)S(1)} all-to-all(bf16[2,4,144,512]{3,2,1,0:T(8,128)(2,1)} %bitcast.18), channel_id=1, replica_groups=mesh['groups'=2,'a'=4,'q'=4,'core'=2,'tp'=8] {'core'}, dimensions={0} | all-to-all | bytes 2359296 | tf_op jit(solution)/shard_map/all_to_all | solution.py:99
  261.6 19.9 %all_to_all.39 = bf16[4,144,512]{2,1,0:T(8,128)(2,1)S(1)} all-to-all(bf16[4,144,512]{2,1,0:T(8,128)(2,1)S(1)} %reduce_sum.100), channel_id=1, replica_groups=mesh['groups'=2,'a'=4,'q'=4,'core'=2,'tp'=8] {'q'}, dimensions={0} | all-to-all | bytes 1179648 | tf_op jit(solution)/shard_map/all_to_all | solution.py:101
  281.5 6.2 %collective-permute-start.2 = (bf16[4,36,512]{2,1,0:T(8,128)(2,1)S(1)}, bf16[4,36,512]{2,1,0:T(8,128)(2,1)S(1)}, u32[]{:S(2)}, u32[]{:S(2)}) collective-permute-start(bf16[4,36,512]{2,1,0:T(8,128)(2,1)S(1)} %reshape.60), channel_id=1, source_target_pairs={{0,0},{1,16},{2,32},{3,48},{4,8},{5,24},{6,40},{7,56},{8,4},{9,20}... | collective-permute-start | bytes 442376 | tf_op jit(solution)/shard_map/ppermute | solution.py:110
  287.8 6.9 %collective-permute-done.2 = bf16[4,36,512]{2,1,0:T(8,128)(2,1)S(1)} collective-permute-done((bf16[4,36,512]{2,1,0:T(8,128)(2,1)S(1)}, bf16[4,36,512]{2,1,0:T(8,128)(2,1)S(1)}, u32[]{:S(2)}, u32[]{:S(2)}) %collective-permute-start.2) | collective-permute-done | bytes 147488 | tf_op jit(solution)/shard_map/ppermute | solution.py:110
  294.7 24.2 %all_to_all.40 = bf16[4,36,512]{2,1,0:T(8,128)(2,1)S(1)} all-to-all(bf16[4,36,512]{2,1,0:T(8,128)(2,1)S(1)} %collective-permute-done.2), channel_id=1, replica_groups=mesh['groups'=2,'a'=4,'q'=4,'core'=2,'tp'=8] {'a'}, dimensions={0} | all-to-all | bytes 294912 | tf_op jit(solution)/shard_map/all_to_all | solution.py:111
  318.9 0.8 fusion.4
  (59 shorter events, 5.3 us)
Async XLA Ops:
  6.5 184.0 %copy-start = (bf16[512,4]{0,1:T(4,128)(2,1)S(1)}, bf16[512,4]{0,1:T(4,128)(2,1)}, u32[]{:S(2)}) copy-start(bf16[512,4]{0,1:T(4,128)(2,1)} %param.13) | copy-start | bytes 12292
  6.6 72.3 %copy-start.4 = (s32[64,2]{0,1:T(2,128)S(1)}, s32[64,2]{0,1:T(2,128)}, u32[]{:S(2)}) copy-start(s32[64,2]{0,1:T(2,128)} %param.14) | copy-start | bytes 1540
  6.6 190.2 %all-gather.3.cloned.1.call-start = ((), (), s32[]{:S(2)}) async-start(), calls=%async_computation.9 | async-start | bytes 8257536 | tf_op jit(solution)/shard_map/all_gather | solution.py:34
  8.9 76.7 %all-to-all-start = ((bf16[4,64,512]{2,1,0:T(8,128)(2,1)}), bf16[4,64,512]{2,1,0:T(8,128)(2,1)S(1)}, u32[]{:S(2)}, u32[]{:S(2)}) async-start(bf16[4,64,512]{2,1,0:T(8,128)(2,1)} %broadcast_in_dim.4), calls=%async_computation | async-start | bytes 524288 | tf_op jit(solution)/shard_map/all_to_all | solution.py:40
  21.8 226.3 %reduce-scatter.2.cloned.1.call-start = ((), (), s32[]{:S(2)}) async-start(), calls=%async_computation.8 | async-start | bytes 4644864 | tf_op jit(solution)/shard_map/reduce_scatter | solution.py:84
  79.1 6.5 %collective-permute-start = (bf16[512,512]{1,0:T(8,128)(2,1)S(1)}, bf16[512,512]{1,0:T(8,128)(2,1)S(1)}, u32[]{:S(2)}, u32[]{:S(2)}) collective-permute-start(bf16[512,512]{1,0:T(8,128)(2,1)S(1)} %all_gather.12), channel_id=1, source_target_pairs={{0,8},{8,0},{1,9},{9,1},{2,10},{10,2},{3,11},{11,3},{4,12},{12,4},... | collective-permute-start | bytes 1572872 | tf_op jit(solution)/shard_map/ppermute | solution.py:39
  121.0 25.6 %copy-start.3 = (bf16[64,512]{1,0:T(8,128)(2,1)S(1)}, bf16[64,512]{1,0:T(8,128)(2,1)}, u32[]{:S(2)}) copy-start(bf16[64,512]{1,0:T(8,128)(2,1)} %param.10) | copy-start | bytes 196612
  121.8 68.5 %copy-start.5 = (bf16[512]{0:T(512)(128)(2,1)S(1)}, bf16[512]{0:T(512)(128)(2,1)}, u32[]{:S(2)}) copy-start(bf16[512]{0:T(512)(128)(2,1)} %param.12) | copy-start | bytes 3076
  121.8 68.5 %copy-start.1 = (bf16[512,896]{1,0:T(8,128)(2,1)S(1)}, bf16[512,896]{1,0:T(8,128)(2,1)}, u32[]{:S(2)}) copy-start(bf16[512,896]{1,0:T(8,128)(2,1)} %param.16) | copy-start | bytes 2752516
  121.8 68.5 %copy-start.2 = (bf16[512,896]{1,0:T(8,128)(2,1)S(1)}, bf16[512,896]{1,0:T(8,128)(2,1)}, u32[]{:S(2)}) copy-start(bf16[512,896]{1,0:T(8,128)(2,1)} %param.15) | copy-start | bytes 2752516
  183.4 8.6 %collective-permute-start.1 = (bf16[576,512]{1,0:T(8,128)(2,1)S(1)}, bf16[576,512]{1,0:T(8,128)(2,1)S(1)}, u32[]{:S(2)}, u32[]{:S(2)}) collective-permute-start(bf16[576,512]{1,0:T(8,128)(2,1)S(1)} %all_gather.13), channel_id=1, source_target_pairs={{0,8},{8,0},{1,9},{9,1},{2,10},{10,2},{3,11},{11,3},{4,12},{12,4},... | collective-permute-start | bytes 1769480 | tf_op jit(solution)/shard_map/ppermute | solution.py:70
  281.5 13.1 %collective-permute-start.2 = (bf16[4,36,512]{2,1,0:T(8,128)(2,1)S(1)}, bf16[4,36,512]{2,1,0:T(8,128)(2,1)S(1)}, u32[]{:S(2)}, u32[]{:S(2)}) collective-permute-start(bf16[4,36,512]{2,1,0:T(8,128)(2,1)S(1)} %reshape.60), channel_id=1, source_target_pairs={{0,0},{1,16},{2,32},{3,48},{4,8},{5,24},{6,40},{7,56},{8,4},{9,20}... | collective-permute-start | bytes 442376 | tf_op jit(solution)/shard_map/ppermute | solution.py:110
Sparse Core Ops, SparseCore 0:
  9.4 130.9 all-gather.2
  196.9 51.1 reduce-scatter.1

commit v7 on v6

--- a/solution.py
+++ b/solution.py
@@ -31,10 +31,12 @@
         (target[:, None] == columns_all[None, :]).astype(f32).reshape(tok_rows, 2, EXPERTS * CAP)
     )
     dispatch = jnp.sum(placement, axis=1).astype(bf16)
-    down_all = lax.all_gather(w_down, "tp", axis=0)
+    ff = w_down.shape[0]
+    early = (ff // 128 + 1) // 2 * 128
+    down_early = lax.all_gather(w_down[:early], "tp", axis=0)
     proj_own = lax.all_gather(out_proj, "a", axis=1, tiled=True)
-    proj_own, dispatch, placement, onehot = lax.optimization_barrier(
-        (proj_own, dispatch, placement, onehot)
+    proj_own, dispatch, placement, onehot, w_late = lax.optimization_barrier(
+        (proj_own, dispatch, placement, onehot, w_down[early:])
     )
     proj_other = lax.ppermute(proj_own, "core", swap)
     context_all = lax.all_to_all(
@@ -55,6 +57,8 @@
     cut = head_part.reshape(quads // per, per, tok_rows, CORES, EXPERTS, cols)
     cut = jnp.transpose(cut, (4, 0, 2, 1, 3, 5)).reshape(tp, tok_rows, width)
     parts = lax.all_to_all(cut, "tp", 0, 0, tiled=True)
+    parts, w_late = lax.optimization_barrier((parts, w_late))
+    down_late = lax.all_gather(w_late, "tp", axis=0)
     attention = jnp.sum(parts.astype(f32), axis=0)
     hstate = (stream.astype(f32) + attention).astype(bf16)
     hfloat = hstate.astype(f32)
@@ -78,8 +82,8 @@
     unscaled = jnp.dot(
         hfloat * gain[None, :], router.astype(f32), precision=lax.Precision.HIGHEST
     )
-    both, down_all, row_sq, squares, unscaled = lax.optimization_barrier(
-        (both, down_all, row_sq, squares, unscaled)
+    both, down_early, down_late, row_sq, squares, unscaled = lax.optimization_barrier(
+        (both, down_early, down_late, row_sq, squares, unscaled)
     )
     share = lax.psum_scatter(both, "tp", scatter_dimension=0, tiled=True)
     row_total, total_sq, raw_logits = lax.psum((row_sq, squares, unscaled), "tp")
@@ -93,7 +97,7 @@
     weights = jnp.stack([leading, 1.0 - leading], axis=1)
     combine = jnp.sum(placement * weights[:, :, None], axis=1)
     share, row_inverse, combine = lax.optimization_barrier((share, row_inverse, combine))
-    partial_value = down_product(share, row_inverse, down_all)
+    partial_value = down_product(share, row_inverse, down_early, down_late)
 
     halves = partial_value.reshape(CORES, quads, chunk, width)
     from_core = lax.all_to_all(halves, "core", 0, 0, tiled=True)
@@ -115,43 +119,51 @@
     return (hfloat + expert_mix).astype(bf16)
 
 
-def down_body(share_ref, inverse_ref, down_ref, out_ref, near_ref, sems):
+def down_body(share_ref, inverse_ref, early_ref, late_ref, out_ref, near_ref, sems):
     blocks, ff, _ = near_ref.shape
+    early = early_ref.shape[1]
     copies = [
-        pltpu.make_async_copy(down_ref.at[f], near_ref.at[f], sems.at[f]) for f in range(blocks)
+        pltpu.make_async_copy(from_ref.at[f], near_ref.at[f, pl.ds(start, size)], sems.at[f, part])
+        for f in range(blocks)
+        for part, (from_ref, start, size) in enumerate(
+            ((early_ref, 0, early), (late_ref, early, ff - early))
+        )
     ]
     for copy in copies:
         copy.start()
     wide = share_ref[...].astype(jnp.float32) * inverse_ref[...]
     hidden = (jax.nn.silu(wide[:, :ff]) * wide[:, ff:]).astype(jnp.bfloat16)
     for f in range(blocks):
-        copies[f].wait()
+        copies[2 * f].wait()
+        copies[2 * f + 1].wait()
         out_ref[f] = jnp.dot(
             hidden, near_ref[f], preferred_element_type=jnp.float32
         ).astype(jnp.bfloat16)
 
 
-def down_product(share, inverse, down_all):
-    blocks, ff, width = down_all.shape
+def down_product(share, inverse, early, late):
+    blocks, _, width = early.shape
+    ff = early.shape[1] + late.shape[1]
     rows = share.shape[0]
     near = pl.BlockSpec(memory_space=pltpu.VMEM)
+    far = pl.BlockSpec(memory_space=pltpu.HBM)
     return pl.pallas_call(
         down_body,
-        in_specs=[near, near, pl.BlockSpec(memory_space=pltpu.HBM)],
+        in_specs=[near, near, far, far],
         out_specs=near,
         out_shape=jax.ShapeDtypeStruct((blocks, rows, width), jnp.bfloat16),
         scratch_shapes=[
-            pltpu.VMEM(down_all.shape, jnp.bfloat16),
-            pltpu.SemaphoreType.DMA((blocks,)),
+            pltpu.VMEM((blocks, ff, width), jnp.bfloat16),
+            pltpu.SemaphoreType.DMA((blocks, 2)),
         ],
-        compiler_params=pltpu.CompilerParams(vmem_limit_bytes=54 * 1024 * 1024),
+        compiler_params=pltpu.CompilerParams(vmem_limit_bytes=60 * 1024 * 1024),
         cost_estimate=pl.CostEstimate(
             flops=2 * blocks * rows * ff * width,
             bytes_accessed=2 * blocks * (ff + rows) * width,
             transcendentals=rows * ff,
         ),
         name="down",
-    )(share, inverse, down_all)
+    )(share, inverse, early, late)
 
 
 def flat(tp, q, core, t):

time: 329 us -> 336 us (1.021)
  waiting for transfers between devices: 38.6 us -> 48.4 us
  blocking collectives: 224 us -> 215 us
    reduce_scatter x1, waiting for transfers between devices: 28.1 us -> 38.6 us  [per_device(): share = lax.psum_scatter(both, 'tp', scatter_dimension=0, tiled=True)]
    slice x0 -> x2, local copies, waits for them, and re-layouts: none -> 3.68 us  [the longest x1 1.91 us: per_device(): down_early = lax.all_gather(w_down[:early], 'tp', axis=0)]
    all_to_all x1, blocking collectives: 24.5 us -> 21 us  [per_device(): parts = lax.all_to_all(cut, 'tp', 0, 0, tiled=True)]
  transfers between devices with their start and end apart: 6 -> 7, of which waited for: 4 -> 4; matrix products, arithmetic and copies ran while one was open for 3% -> 4% of each run, Pallas kernels for 0% -> 0%
where the time goes in v7:
time: 336 us; the launch traced here: 333 us
  blocking collectives  215 us (64%)
  waiting for transfers between devices  48.4 us (14%)
  starting transfers between devices  33.5 us (10%)
  between operations  13.4 us (4%)
  local copies, waits for them, and re-layouts  8.02 us (2%)
  matrix products  6.12 us (2%)
  Pallas kernels  5.97 us (2%)
    all_gather x1, blocking collectives, per_device(): proj_own = lax.all_gather(out_proj, 'a', axis=1, tiled=True)  55.1 us
    reduce_scatter x1, waiting for transfers between devices, per_device(): share = lax.psum_scatter(both, 'tp', scatter_dimension=0, tiled=True)  38.6 us
    all_to_all x1, blocking collectives, per_device(): lax.all_to_all(head_part.reshape(quads, tok_rows, -1), 'q', 0, 0, tiled=T...  33.9 us
    all_to_all x1, blocking collectives, per_device(): back = lax.all_to_all(turned, 'a', 0, 0, tiled=True)  24.5 us
    all_to_all x1, blocking collectives, per_device(): parts = lax.all_to_all(cut, 'tp', 0, 0, tiled=True)  21 us
    psum x1, blocking collectives, per_device(): lax.psum((row_sq, squares, unscaled), 'tp')  21 us
    all_to_all x1, blocking collectives, per_device(): lax.all_to_all(sectioned.reshape(EXPERTS, CAP, width), 'a', 0, 0, tiled=T...  20.1 us
    all_to_all x1, blocking collectives, per_device(): from_chips = lax.all_to_all(on_chip, 'q', 0, 0, tiled=True)  19.8 us
  transfers between devices with their start and end apart: 7, of which 4 were waited for; matrix products, arithmetic and copies ran while one was open for 4% of the time, Pallas kernels for 0%

profile of v7, /device:TPU:65, one launch (start us, length us, event | category | flops | bytes accessed | tf_op | source)
XLA Modules:
  0.0 333.0 jit_solution(5178297241598512054)
XLA Ops:
  6.6 1.9 slice.13
  8.5 1.5 broadcast_in_dim.4
  10.1 13.0 %all-to-all-start = ((bf16[4,64,512]{2,1,0:T(8,128)(2,1)}), bf16[4,64,512]{2,1,0:T(8,128)(2,1)S(1)}, u32[]{:S(2)}, u32[]{:S(2)}) async-start(bf16[4,64,512]{2,1,0:T(8,128)(2,1)} %broadcast_in_dim.4), calls=%async_computation | async-start | bytes 524288 | tf_op jit(solution)/shard_map/all_to_all | solution.py:42
  24.0 55.1 %all_gather.18 = bf16[512,512]{1,0:T(8,128)(2,1)S(1)} all-gather(bf16[512,128]{1,0:T(8,128)(2,1)S(1)} %copy-done.3), channel_id=1, replica_groups=mesh['groups'=2,'a'=4,'q'=4,'core'=2,'tp'=8] {'a'}, dimensions={1}, use_global_device_ids=true | all-gather | bytes 655360 | tf_op jit(solution)/shard_map/all_gather | solution.py:37
  79.2 1.8 slice.12
  81.0 5.0 %collective-permute-start = (bf16[512,512]{1,0:T(8,128)(2,1)S(1)}, bf16[512,512]{1,0:T(8,128)(2,1)S(1)}, u32[]{:S(2)}, u32[]{:S(2)}) collective-permute-start(bf16[512,512]{1,0:T(8,128)(2,1)S(1)} %all_gather.18), channel_id=1, source_target_pairs={{0,8},{8,0},{1,9},{9,1},{2,10},{10,2},{3,11},{11,3},{4,12},{12,4},... | collective-permute-start | bytes 1572872 | tf_op jit(solution)/shard_map/ppermute | solution.py:41
  86.0 1.5 collective-permute-done
  88.2 33.9 %all_to_all.35 = bf16[4,64,1024]{2,1,0:T(8,128)(2,1)S(1)} all-to-all(bf16[4,64,1024]{2,1,0:T(8,128)(2,1)S(1)} %bitcast.23), channel_id=1, replica_groups=mesh['groups'=2,'a'=4,'q'=4,'core'=2,'tp'=8] {'q'}, dimensions={0} | all-to-all | bytes 1048576 | tf_op jit(solution)/shard_map/all_to_all | solution.py:54
  123.1 21.0 %all_to_all.36 = bf16[8,64,512]{2,1,0:T(8,128)(2,1)S(1)} all-to-all(bf16[8,64,512]{2,1,0:T(8,128)(2,1)S(1)} %reshape.56), channel_id=1, replica_groups=mesh['groups'=2,'a'=4,'q'=4,'core'=2,'tp'=8] {'tp'}, dimensions={0} | all-to-all | bytes 1048576 | tf_op jit(solution)/shard_map/all_to_all | solution.py:59
  144.8 20.1 %all_to_all.37 = bf16[4,36,512]{2,1,0:T(8,128)(2,1)S(1)} all-to-all(bf16[4,36,512]{2,1,0:T(8,128)(2,1)S(1)} %reshape.57), channel_id=1, replica_groups=mesh['groups'=2,'a'=4,'q'=4,'core'=2,'tp'=8] {'a'}, dimensions={0} | all-to-all | bytes 294912 | tf_op jit(solution)/shard_map/all_to_all | solution.py:71
  164.9 13.6 %all_gather.19 = bf16[576,512]{1,0:T(8,128)(2,1)S(1)} all-gather(bf16[144,512]{1,0:T(8,128)(2,1)S(1)} %reshape.58), channel_id=1, replica_groups=mesh['groups'=2,'a'=4,'q'=4,'core'=2,'tp'=8] {'q'}, dimensions={0}, use_global_device_ids=true | all-gather | bytes 737280 | tf_op jit(solution)/shard_map/all_gather | solution.py:73
  178.5 9.1 %collective-permute-start.1 = (bf16[576,512]{1,0:T(8,128)(2,1)S(1)}, bf16[576,512]{1,0:T(8,128)(2,1)S(1)}, u32[]{:S(2)}, u32[]{:S(2)}) collective-permute-start(bf16[576,512]{1,0:T(8,128)(2,1)S(1)} %all_gather.19), channel_id=1, source_target_pairs={{0,8},{8,0},{1,9},{9,1},{2,10},{10,2},{3,11},{11,3},{4,12},{12,4},... | collective-permute-start | bytes 1769480 | tf_op jit(solution)/shard_map/ppermute | solution.py:74
  188.0 1.2 collective-permute-done.1
  189.6 4.3 %convolution_convert_fusion = bf16[1152,1792]{1,0:T(8,128)(2,1)} fusion(bf16[512,1792]{1,0:T(8,128)(2,1)S(1)} %pad_maximum_fusion, f32[512]{0:T(512)S(1)} %convert_element_type.67, bf16[576,512]{1,0:T(8,128)(2,1)S(1)} %get-tuple-element.49, bf16[576,512]{1,0:T(8,128)(2,1)S(1)} %get-tuple-element.48), kind=kOutput, calls=%fused_computation | convolution fusion | flops 2119532544 | bytes 7145472 | tf_op jit(solution)/shard_map/dot_general | solution.py:80
  194.0 21.0 %all-reduce = (f32[1152]{0:T(1024)S(1)}, f32[64,4]{0,1:T(4,128)S(1)}, f32[64]{0:T(128)S(1)}) all-reduce(f32[1152]{0:T(1024)S(1)} %fusion.1, f32[64,4]{0,1:T(4,128)S(1)} %fusion.6, f32[64]{0:T(128)S(1)} %get-tuple-element.35), channel_id=1, replica_groups=mesh['groups'=2,'a'=4,'q'=4,'core'=2,'tp'=8] {'tp'}, use_global_device_ids=true, to_apply=%region_7.8 | all-reduce | flops 1472 | bytes 11776 | tf_op jit(solution)/shard_map/psum | solution.py:89
  215.9 38.6 %reduce-scatter.2.cloned.1.call-done.share_ref = bf16[144,1792]{1,0:T(8,128)(2,1)} async-done(((bf16[1152,1792]{1,0:T(8,128)(2,1)}), bf16[144,1792]{1,0:T(8,128)(2,1)}) %reduce-scatter.2.cloned.1.call-update) | async-done | bytes 516112 | tf_op jit(solution)/shard_map/reduce_scatter | solution.py:88
  254.5 0.7 copy.48.inverse_ref
  255.2 6.0 %down.1 = bf16[8,144,512]{2,1,0:T(8,128)(2,1)} custom-call(bf16[144,1792]{1,0:T(8,128)(2,1)} %reduce-scatter.2.cloned.1.call-done.share_ref, f32[144,1]{1,0:T(8,128)} %copy.48.inverse_ref, bf16[8,512,512]{2,1,0:T(8,128)(2,1)} %bitcast.19, bf16[8,384,512]{2,1,0:T(8,128)(2,1)} %bitcast.20), custom_call_target="tpu_custom_call" | custom-call | flops 1056964608 | bytes 8519680 | tf_op jit(solution)/shard_map/down/pallas_call | solution.py:150
  261.2 6.2 %all_to_all.38 = bf16[2,4,144,512]{3,2,1,0:T(8,128)(2,1)S(1)} all-to-all(bf16[2,4,144,512]{3,2,1,0:T(8,128)(2,1)} %bitcast.18), channel_id=1, replica_groups=mesh['groups'=2,'a'=4,'q'=4,'core'=2,'tp'=8] {'core'}, dimensions={0} | all-to-all | bytes 2359296 | tf_op jit(solution)/shard_map/all_to_all | solution.py:103
  268.0 19.8 %all_to_all.39 = bf16[4,144,512]{2,1,0:T(8,128)(2,1)S(1)} all-to-all(bf16[4,144,512]{2,1,0:T(8,128)(2,1)S(1)} %reduce_sum.100), channel_id=1, replica_groups=mesh['groups'=2,'a'=4,'q'=4,'core'=2,'tp'=8] {'q'}, dimensions={0} | all-to-all | bytes 1179648 | tf_op jit(solution)/shard_map/all_to_all | solution.py:105
  287.9 6.3 %collective-permute-start.2 = (bf16[4,36,512]{2,1,0:T(8,128)(2,1)S(1)}, bf16[4,36,512]{2,1,0:T(8,128)(2,1)S(1)}, u32[]{:S(2)}, u32[]{:S(2)}) collective-permute-start(bf16[4,36,512]{2,1,0:T(8,128)(2,1)S(1)} %reshape.60), channel_id=1, source_target_pairs={{0,0},{1,16},{2,32},{3,48},{4,8},{5,24},{6,40},{7,56},{8,4},{9,20}... | collective-permute-start | bytes 442376 | tf_op jit(solution)/shard_map/ppermute | solution.py:114
  294.3 6.8 %collective-permute-done.2 = bf16[4,36,512]{2,1,0:T(8,128)(2,1)S(1)} collective-permute-done((bf16[4,36,512]{2,1,0:T(8,128)(2,1)S(1)}, bf16[4,36,512]{2,1,0:T(8,128)(2,1)S(1)}, u32[]{:S(2)}, u32[]{:S(2)}) %collective-permute-start.2) | collective-permute-done | bytes 147488 | tf_op jit(solution)/shard_map/ppermute | solution.py:114
  301.1 24.5 %all_to_all.40 = bf16[4,36,512]{2,1,0:T(8,128)(2,1)S(1)} all-to-all(bf16[4,36,512]{2,1,0:T(8,128)(2,1)S(1)} %collective-permute-done.2), channel_id=1, replica_groups=mesh['groups'=2,'a'=4,'q'=4,'core'=2,'tp'=8] {'a'}, dimensions={0} | all-to-all | bytes 294912 | tf_op jit(solution)/shard_map/all_to_all | solution.py:115
  325.6 0.8 fusion.4
  (66 shorter events, 5.6 us)
Async XLA Ops:
  6.5 181.3 %copy-start = (bf16[512,4]{0,1:T(4,128)(2,1)S(1)}, bf16[512,4]{0,1:T(4,128)(2,1)}, u32[]{:S(2)}) copy-start(bf16[512,4]{0,1:T(4,128)(2,1)} %param.13) | copy-start | bytes 12292
  6.6 16.5 %copy-start.5 = (s32[64,2]{0,1:T(2,128)S(1)}, s32[64,2]{0,1:T(2,128)}, u32[]{:S(2)}) copy-start(s32[64,2]{0,1:T(2,128)} %param.14) | copy-start | bytes 1540
  6.6 17.4 %copy-start.3 = (bf16[512,128]{1,0:T(8,128)(2,1)S(1)}, bf16[512,128]{1,0:T(8,128)(2,1)}, u32[]{:S(2)}) copy-start(bf16[512,128]{1,0:T(8,128)(2,1)} %param.11) | copy-start | bytes 393220
  6.6 187.4 %all-gather.5.cloned.1.call-start = ((), (), s32[]{:S(2)}) async-start(), calls=%async_computation.9 | async-start | bytes 4718592 | tf_op jit(solution)/shard_map/all_gather | solution.py:36
  10.1 77.4 %all-to-all-start = ((bf16[4,64,512]{2,1,0:T(8,128)(2,1)}), bf16[4,64,512]{2,1,0:T(8,128)(2,1)S(1)}, u32[]{:S(2)}, u32[]{:S(2)}) async-start(bf16[4,64,512]{2,1,0:T(8,128)(2,1)} %broadcast_in_dim.4), calls=%async_computation | async-start | bytes 524288 | tf_op jit(solution)/shard_map/all_to_all | solution.py:42
  23.0 170.9 %all-gather.7.cloned.1.call-start = ((), (), s32[]{:S(2)}) async-start(), calls=%async_computation.10 | async-start | bytes 3538944 | tf_op jit(solution)/shard_map/all_gather | solution.py:61
  81.0 6.5 %collective-permute-start = (bf16[512,512]{1,0:T(8,128)(2,1)S(1)}, bf16[512,512]{1,0:T(8,128)(2,1)S(1)}, u32[]{:S(2)}, u32[]{:S(2)}) collective-permute-start(bf16[512,512]{1,0:T(8,128)(2,1)S(1)} %all_gather.18), channel_id=1, source_target_pairs={{0,8},{8,0},{1,9},{9,1},{2,10},{10,2},{3,11},{11,3},{4,12},{12,4},... | collective-permute-start | bytes 1572872 | tf_op jit(solution)/shard_map/ppermute | solution.py:41
  122.5 21.9 %copy-start.4 = (bf16[64,512]{1,0:T(8,128)(2,1)S(1)}, bf16[64,512]{1,0:T(8,128)(2,1)}, u32[]{:S(2)}) copy-start(bf16[64,512]{1,0:T(8,128)(2,1)} %param.10) | copy-start | bytes 196612
  123.1 64.5 %copy-start.6 = (bf16[512]{0:T(512)(128)(2,1)S(1)}, bf16[512]{0:T(512)(128)(2,1)}, u32[]{:S(2)}) copy-start(bf16[512]{0:T(512)(128)(2,1)} %param.12) | copy-start | bytes 3076
  123.1 64.5 %copy-start.1 = (bf16[512,896]{1,0:T(8,128)(2,1)S(1)}, bf16[512,896]{1,0:T(8,128)(2,1)}, u32[]{:S(2)}) copy-start(bf16[512,896]{1,0:T(8,128)(2,1)} %param.16) | copy-start | bytes 2752516
  144.2 43.5 %copy-start.2 = (bf16[512,896]{1,0:T(8,128)(2,1)S(1)}, bf16[512,896]{1,0:T(8,128)(2,1)}, u32[]{:S(2)}) copy-start(bf16[512,896]{1,0:T(8,128)(2,1)} %param.15) | copy-start | bytes 2752516
  144.2 110.3 %reduce-scatter.2.cloned.1.call-start = ((), (), s32[]{:S(2)}) async-start(), calls=%async_computation.8 | async-start | bytes 4644864 | tf_op jit(solution)/shard_map/reduce_scatter | solution.py:88
  178.5 10.8 %collective-permute-start.1 = (bf16[576,512]{1,0:T(8,128)(2,1)S(1)}, bf16[576,512]{1,0:T(8,128)(2,1)S(1)}, u32[]{:S(2)}, u32[]{:S(2)}) collective-permute-start(bf16[576,512]{1,0:T(8,128)(2,1)S(1)} %all_gather.19), channel_id=1, source_target_pairs={{0,8},{8,0},{1,9},{9,1},{2,10},{10,2},{3,11},{11,3},{4,12},{12,4},... | collective-permute-start | bytes 1769480 | tf_op jit(solution)/shard_map/ppermute | solution.py:74
  287.9 13.2 %collective-permute-start.2 = (bf16[4,36,512]{2,1,0:T(8,128)(2,1)S(1)}, bf16[4,36,512]{2,1,0:T(8,128)(2,1)S(1)}, u32[]{:S(2)}, u32[]{:S(2)}) collective-permute-start(bf16[4,36,512]{2,1,0:T(8,128)(2,1)S(1)} %reshape.60), channel_id=1, source_target_pairs={{0,0},{1,16},{2,32},{3,48},{4,8},{5,24},{6,40},{7,56},{8,4},{9,20}... | collective-permute-start | bytes 442376 | tf_op jit(solution)/shard_map/ppermute | solution.py:114
Sparse Core Ops, SparseCore 0:
  9.4 95.2 all-gather.4
  144.4 46.1 all-gather.6
  194.1 60.3 reduce-scatter.1

commit v8 on v7

--- a/solution.py
+++ b/solution.py
@@ -32,7 +32,7 @@
     )
     dispatch = jnp.sum(placement, axis=1).astype(bf16)
     ff = w_down.shape[0]
-    early = (ff // 128 + 1) // 2 * 128
+    early = ff - 256
     down_early = lax.all_gather(w_down[:early], "tp", axis=0)
     proj_own = lax.all_gather(out_proj, "a", axis=1, tiled=True)
     proj_own, dispatch, placement, onehot, w_late = lax.optimization_barrier(
@@ -57,7 +57,7 @@
     cut = head_part.reshape(quads // per, per, tok_rows, CORES, EXPERTS, cols)
     cut = jnp.transpose(cut, (4, 0, 2, 1, 3, 5)).reshape(tp, tok_rows, width)
     parts = lax.all_to_all(cut, "tp", 0, 0, tiled=True)
-    parts, w_late = lax.optimization_barrier((parts, w_late))
+    parts, w_late, down_early = lax.optimization_barrier((parts, w_late, down_early))
     down_late = lax.all_gather(w_late, "tp", axis=0)
     attention = jnp.sum(parts.astype(f32), axis=0)
     hstate = (stream.astype(f32) + attention).astype(bf16)
@@ -82,13 +82,13 @@
     unscaled = jnp.dot(
         hfloat * gain[None, :], router.astype(f32), precision=lax.Precision.HIGHEST
     )
-    both, down_early, down_late, row_sq, squares, unscaled = lax.optimization_barrier(
-        (both, down_early, down_late, row_sq, squares, unscaled)
+    both, down_late, row_sq, squares, unscaled = lax.optimization_barrier(
+        (both, down_late, row_sq, squares, unscaled)
     )
     share = lax.psum_scatter(both, "tp", scatter_dimension=0, tiled=True)
     row_total, total_sq, raw_logits = lax.psum((row_sq, squares, unscaled), "tp")
     my_total = lax.dynamic_slice_in_dim(row_total, lax.axis_index("tp") * chunk, chunk)
-    row_inverse = lax.rsqrt(my_total / D + 1e-05)[:, None]
+    row_inverse = jnp.broadcast_to(lax.rsqrt(my_total / D + 1e-05)[:, None], (chunk, 128))
     inverse = lax.rsqrt(total_sq / D + 1e-05)[:, None]
     logits = raw_logits * inverse
     picked = onehot.reshape(tok_rows, 2, EXPERTS).astype(f32)
@@ -131,7 +131,7 @@
     ]
     for copy in copies:
         copy.start()
-    wide = share_ref[...].astype(jnp.float32) * inverse_ref[...]
+    wide = share_ref[...].astype(jnp.float32) * inverse_ref[:, :1]
     hidden = (jax.nn.silu(wide[:, :ff]) * wide[:, ff:]).astype(jnp.bfloat16)
     for f in range(blocks):
         copies[2 * f].wait()

time: 336 us -> 332 us (0.988)
  waiting for transfers between devices: 48.4 us -> 43.5 us
    reduce_scatter x1, waiting for transfers between devices: 38.6 us -> 33.6 us  [per_device(): share = lax.psum_scatter(both, 'tp', scatter_dimension=0, tiled=True)]
where the time goes in v8:
time: 332 us; the launch traced here: 329 us
  blocking collectives  216 us (65%)
  waiting for transfers between devices  43.5 us (13%)
  starting transfers between devices  33.3 us (10%)
  between operations  13.4 us (4%)
  local copies, waits for them, and re-layouts  8.02 us (2%)
  matrix products  6.1 us (2%)
  Pallas kernels  6 us (2%)
    all_gather x1, blocking collectives, per_device(): proj_own = lax.all_gather(out_proj, 'a', axis=1, tiled=True)  55.1 us
    all_to_all x1, blocking collectives, per_device(): lax.all_to_all(head_part.reshape(quads, tok_rows, -1), 'q', 0, 0, tiled=T...  33.9 us
    reduce_scatter x1, waiting for transfers between devices, per_device(): share = lax.psum_scatter(both, 'tp', scatter_dimension=0, tiled=True)  33.6 us
    all_to_all x1, blocking collectives, per_device(): back = lax.all_to_all(turned, 'a', 0, 0, tiled=True)  24.4 us
    psum x1, blocking collectives, per_device(): lax.psum((row_sq, squares, unscaled), 'tp')  22 us
    all_to_all x1, blocking collectives, per_device(): parts = lax.all_to_all(cut, 'tp', 0, 0, tiled=True)  21.1 us
    all_to_all x1, blocking collectives, per_device(): lax.all_to_all(sectioned.reshape(EXPERTS, CAP, width), 'a', 0, 0, tiled=T...  20.1 us
    all_to_all x1, blocking collectives, per_device(): from_chips = lax.all_to_all(on_chip, 'q', 0, 0, tiled=True)  19.9 us
  transfers between devices with their start and end apart: 7, of which 4 were waited for; matrix products, arithmetic and copies ran while one was open for 4% of the time, Pallas kernels for 0%

profile of v8, /device:TPU:65, one launch (start us, length us, event | category | flops | bytes accessed | tf_op | source)
XLA Modules:
  0.0 328.8 jit_solution(6401955347545467938)
XLA Ops:
  6.6 2.0 slice.13
  8.6 1.6 broadcast_in_dim.4
  10.2 13.0 %all-to-all-start = ((bf16[4,64,512]{2,1,0:T(8,128)(2,1)}), bf16[4,64,512]{2,1,0:T(8,128)(2,1)S(1)}, u32[]{:S(2)}, u32[]{:S(2)}) async-start(bf16[4,64,512]{2,1,0:T(8,128)(2,1)} %broadcast_in_dim.4), calls=%async_computation | async-start | bytes 524288 | tf_op jit(solution)/shard_map/all_to_all | solution.py:42
  24.1 55.1 %all_gather.18 = bf16[512,512]{1,0:T(8,128)(2,1)S(1)} all-gather(bf16[512,128]{1,0:T(8,128)(2,1)S(1)} %copy-done.3), channel_id=1, replica_groups=mesh['groups'=2,'a'=4,'q'=4,'core'=2,'tp'=8] {'a'}, dimensions={1}, use_global_device_ids=true | all-gather | bytes 655360 | tf_op jit(solution)/shard_map/all_gather | solution.py:37
  79.3 1.7 slice.12
  81.0 5.0 %collective-permute-start = (bf16[512,512]{1,0:T(8,128)(2,1)S(1)}, bf16[512,512]{1,0:T(8,128)(2,1)S(1)}, u32[]{:S(2)}, u32[]{:S(2)}) collective-permute-start(bf16[512,512]{1,0:T(8,128)(2,1)S(1)} %all_gather.18), channel_id=1, source_target_pairs={{0,8},{8,0},{1,9},{9,1},{2,10},{10,2},{3,11},{11,3},{4,12},{12,4},... | collective-permute-start | bytes 1572872 | tf_op jit(solution)/shard_map/ppermute | solution.py:41
  86.0 1.5 collective-permute-done
  88.2 33.9 %all_to_all.35 = bf16[4,64,1024]{2,1,0:T(8,128)(2,1)S(1)} all-to-all(bf16[4,64,1024]{2,1,0:T(8,128)(2,1)S(1)} %bitcast.22), channel_id=1, replica_groups=mesh['groups'=2,'a'=4,'q'=4,'core'=2,'tp'=8] {'q'}, dimensions={0} | all-to-all | bytes 1048576 | tf_op jit(solution)/shard_map/all_to_all | solution.py:54
  123.1 21.1 %all_to_all.36 = bf16[8,64,512]{2,1,0:T(8,128)(2,1)S(1)} all-to-all(bf16[8,64,512]{2,1,0:T(8,128)(2,1)S(1)} %reshape.57), channel_id=1, replica_groups=mesh['groups'=2,'a'=4,'q'=4,'core'=2,'tp'=8] {'tp'}, dimensions={0} | all-to-all | bytes 1048576 | tf_op jit(solution)/shard_map/all_to_all | solution.py:59
  144.8 20.1 %all_to_all.37 = bf16[4,36,512]{2,1,0:T(8,128)(2,1)S(1)} all-to-all(bf16[4,36,512]{2,1,0:T(8,128)(2,1)S(1)} %reshape.58), channel_id=1, replica_groups=mesh['groups'=2,'a'=4,'q'=4,'core'=2,'tp'=8] {'a'}, dimensions={0} | all-to-all | bytes 294912 | tf_op jit(solution)/shard_map/all_to_all | solution.py:71
  164.9 13.6 %all_gather.21 = bf16[576,512]{1,0:T(8,128)(2,1)S(1)} all-gather(bf16[144,512]{1,0:T(8,128)(2,1)S(1)} %reshape.59), channel_id=1, replica_groups=mesh['groups'=2,'a'=4,'q'=4,'core'=2,'tp'=8] {'q'}, dimensions={0}, use_global_device_ids=true | all-gather | bytes 737280 | tf_op jit(solution)/shard_map/all_gather | solution.py:73
  178.5 9.1 %collective-permute-start.1 = (bf16[576,512]{1,0:T(8,128)(2,1)S(1)}, bf16[576,512]{1,0:T(8,128)(2,1)S(1)}, u32[]{:S(2)}, u32[]{:S(2)}) collective-permute-start(bf16[576,512]{1,0:T(8,128)(2,1)S(1)} %all_gather.21), channel_id=1, source_target_pairs={{0,8},{8,0},{1,9},{9,1},{2,10},{10,2},{3,11},{11,3},{4,12},{12,4},... | collective-permute-start | bytes 1769480 | tf_op jit(solution)/shard_map/ppermute | solution.py:74
  187.9 1.3 collective-permute-done.1
  189.6 4.3 %convolution_convert_fusion = bf16[1152,1792]{1,0:T(8,128)(2,1)} fusion(bf16[512,1792]{1,0:T(8,128)(2,1)S(1)} %pad_maximum_fusion, f32[512]{0:T(512)S(1)} %convert_element_type.67, bf16[576,512]{1,0:T(8,128)(2,1)S(1)} %get-tuple-element.49, bf16[576,512]{1,0:T(8,128)(2,1)S(1)} %get-tuple-element.48), kind=kOutput, calls=%fused_computation | convolution fusion | flops 2119532544 | bytes 7145472 | tf_op jit(solution)/shard_map/dot_general | solution.py:80
  194.0 22.0 %all-reduce = (f32[1152]{0:T(1024)S(1)}, f32[64,4]{0,1:T(4,128)S(1)}, f32[64]{0:T(128)S(1)}) all-reduce(f32[1152]{0:T(1024)S(1)} %fusion.1, f32[64,4]{0,1:T(4,128)S(1)} %fusion.6, f32[64]{0:T(128)S(1)} %get-tuple-element.35), channel_id=1, replica_groups=mesh['groups'=2,'a'=4,'q'=4,'core'=2,'tp'=8] {'tp'}, use_global_device_ids=true, to_apply=%region_7.8 | all-reduce | flops 1472 | bytes 11776 | tf_op jit(solution)/shard_map/psum | solution.py:89
  216.8 33.6 %reduce-scatter.2.cloned.1.call-done.share_ref = bf16[144,1792]{1,0:T(8,128)(2,1)} async-done(((bf16[1152,1792]{1,0:T(8,128)(2,1)}), bf16[144,1792]{1,0:T(8,128)(2,1)}) %reduce-scatter.2.cloned.1.call-update) | async-done | bytes 516112 | tf_op jit(solution)/shard_map/reduce_scatter | solution.py:88
  250.4 0.7 broadcast_in_dim.5.inverse_ref
  251.1 6.0 %down.1 = bf16[8,144,512]{2,1,0:T(8,128)(2,1)} custom-call(bf16[144,1792]{1,0:T(8,128)(2,1)} %reduce-scatter.2.cloned.1.call-done.share_ref, f32[144,128]{1,0:T(8,128)} %broadcast_in_dim.5.inverse_ref, bf16[8,640,512]{2,1,0:T(8,128)(2,1)} %bitcast.17, bf16[8,256,512]{2,1,0:T(8,128)(2,1)} %bitcast.21), custom_call_target="tpu_custom_call" | custom-call | flops 1056964608 | bytes 8519680 | tf_op jit(solution)/shard_map/down/pallas_call | solution.py:150
  257.1 6.2 %all_to_all.38 = bf16[2,4,144,512]{3,2,1,0:T(8,128)(2,1)S(1)} all-to-all(bf16[2,4,144,512]{3,2,1,0:T(8,128)(2,1)} %bitcast.18), channel_id=1, replica_groups=mesh['groups'=2,'a'=4,'q'=4,'core'=2,'tp'=8] {'core'}, dimensions={0} | all-to-all | bytes 2359296 | tf_op jit(solution)/shard_map/all_to_all | solution.py:103
  263.9 19.9 %all_to_all.39 = bf16[4,144,512]{2,1,0:T(8,128)(2,1)S(1)} all-to-all(bf16[4,144,512]{2,1,0:T(8,128)(2,1)S(1)} %reduce_sum.100), channel_id=1, replica_groups=mesh['groups'=2,'a'=4,'q'=4,'core'=2,'tp'=8] {'q'}, dimensions={0} | all-to-all | bytes 1179648 | tf_op jit(solution)/shard_map/all_to_all | solution.py:105
  283.9 6.2 %collective-permute-start.2 = (bf16[4,36,512]{2,1,0:T(8,128)(2,1)S(1)}, bf16[4,36,512]{2,1,0:T(8,128)(2,1)S(1)}, u32[]{:S(2)}, u32[]{:S(2)}) collective-permute-start(bf16[4,36,512]{2,1,0:T(8,128)(2,1)S(1)} %reshape.61), channel_id=1, source_target_pairs={{0,0},{1,16},{2,32},{3,48},{4,8},{5,24},{6,40},{7,56},{8,4},{9,20}... | collective-permute-start | bytes 442376 | tf_op jit(solution)/shard_map/ppermute | solution.py:114
  290.1 6.9 %collective-permute-done.2 = bf16[4,36,512]{2,1,0:T(8,128)(2,1)S(1)} collective-permute-done((bf16[4,36,512]{2,1,0:T(8,128)(2,1)S(1)}, bf16[4,36,512]{2,1,0:T(8,128)(2,1)S(1)}, u32[]{:S(2)}, u32[]{:S(2)}) %collective-permute-start.2) | collective-permute-done | bytes 147488 | tf_op jit(solution)/shard_map/ppermute | solution.py:114
  297.0 24.4 %all_to_all.40 = bf16[4,36,512]{2,1,0:T(8,128)(2,1)S(1)} all-to-all(bf16[4,36,512]{2,1,0:T(8,128)(2,1)S(1)} %collective-permute-done.2), channel_id=1, replica_groups=mesh['groups'=2,'a'=4,'q'=4,'core'=2,'tp'=8] {'a'}, dimensions={0} | all-to-all | bytes 294912 | tf_op jit(solution)/shard_map/all_to_all | solution.py:115
  321.4 0.8 fusion.4
  (66 shorter events, 5.6 us)
Async XLA Ops:
  6.5 181.2 %copy-start = (bf16[512,4]{0,1:T(4,128)(2,1)S(1)}, bf16[512,4]{0,1:T(4,128)(2,1)}, u32[]{:S(2)}) copy-start(bf16[512,4]{0,1:T(4,128)(2,1)} %param.13) | copy-start | bytes 12292
  6.6 16.6 %copy-start.5 = (s32[64,2]{0,1:T(2,128)S(1)}, s32[64,2]{0,1:T(2,128)}, u32[]{:S(2)}) copy-start(s32[64,2]{0,1:T(2,128)} %param.14) | copy-start | bytes 1540
  6.6 17.5 %copy-start.3 = (bf16[512,128]{1,0:T(8,128)(2,1)S(1)}, bf16[512,128]{1,0:T(8,128)(2,1)}, u32[]{:S(2)}) copy-start(bf16[512,128]{1,0:T(8,128)(2,1)} %param.11) | copy-start | bytes 393220
  6.6 137.6 %all-gather.5.cloned.1.call-start = ((), (), s32[]{:S(2)}) async-start(), calls=%async_computation.9 | async-start | bytes 5898240 | tf_op jit(solution)/shard_map/all_gather | solution.py:36
  10.2 77.3 %all-to-all-start = ((bf16[4,64,512]{2,1,0:T(8,128)(2,1)}), bf16[4,64,512]{2,1,0:T(8,128)(2,1)S(1)}, u32[]{:S(2)}, u32[]{:S(2)}) async-start(bf16[4,64,512]{2,1,0:T(8,128)(2,1)} %broadcast_in_dim.4), calls=%async_computation | async-start | bytes 524288 | tf_op jit(solution)/shard_map/all_to_all | solution.py:42
  23.2 170.8 %all-gather.7.cloned.1.call-start = ((), (), s32[]{:S(2)}) async-start(), calls=%async_computation.10 | async-start | bytes 2359296 | tf_op jit(solution)/shard_map/all_gather | solution.py:61
  81.0 6.5 %collective-permute-start = (bf16[512,512]{1,0:T(8,128)(2,1)S(1)}, bf16[512,512]{1,0:T(8,128)(2,1)S(1)}, u32[]{:S(2)}, u32[]{:S(2)}) collective-permute-start(bf16[512,512]{1,0:T(8,128)(2,1)S(1)} %all_gather.18), channel_id=1, source_target_pairs={{0,8},{8,0},{1,9},{9,1},{2,10},{10,2},{3,11},{11,3},{4,12},{12,4},... | collective-permute-start | bytes 1572872 | tf_op jit(solution)/shard_map/ppermute | solution.py:41
  122.1 22.3 %copy-start.4 = (bf16[64,512]{1,0:T(8,128)(2,1)S(1)}, bf16[64,512]{1,0:T(8,128)(2,1)}, u32[]{:S(2)}) copy-start(bf16[64,512]{1,0:T(8,128)(2,1)} %param.10) | copy-start | bytes 196612
  122.9 64.7 %copy-start.6 = (bf16[512]{0:T(512)(128)(2,1)S(1)}, bf16[512]{0:T(512)(128)(2,1)}, u32[]{:S(2)}) copy-start(bf16[512]{0:T(512)(128)(2,1)} %param.12) | copy-start | bytes 3076
  122.9 64.7 %copy-start.1 = (bf16[512,896]{1,0:T(8,128)(2,1)S(1)}, bf16[512,896]{1,0:T(8,128)(2,1)}, u32[]{:S(2)}) copy-start(bf16[512,896]{1,0:T(8,128)(2,1)} %param.16) | copy-start | bytes 2752516
  122.9 64.7 %copy-start.2 = (bf16[512,896]{1,0:T(8,128)(2,1)S(1)}, bf16[512,896]{1,0:T(8,128)(2,1)}, u32[]{:S(2)}) copy-start(bf16[512,896]{1,0:T(8,128)(2,1)} %param.15) | copy-start | bytes 2752516
  144.3 106.1 %reduce-scatter.2.cloned.1.call-start = ((), (), s32[]{:S(2)}) async-start(), calls=%async_computation.8 | async-start | bytes 4644864 | tf_op jit(solution)/shard_map/reduce_scatter | solution.py:88
  178.5 10.7 %collective-permute-start.1 = (bf16[576,512]{1,0:T(8,128)(2,1)S(1)}, bf16[576,512]{1,0:T(8,128)(2,1)S(1)}, u32[]{:S(2)}, u32[]{:S(2)}) collective-permute-start(bf16[576,512]{1,0:T(8,128)(2,1)S(1)} %all_gather.21), channel_id=1, source_target_pairs={{0,8},{8,0},{1,9},{9,1},{2,10},{10,2},{3,11},{11,3},{4,12},{12,4},... | collective-permute-start | bytes 1769480 | tf_op jit(solution)/shard_map/ppermute | solution.py:74
  283.9 13.1 %collective-permute-start.2 = (bf16[4,36,512]{2,1,0:T(8,128)(2,1)S(1)}, bf16[4,36,512]{2,1,0:T(8,128)(2,1)S(1)}, u32[]{:S(2)}, u32[]{:S(2)}) collective-permute-start(bf16[4,36,512]{2,1,0:T(8,128)(2,1)S(1)} %reshape.61), channel_id=1, source_target_pairs={{0,0},{1,16},{2,32},{3,48},{4,8},{5,24},{6,40},{7,56},{8,4},{9,20}... | collective-permute-start | bytes 442376 | tf_op jit(solution)/shard_map/ppermute | solution.py:114
Sparse Core Ops, SparseCore 0:
  9.4 105.0 all-gather.4
  144.4 38.8 all-gather.6
  194.1 56.2 reduce-scatter.1

commit v9 on v6

--- a/solution.py
+++ b/solution.py
@@ -144,7 +144,7 @@
             pltpu.VMEM(down_all.shape, jnp.bfloat16),
             pltpu.SemaphoreType.DMA((blocks,)),
         ],
-        compiler_params=pltpu.CompilerParams(vmem_limit_bytes=54 * 1024 * 1024),
+        compiler_params=pltpu.CompilerParams(vmem_limit_bytes=50 * 1024 * 1024),
         cost_estimate=pl.CostEstimate(
             flops=2 * blocks * rows * ff * width,
             bytes_accessed=2 * blocks * (ff + rows) * width,

time: 329 us -> 327 us (level)
  no operation moved by 1% of the time
where the time goes in v9:
time: 327 us; the launch traced here: 324 us
  blocking collectives  222 us (68%)
  waiting for transfers between devices  38.6 us (12%)
  starting transfers between devices  31.2 us (10%)
  between operations  13.7 us (4%)
  matrix products  6.19 us (2%)
  local copies, waits for them, and re-layouts  5.43 us (2%)
  Pallas kernels  3.87 us (1%)
    all_gather x1, blocking collectives, per_device(): proj_own = lax.all_gather(out_proj, 'a', axis=1, tiled=True)  55.5 us
    all_to_all x1, blocking collectives, per_device(): lax.all_to_all(head_part.reshape(quads, tok_rows, -1), 'q', 0, 0, tiled=T...  34.7 us
    reduce_scatter x1, waiting for transfers between devices, per_device(): share = lax.psum_scatter(both, 'tp', scatter_dimension=0, tiled=True)  28.1 us
    all_to_all x1, blocking collectives, per_device(): parts = lax.all_to_all(cut, 'tp', 0, 0, tiled=True)  24.5 us
    all_to_all x1, blocking collectives, per_device(): back = lax.all_to_all(turned, 'a', 0, 0, tiled=True)  24.2 us
    all_to_all x1, blocking collectives, per_device(): lax.all_to_all(sectioned.reshape(EXPERTS, CAP, width), 'a', 0, 0, tiled=T...  22.5 us
    psum x1, blocking collectives, per_device(): lax.psum((row_sq, squares, unscaled), 'tp')  22.3 us
    all_to_all x1, blocking collectives, per_device(): from_chips = lax.all_to_all(on_chip, 'q', 0, 0, tiled=True)  19.9 us
  transfers between devices with their start and end apart: 6, of which 4 were waited for; matrix products, arithmetic and copies ran while one was open for 3% of the time, Pallas kernels for 0%

profile of v9, /device:TPU:65, one launch (start us, length us, event | category | flops | bytes accessed | tf_op | source)
XLA Modules:
  0.0 323.8 jit_solution(12755700100072684258)
XLA Ops:
  6.6 0.7 all-gather.3.cloned.1.call-update
  7.3 1.6 broadcast_in_dim.4
  8.9 13.0 %all-to-all-start = ((bf16[4,64,512]{2,1,0:T(8,128)(2,1)}), bf16[4,64,512]{2,1,0:T(8,128)(2,1)S(1)}, u32[]{:S(2)}, u32[]{:S(2)}) async-start(bf16[4,64,512]{2,1,0:T(8,128)(2,1)} %broadcast_in_dim.4), calls=%async_computation | async-start | bytes 524288 | tf_op jit(solution)/shard_map/all_to_all | solution.py:40
  21.8 0.8 copy.42
  23.4 55.5 %all_gather.12 = bf16[512,512]{1,0:T(8,128)(2,1)S(1)} all-gather(bf16[512,128]{1,0:T(8,128)(2,1)} %param.11), channel_id=1, replica_groups=mesh['groups'=2,'a'=4,'q'=4,'core'=2,'tp'=8] {'a'}, dimensions={1}, use_global_device_ids=true | all-gather | bytes 655360 | tf_op jit(solution)/shard_map/all_gather | solution.py:35
  79.1 5.0 %collective-permute-start = (bf16[512,512]{1,0:T(8,128)(2,1)S(1)}, bf16[512,512]{1,0:T(8,128)(2,1)S(1)}, u32[]{:S(2)}, u32[]{:S(2)}) collective-permute-start(bf16[512,512]{1,0:T(8,128)(2,1)S(1)} %all_gather.12), channel_id=1, source_target_pairs={{0,8},{8,0},{1,9},{9,1},{2,10},{10,2},{3,11},{11,3},{4,12},{12,4},... | collective-permute-start | bytes 1572872 | tf_op jit(solution)/shard_map/ppermute | solution.py:39
  84.1 1.5 collective-permute-done
  86.3 34.7 %all_to_all.35 = bf16[4,64,1024]{2,1,0:T(8,128)(2,1)S(1)} all-to-all(bf16[4,64,1024]{2,1,0:T(8,128)(2,1)S(1)} %bitcast.21), channel_id=1, replica_groups=mesh['groups'=2,'a'=4,'q'=4,'core'=2,'tp'=8] {'q'}, dimensions={0} | all-to-all | bytes 1048576 | tf_op jit(solution)/shard_map/all_to_all | solution.py:52
  122.1 24.5 %all_to_all.36 = bf16[8,64,512]{2,1,0:T(8,128)(2,1)S(1)} all-to-all(bf16[8,64,512]{2,1,0:T(8,128)(2,1)S(1)} %reshape.56), channel_id=1, replica_groups=mesh['groups'=2,'a'=4,'q'=4,'core'=2,'tp'=8] {'tp'}, dimensions={0} | all-to-all | bytes 1048576 | tf_op jit(solution)/shard_map/all_to_all | solution.py:57
  147.0 22.5 %all_to_all.37 = bf16[4,36,512]{2,1,0:T(8,128)(2,1)S(1)} all-to-all(bf16[4,36,512]{2,1,0:T(8,128)(2,1)S(1)} %reshape.57), channel_id=1, replica_groups=mesh['groups'=2,'a'=4,'q'=4,'core'=2,'tp'=8] {'a'}, dimensions={0} | all-to-all | bytes 294912 | tf_op jit(solution)/shard_map/all_to_all | solution.py:67
  169.5 13.9 %all_gather.13 = bf16[576,512]{1,0:T(8,128)(2,1)S(1)} all-gather(bf16[144,512]{1,0:T(8,128)(2,1)S(1)} %reshape.58), channel_id=1, replica_groups=mesh['groups'=2,'a'=4,'q'=4,'core'=2,'tp'=8] {'q'}, dimensions={0}, use_global_device_ids=true | all-gather | bytes 737280 | tf_op jit(solution)/shard_map/all_gather | solution.py:69
  183.4 7.0 %collective-permute-start.1 = (bf16[576,512]{1,0:T(8,128)(2,1)S(1)}, bf16[576,512]{1,0:T(8,128)(2,1)S(1)}, u32[]{:S(2)}, u32[]{:S(2)}) collective-permute-start(bf16[576,512]{1,0:T(8,128)(2,1)S(1)} %all_gather.13), channel_id=1, source_target_pairs={{0,8},{8,0},{1,9},{9,1},{2,10},{10,2},{3,11},{11,3},{4,12},{12,4},... | collective-permute-start | bytes 1769480 | tf_op jit(solution)/shard_map/ppermute | solution.py:70
  190.7 1.3 collective-permute-done.1
  192.4 4.4 %convolution_convert_fusion = bf16[1152,1792]{1,0:T(8,128)(2,1)} fusion(bf16[512,1792]{1,0:T(8,128)(2,1)S(1)} %pad_maximum_fusion, f32[512]{0:T(512)S(1)} %convert_element_type.67, bf16[576,512]{1,0:T(8,128)(2,1)S(1)} %get-tuple-element.41, bf16[576,512]{1,0:T(8,128)(2,1)S(1)} %get-tuple-element.40), kind=kOutput, calls=%fused_computation | convolution fusion | flops 2119532544 | bytes 7145472 | tf_op jit(solution)/shard_map/dot_general | solution.py:76
  196.8 22.3 %all-reduce = (f32[1152]{0:T(1024)S(1)}, f32[64,4]{0,1:T(4,128)S(1)}, f32[64]{0:T(128)S(1)}) all-reduce(f32[1152]{0:T(1024)S(1)} %fusion.1, f32[64,4]{0,1:T(4,128)S(1)} %fusion.6, f32[64]{0:T(128)S(1)} %get-tuple-element.28), channel_id=1, replica_groups=mesh['groups'=2,'a'=4,'q'=4,'core'=2,'tp'=8] {'tp'}, use_global_device_ids=true, to_apply=%region_7.8 | all-reduce | flops 1472 | bytes 11776 | tf_op jit(solution)/shard_map/psum | solution.py:85
  220.0 28.1 %reduce-scatter.2.cloned.1.call-done.share_ref = bf16[144,1792]{1,0:T(8,128)(2,1)} async-done(((bf16[1152,1792]{1,0:T(8,128)(2,1)}), bf16[144,1792]{1,0:T(8,128)(2,1)}) %reduce-scatter.2.cloned.1.call-update) | async-done | bytes 516112 | tf_op jit(solution)/shard_map/reduce_scatter | solution.py:84
  248.2 1.0 copy-done.1
  249.3 3.9 %down.1 = bf16[8,144,512]{2,1,0:T(8,128)(2,1)S(1)} custom-call(bf16[144,1792]{1,0:T(8,128)(2,1)S(1)} %copy-done.1, f32[144,1]{1,0:T(8,128)S(1)} %copy.48.inverse_ref, bf16[8,896,512]{2,1,0:T(8,128)(2,1)} %bitcast.18), custom_call_target="tpu_custom_call" | custom-call | flops 1056964608 | bytes 8519680 | tf_op jit(solution)/shard_map/down/pallas_call | solution.py:138
  253.2 5.1 %all_to_all.38 = bf16[2,4,144,512]{3,2,1,0:T(8,128)(2,1)S(1)} all-to-all(bf16[2,4,144,512]{3,2,1,0:T(8,128)(2,1)S(1)} %bitcast.17), channel_id=1, replica_groups=mesh['groups'=2,'a'=4,'q'=4,'core'=2,'tp'=8] {'core'}, dimensions={0} | all-to-all | bytes 2359296 | tf_op jit(solution)/shard_map/all_to_all | solution.py:99
  258.8 19.9 %all_to_all.39 = bf16[4,144,512]{2,1,0:T(8,128)(2,1)S(1)} all-to-all(bf16[4,144,512]{2,1,0:T(8,128)(2,1)S(1)} %reduce_sum.100), channel_id=1, replica_groups=mesh['groups'=2,'a'=4,'q'=4,'core'=2,'tp'=8] {'q'}, dimensions={0} | all-to-all | bytes 1179648 | tf_op jit(solution)/shard_map/all_to_all | solution.py:101
  278.8 6.2 %collective-permute-start.2 = (bf16[4,36,512]{2,1,0:T(8,128)(2,1)S(1)}, bf16[4,36,512]{2,1,0:T(8,128)(2,1)S(1)}, u32[]{:S(2)}, u32[]{:S(2)}) collective-permute-start(bf16[4,36,512]{2,1,0:T(8,128)(2,1)S(1)} %reshape.60), channel_id=1, source_target_pairs={{0,0},{1,16},{2,32},{3,48},{4,8},{5,24},{6,40},{7,56},{8,4},{9,20}... | collective-permute-start | bytes 442376 | tf_op jit(solution)/shard_map/ppermute | solution.py:110
  285.0 6.9 %collective-permute-done.2 = bf16[4,36,512]{2,1,0:T(8,128)(2,1)S(1)} collective-permute-done((bf16[4,36,512]{2,1,0:T(8,128)(2,1)S(1)}, bf16[4,36,512]{2,1,0:T(8,128)(2,1)S(1)}, u32[]{:S(2)}, u32[]{:S(2)}) %collective-permute-start.2) | collective-permute-done | bytes 147488 | tf_op jit(solution)/shard_map/ppermute | solution.py:110
  291.9 24.2 %all_to_all.40 = bf16[4,36,512]{2,1,0:T(8,128)(2,1)S(1)} all-to-all(bf16[4,36,512]{2,1,0:T(8,128)(2,1)S(1)} %collective-permute-done.2), channel_id=1, replica_groups=mesh['groups'=2,'a'=4,'q'=4,'core'=2,'tp'=8] {'a'}, dimensions={0} | all-to-all | bytes 294912 | tf_op jit(solution)/shard_map/all_to_all | solution.py:111
  316.1 0.8 fusion.4
  (61 shorter events, 5.4 us)
Async XLA Ops:
  6.5 184.0 %copy-start = (bf16[512,4]{0,1:T(4,128)(2,1)S(1)}, bf16[512,4]{0,1:T(4,128)(2,1)}, u32[]{:S(2)}) copy-start(bf16[512,4]{0,1:T(4,128)(2,1)} %param.13) | copy-start | bytes 12292
  6.6 72.3 %copy-start.5 = (s32[64,2]{0,1:T(2,128)S(1)}, s32[64,2]{0,1:T(2,128)}, u32[]{:S(2)}) copy-start(s32[64,2]{0,1:T(2,128)} %param.14) | copy-start | bytes 1540
  6.6 190.2 %all-gather.3.cloned.1.call-start = ((), (), s32[]{:S(2)}) async-start(), calls=%async_computation.9 | async-start | bytes 8257536 | tf_op jit(solution)/shard_map/all_gather | solution.py:34
  8.9 76.7 %all-to-all-start = ((bf16[4,64,512]{2,1,0:T(8,128)(2,1)}), bf16[4,64,512]{2,1,0:T(8,128)(2,1)S(1)}, u32[]{:S(2)}, u32[]{:S(2)}) async-start(bf16[4,64,512]{2,1,0:T(8,128)(2,1)} %broadcast_in_dim.4), calls=%async_computation | async-start | bytes 524288 | tf_op jit(solution)/shard_map/all_to_all | solution.py:40
  21.8 226.3 %reduce-scatter.2.cloned.1.call-start = ((), (), s32[]{:S(2)}) async-start(), calls=%async_computation.8 | async-start | bytes 4644864 | tf_op jit(solution)/shard_map/reduce_scatter | solution.py:84
  79.1 6.5 %collective-permute-start = (bf16[512,512]{1,0:T(8,128)(2,1)S(1)}, bf16[512,512]{1,0:T(8,128)(2,1)S(1)}, u32[]{:S(2)}, u32[]{:S(2)}) collective-permute-start(bf16[512,512]{1,0:T(8,128)(2,1)S(1)} %all_gather.12), channel_id=1, source_target_pairs={{0,8},{8,0},{1,9},{9,1},{2,10},{10,2},{3,11},{11,3},{4,12},{12,4},... | collective-permute-start | bytes 1572872 | tf_op jit(solution)/shard_map/ppermute | solution.py:39
  121.0 25.6 %copy-start.4 = (bf16[64,512]{1,0:T(8,128)(2,1)S(1)}, bf16[64,512]{1,0:T(8,128)(2,1)}, u32[]{:S(2)}) copy-start(bf16[64,512]{1,0:T(8,128)(2,1)} %param.10) | copy-start | bytes 196612
  121.8 68.5 %copy-start.6 = (bf16[512]{0:T(512)(128)(2,1)S(1)}, bf16[512]{0:T(512)(128)(2,1)}, u32[]{:S(2)}) copy-start(bf16[512]{0:T(512)(128)(2,1)} %param.12) | copy-start | bytes 3076
  121.8 68.5 %copy-start.2 = (bf16[512,896]{1,0:T(8,128)(2,1)S(1)}, bf16[512,896]{1,0:T(8,128)(2,1)}, u32[]{:S(2)}) copy-start(bf16[512,896]{1,0:T(8,128)(2,1)} %param.16) | copy-start | bytes 2752516
  121.8 68.5 %copy-start.3 = (bf16[512,896]{1,0:T(8,128)(2,1)S(1)}, bf16[512,896]{1,0:T(8,128)(2,1)}, u32[]{:S(2)}) copy-start(bf16[512,896]{1,0:T(8,128)(2,1)} %param.15) | copy-start | bytes 2752516
  183.4 8.6 %collective-permute-start.1 = (bf16[576,512]{1,0:T(8,128)(2,1)S(1)}, bf16[576,512]{1,0:T(8,128)(2,1)S(1)}, u32[]{:S(2)}, u32[]{:S(2)}) collective-permute-start(bf16[576,512]{1,0:T(8,128)(2,1)S(1)} %all_gather.13), channel_id=1, source_target_pairs={{0,8},{8,0},{1,9},{9,1},{2,10},{10,2},{3,11},{11,3},{4,12},{12,4},... | collective-permute-start | bytes 1769480 | tf_op jit(solution)/shard_map/ppermute | solution.py:70
  248.2 1.0 copy-start.1
  278.8 13.1 %collective-permute-start.2 = (bf16[4,36,512]{2,1,0:T(8,128)(2,1)S(1)}, bf16[4,36,512]{2,1,0:T(8,128)(2,1)S(1)}, u32[]{:S(2)}, u32[]{:S(2)}) collective-permute-start(bf16[4,36,512]{2,1,0:T(8,128)(2,1)S(1)} %reshape.60), channel_id=1, source_target_pairs={{0,0},{1,16},{2,32},{3,48},{4,8},{5,24},{6,40},{7,56},{8,4},{9,20}... | collective-permute-start | bytes 442376 | tf_op jit(solution)/shard_map/ppermute | solution.py:110
Sparse Core Ops, SparseCore 0:
  9.4 130.9 all-gather.2
  196.9 51.1 reduce-scatter.1
